TPU v7x, 32 devices: a whole 2x2x4 slice. The times are simulated.
32 devices in a mesh: ep: 8 (over z, x), dp: 4 (over y, core).
Axes of the slice: x: 2, y: 2, z: 4, core: 2. Of those that a mesh axis runs over, the one named last changes fastest.
Arguments:
- grad_out: float32 [4096, 1536], P(('ep', 'dp')), may hold values from -6 to 6
- tokens: bfloat16 [4096, 1536], P(('ep', 'dp')), may hold values from -6 to 6
- probs: float32 [4096, 4], P(('ep', 'dp')), may hold values from 0.1 to 0.5
- expert_ids: int32 [4096, 4], P(('ep', 'dp')), may hold values from 0 to 7, all different within a row; in each aligned block of 128 rows (0 to 127, 128 to 255, ...) at most 80 rows name the same one
- priority: int32 [32, 128], P(('ep', 'dp')), may hold values from 0 to 127, each once within a row
- cap_counts: int32 [8], replicated, may hold values from 40 to 80, as said below
- gate_weight: bfloat16 [8, 1536, 1536], P('ep'), may hold values from -0.15625 to 0.15625
- up_weight: bfloat16 [8, 1536, 1536], P('ep'), may hold values from -0.15625 to 0.15625
- down_weight: bfloat16 [8, 1536, 1536], P('ep'), may hold values from -0.15625 to 0.15625
Outputs:
- input_grad: bfloat16 [4096, 1536], P(('ep', 'dp'))
- prob_grad: float32 [4096, 4], P(('ep', 'dp'))
- gate_grad: bfloat16 [8, 1536, 1536], P('ep', 'dp')
- up_grad: bfloat16 [8, 1536, 1536], P('ep', 'dp')
- down_grad: bfloat16 [8, 1536, 1536], P('ep', 'dp')
Inputs may be any that keep to these rules, and one draw needn't show every extreme that they name: `expert_ids`: each row names 4 different experts; among the rows of one device no expert is named by more than 80 rows, and in some device some expert is named by exactly 80 rows. `priority`: each row orders the 128 tokens of one device, each number once. `cap_counts`: some expert has exactly 80.
All inputs are finite; a program needn't handle non-finite values. Where the computation divides by a largest or mean magnitude, that divisor is 1e-20 or more.
Results may differ from a plain program's by a relative error of at most 0.017.
Values may be sent and summed in bfloat16 or wider, within the bound.
No kernel may reach another device: no remote copies, remote signals or barrier semaphores. Data moves between devices by JAX's collectives and lax.ppermute only.
A program may use at most 128 MiB of HBM per device.

v0:
```python
import functools

import jax
import jax.numpy as jnp
from jax import lax
from jax.experimental import pallas as pl
from jax.experimental.pallas import tpu as pltpu
from jax.sharding import PartitionSpec as P


sharpness = 1.702
lanes = 128

params = functools.partial(pltpu.CompilerParams, vmem_limit_bytes=56 * 1024 * 1024)


def contract_last(first_op, second_op):
    return lax.dot_general(
        first_op, second_op, (((1,), (1,)), ((), ())), preferred_element_type=jnp.float32
    )


def contract_first(first_op, second_op):
    return lax.dot_general(
        first_op, second_op, (((0,), (0,)), ((), ())), preferred_element_type=jnp.float32
    )


def high_low(values):
    high = values.astype(jnp.bfloat16)
    return high, (values - high.astype(jnp.float32)).astype(jnp.bfloat16)


def iota(shape, dim):
    return lax.broadcasted_iota(jnp.int32, shape, dim)


def lane_sum(values, first, stop):
    lane = iota(values.shape, 1)
    return jnp.sum(jnp.where((lane >= first) & (lane < stop), values, 0.0), axis=1, keepdims=True)


def columns_of(rows_ref, count):
    n = rows_ref.shape[1]
    return [
        jnp.broadcast_to(rows_ref[k : k + 1, :].astype(jnp.float32), (n, n)).T
        for k in range(count)
    ]


def prep_kernel(cap_ref, ids_ref, order_ref, probs_ref, grad_ref, tok_ref, x_ref, q_ref, *, experts):
    rows, width = tok_ref.shape
    routes = ids_ref.shape[0]
    lane = iota((rows, lanes), 1)
    lane_f = lane.astype(jnp.float32)
    order = jnp.broadcast_to(order_ref[...].astype(jnp.float32), (rows, rows))
    earlier = (order < order.T).astype(jnp.bfloat16)
    ids = columns_of(ids_ref, routes)
    chances = columns_of(probs_ref, routes)
    hits = [lane_f == i for i in ids]
    routed = sum(h.astype(jnp.float32) for h in hits)
    before = jnp.dot(earlier, routed.astype(jnp.bfloat16), preferred_element_type=jnp.float32)
    limit = jnp.zeros((rows, lanes), jnp.float32)
    for e in range(experts):
        limit = jnp.where(lane == e, cap_ref[e].astype(jnp.float32), limit)
    grad = grad_ref[...]
    scale = jnp.maximum(jnp.max(jnp.abs(grad), axis=1, keepdims=True), 1.0)
    q_ref[...] = (grad / scale).astype(jnp.bfloat16)
    facts = jnp.zeros((rows, lanes), jnp.float32)
    for k in range(routes):
        rank = jnp.sum(jnp.where(hits[k], before, 0.0), axis=1, keepdims=True)
        most = jnp.sum(jnp.where(hits[k], limit, 0.0), axis=1, keepdims=True)
        high, low = (p.astype(jnp.float32) for p in high_low(chances[k]))
        facts = jnp.where(lane == k, ids[k], facts)
        facts = jnp.where(lane == routes + k, jnp.where(rank < most, rank, -1.0), facts)
        facts = jnp.where(lane == 2 * routes + k, high, facts)
        facts = jnp.where(lane == 3 * routes + k, low, facts)
    high, low = (s.astype(jnp.float32) for s in high_low(scale))
    facts = jnp.where(lane == 4 * routes, high, facts)
    facts = jnp.where(lane == 4 * routes + 1, low, facts)
    x_ref[:, :width] = tok_ref[...]
    x_ref[:, width:] = facts.astype(jnp.bfloat16)


def chunks_of(place_ref, refs, outer, inner):
    if len(refs) == outer:
        return jnp.concatenate([r[...] for r in refs], axis=0)
    own, below, above, down, up, across = refs
    z = lax.div(place_ref[0], inner)
    back = jnp.where(z == 0, across[...], below[...])
    ahead = jnp.where(z == outer - 1, across[...], above[...])
    middle = jnp.where(z < outer // 2, down[...], up[...])
    return jnp.concatenate([own[...], back, middle, ahead], axis=0)


def partner(ep_rank, steps, places, outer, inner):
    z = lax.rem(lax.div(ep_rank, inner) + steps, outer)
    return (z * inner + lax.rem(lax.rem(ep_rank, inner) + places, inner)).astype(jnp.float32)


def x_slots_kernel(place_ref, *refs, outer, inner, capacity, routes):
    outs = refs[-inner - 1 :]
    rows = chunks_of(place_ref, refs[: -inner - 1], outer, inner)
    count, wide = rows.shape
    width = wide - lanes
    block = outer * capacity
    facts = rows[:, width:].astype(jnp.float32)
    chunk = (iota((count, 1), 0) // (count // outer)).astype(jnp.float32)
    slot = iota((count, inner * block), 1).astype(jnp.float32)
    table = jnp.zeros((count, inner * block), jnp.float32)
    chance = jnp.zeros((count, inner * block), jnp.float32)
    for k in range(routes):
        expert = facts[:, k : k + 1]
        rank = facts[:, routes + k : routes + k + 1]
        prob = facts[:, 2 * routes + k : 2 * routes + k + 1]
        prob = prob + facts[:, 3 * routes + k : 3 * routes + k + 1]
        column = jnp.full((count, 1), -1.0, jnp.float32)
        for d in range(inner):
            mine = (expert == partner(place_ref[0], 0, d, outer, inner)) & (rank >= 0.0)
            column = jnp.where(mine, d * block + chunk * capacity + rank, column)
        hit = (slot == column).astype(jnp.float32)
        table = table + hit
        chance = chance + hit * prob
    table = table.astype(jnp.bfloat16)
    outs[-1][...] = table
    chance_high, chance_low = high_low(chance)
    lane = iota((count, lanes), 1)
    scales = jnp.where(
        lane == 2,
        facts[:, 4 * routes : 4 * routes + 1],
        jnp.where(lane == 3, facts[:, 4 * routes + 1 : 4 * routes + 2], 0.0),
    ).astype(jnp.bfloat16)
    kept = (
        contract_first(chance_high, (lane == 0).astype(jnp.bfloat16))
        + contract_first(chance_low, (lane == 1).astype(jnp.bfloat16))
        + contract_first(table, scales)
    ).astype(jnp.bfloat16)
    for d in range(inner):
        part = slice(d * block, (d + 1) * block)
        outs[d][:, :width] = contract_first(table[:, part], rows[:, :width]).astype(jnp.bfloat16)
        outs[d][:, width:] = kept[part]


def q_slots_kernel(place_ref, table_ref, *refs, outer, inner):
    outs = refs[-inner:]
    rows = chunks_of(place_ref, refs[:-inner], outer, inner)
    block = table_ref.shape[1] // inner
    for d in range(inner):
        part = table_ref[:, d * block : (d + 1) * block]
        outs[d][...] = contract_first(part, rows).astype(jnp.bfloat16)


def slot_facts(values):
    values = values.astype(jnp.float32)
    scale = lane_sum(values, 2, 4)
    return scale, scale * lane_sum(values, 0, 2)


def x_kernel(rank_ref, x_ref, gate_ref, up_ref, gated_ref, slope_ref, act_ref):
    del rank_ref
    width = gate_ref.shape[1]
    x = x_ref[:, :width]
    gate_pre = contract_last(x, gate_ref[...])
    up_pre = contract_last(x, up_ref[...])
    squash = jax.nn.sigmoid(sharpness * gate_pre)
    gated = gate_pre * squash
    more = up_pre + 1.0
    gated_ref[0] = gated.astype(jnp.bfloat16)
    slope_ref[0] = (more * (squash + sharpness * gated * (1.0 - squash))).astype(jnp.bfloat16)
    act_ref[0] = (more * gated).astype(jnp.bfloat16)


def q_kernel(rank_ref, q_ref, facts_ref, gate_ref, up_ref, down_ref, gated_ref, slope_ref, act_ref,
             out_ref, sum_ref, prob_ref):
    del rank_ref
    step = pl.program_id(0)
    width = q_ref.shape[1]
    scale, weight = slot_facts(facts_ref[...])
    back_proj = contract_last(q_ref[...], down_ref[...])
    delta = weight * back_proj
    up_delta = (delta * gated_ref[0].astype(jnp.float32)).astype(jnp.bfloat16)
    gate_delta = (delta * slope_ref[0].astype(jnp.float32)).astype(jnp.bfloat16)
    share = jnp.dot(gate_delta, gate_ref[...], preferred_element_type=jnp.float32) + jnp.dot(
        up_delta, up_ref[...], preferred_element_type=jnp.float32
    )
    term = jnp.sum(act_ref[0].astype(jnp.float32) * back_proj, axis=1, keepdims=True)

    @pl.when(step == 0)
    def _():
        sum_ref[...] = share
        prob_ref[...] = term

    @pl.when(step > 0)
    def _():
        sum_ref[...] += share
        prob_ref[...] += term

    @pl.when(step == pl.num_programs(0) - 1)
    def _():
        out_ref[:, :width] = sum_ref[...].astype(jnp.bfloat16)
        high, low = high_low(scale * prob_ref[...])
        lane = iota((out_ref.shape[0], lanes), 1)
        out_ref[:, width:] = jnp.where(
            lane == 0, high.astype(jnp.float32), jnp.where(lane == 1, low.astype(jnp.float32), 0.0)
        ).astype(jnp.bfloat16)


def weight_kernel(rank_ref, *refs, blocks, rows, with_start):
    x_hbm, refs = refs[:blocks], refs[blocks:]
    q_hbm, refs = refs[:blocks], refs[blocks:]
    weights_hbm, refs = refs[:3], refs[3:]
    starts, refs = (refs[:3], refs[3:]) if with_start else ((), refs)
    outs, refs = refs[:3], refs[3:]
    x, q, refs = refs[0], refs[1], refs[2:]
    weights, refs = refs[:3], refs[3:]
    held = refs[:3] if with_start else ()
    sems = refs[-1]
    copies = []

    def fetch(source, target):
        copy = pltpu.make_async_copy(source, target, sems.at[len(copies)])
        copy.start()
        copies.append(copy)
        return copy

    quarter = weights[0].shape[0]
    mine = pl.ds(rank_ref[0] * quarter, quarter)
    first = [fetch(w.at[mine, :], v) for w, v in zip(weights_hbm, weights)]
    first += [fetch(x_hbm[b], x.at[pl.ds(b * rows, rows)]) for b in range(blocks)]
    second = [fetch(q_hbm[b], q.at[pl.ds(b * rows, rows)]) for b in range(blocks)]
    third = [fetch(s, h) for s, h in zip(starts, held)]
    for copy in first:
        copy.wait()
    width = q.shape[1]
    gate_pre = contract_last(x[:, :width], weights[0][...])
    up_pre = contract_last(x[:, :width], weights[1][...])
    for copy in second:
        copy.wait()
    back_proj = contract_last(q[...], weights[2][...])
    _, weight = slot_facts(x[:, width:])
    squash = jax.nn.sigmoid(sharpness * gate_pre)
    gated = gate_pre * squash
    more = up_pre + 1.0
    delta = weight * back_proj
    up_delta = (delta * gated).astype(jnp.bfloat16)
    slope = more * (squash + sharpness * gated * (1.0 - squash))
    gate_delta = (delta * slope).astype(jnp.bfloat16)
    act_scaled = (more * gated * weight).astype(jnp.bfloat16)
    for copy in third:
        copy.wait()
    for i, (left, right) in enumerate(
        ((gate_delta, x[:, :width]), (up_delta, x[:, :width]), (act_scaled, q[...]))
    ):
        total = contract_first(left, right)
        if with_start:
            total = total + held[i][...]
        outs[i][...] = total.astype(outs[i].dtype)


def combine_kernel(place_ref, facts_ref, *refs, routes, outer, inner):
    backs, (grad_ref, prob_ref) = refs[:-2], refs[-2:]
    rows = facts_ref.shape[0]
    capacity, wide = backs[0].shape
    width = wide - lanes
    facts = facts_ref[...].astype(jnp.float32)
    slot = iota((rows, capacity), 1).astype(jnp.float32)
    lane = iota((rows, lanes), 1)
    total = jnp.zeros((rows, width), jnp.float32)
    pairs = jnp.zeros((rows, lanes), jnp.float32)
    for p, back in enumerate(backs):
        expert = partner(place_ref[0], p % outer, p // outer, outer, inner)
        table = jnp.zeros((rows, capacity), jnp.float32)
        where_k = jnp.zeros((rows, 1), jnp.float32) - 1.0
        for k in range(routes):
            mine = facts[:, k : k + 1] == expert
            rank = jnp.where(mine, facts[:, routes + k : routes + k + 1], -1.0)
            table = table + (slot == rank).astype(jnp.float32)
            where_k = jnp.where(mine, float(k), where_k)
        table = table.astype(jnp.bfloat16)
        total = total + jnp.dot(table, back[:, :width], preferred_element_type=jnp.float32)
        term = lane_sum(
            jnp.dot(table, back[:, width:], preferred_element_type=jnp.float32), 0, 2
        )
        pairs = pairs + jnp.where(lane.astype(jnp.float32) == where_k, term, 0.0)
    grad_ref[...] = total.astype(jnp.bfloat16)
    prob_ref[...] = pairs.T[:routes]


def on_device(
    grad_out, tokens, probs, expert_ids, priority, cap_counts, gate_weight, up_weight, down_weight,
    *, outer,
):
    ep_size = lax.axis_size("ep")
    dp_size = lax.axis_size("dp")
    inner = ep_size // outer
    ep_rank = lax.axis_index("ep").astype(jnp.int32)
    rank = lax.axis_index("dp").reshape(1).astype(jnp.int32)
    tok_rows, model_width = tokens.shape
    routes = expert_ids.shape[1]
    hidden = gate_weight.shape[1]
    quarter = hidden // dp_size
    capacity = 5 * routes * tok_rows // (4 * ep_size)
    block = outer * capacity
    wide = model_width + lanes
    w_gate, w_up, w_down = gate_weight[0], up_weight[0], down_weight[0]
    bf16, f32 = jnp.bfloat16, jnp.float32
    shape = jax.ShapeDtypeStruct
    vmem = pl.BlockSpec(memory_space=pltpu.VMEM)
    smem = pl.BlockSpec(memory_space=pltpu.SMEM)
    hbm = pl.BlockSpec(memory_space=pltpu.HBM)

    token_x, token_q = pl.pallas_call(
        functools.partial(prep_kernel, experts=ep_size),
        out_shape=(shape((tok_rows, wide), bf16), shape((tok_rows, model_width), bf16)),
        in_specs=[smem] + [vmem] * 5,
        out_specs=(vmem,) * 2,
        compiler_params=params(),
        name="prep",
    )(cap_counts, expert_ids.T, priority, probs.T, grad_out, tokens)

    def move(rows, target):
        pairs = []
        for zz in range(outer):
            for i in range(inner):
                to = target(zz, i)
                if to is not None:
                    pairs.append((zz * inner + i, to[0] * inner + to[1]))
        return lax.ppermute(rows, "ep", pairs)

    def gather_near(rows):
        if outer != 4:
            return []
        below = move(rows, lambda zz, i: (zz + 1, i) if zz + 1 < outer else None)
        above = move(rows, lambda zz, i: (zz - 1, i) if zz else None)
        return [below, above]

    def gather_far(rows, near):
        if not near:
            back = lambda s: lambda zz, i: ((zz + s) % outer, i)
            return [rows] + [move(rows, back(s)) for s in range(1, outer)]
        below, above = near
        mixed = jnp.where(ep_rank < 2 * inner, below, above)
        across = move(mixed, lambda zz, i: {1: (3, i), 2: (0, i)}.get(zz))
        down = move(above, lambda zz, i: (zz - 1, i) if zz in (1, 2) else None)
        up = move(below, lambda zz, i: (zz + 1, i) if zz in (1, 2) else None)
        return [rows, below, above, down, up, across]

    spot = ep_rank.reshape(1)

    def x_slots(chunks):
        return pl.pallas_call(
            functools.partial(
                x_slots_kernel, outer=outer, inner=inner, capacity=capacity, routes=routes
            ),
            out_shape=(shape((block, wide), bf16),) * inner
            + (shape((outer * tok_rows, inner * block), bf16),),
            in_specs=[smem] + [vmem] * len(chunks),
            out_specs=(vmem,) * (inner + 1),
            compiler_params=params(),
            name="x_slots",
        )(spot, *chunks)

    def q_slots(table, chunks):
        return pl.pallas_call(
            functools.partial(q_slots_kernel, outer=outer, inner=inner),
            out_shape=(shape((block, model_width), bf16),) * inner,
            in_specs=[smem] + [vmem] * (1 + len(chunks)),
            out_specs=(vmem,) * inner,
            compiler_params=params(),
            name="q_slots",
        )(spot, table, *chunks)

    def exchange_inner(parts):
        step = lambda d: lambda zz, i: (zz, (i + d) % inner)
        got = [move(parts[d], step(d)) for d in range(1, inner)]
        return got[0] if inner == 2 else jnp.concatenate(got, axis=0)

    def swap(rows, step):
        return lax.ppermute(rows, "dp", [(d, d ^ step) for d in range(dp_size)])

    def x_part(rows, tiles):
        count = rows.shape[0]
        turn = lambda j, r: ((r[0] + j) % dp_size, 0)
        out = pl.BlockSpec((1, count, quarter), lambda j, r: (j, 0, 0))
        return pl.pallas_call(
            x_kernel,
            grid_spec=pltpu.PrefetchScalarGridSpec(
                num_scalar_prefetch=1,
                grid=(tiles,),
                in_specs=[
                    pl.BlockSpec((count, wide), lambda j, r: (0, 0)),
                    pl.BlockSpec((quarter, model_width), turn),
                    pl.BlockSpec((quarter, model_width), turn),
                ],
                out_specs=(out,) * 3,
            ),
            out_shape=(shape((tiles, count, quarter), bf16),) * 3,
            compiler_params=params(),
            cost_estimate=pl.CostEstimate(
                flops=4 * count * model_width * quarter * tiles,
                bytes_accessed=2 * count * wide + 4 * tiles * quarter * model_width,
                transcendentals=tiles * count * quarter,
            ),
            name="x_part",
        )(rank, rows, w_gate, w_up)

    def q_part(rows_q, rows_x, parts):
        count = rows_q.shape[0]
        turn = lambda j, r: ((r[0] + j) % dp_size, 0)
        tile = pl.BlockSpec((1, count, quarter), lambda j, r: (j, 0, 0))
        return pl.pallas_call(
            q_kernel,
            grid_spec=pltpu.PrefetchScalarGridSpec(
                num_scalar_prefetch=1,
                grid=(dp_size,),
                in_specs=[
                    pl.BlockSpec((count, model_width), lambda j, r: (0, 0)),
                    pl.BlockSpec((count, lanes), lambda j, r: (0, model_width // lanes)),
                    pl.BlockSpec((quarter, model_width), turn),
                    pl.BlockSpec((quarter, model_width), turn),
                    pl.BlockSpec((quarter, model_width), turn),
                    tile,
                    tile,
                    tile,
                ],
                out_specs=pl.BlockSpec((count, wide), lambda j, r: (0, 0)),
                scratch_shapes=[
                    pltpu.VMEM((count, model_width), f32),
                    pltpu.VMEM((count, 1), f32),
                ],
            ),
            out_shape=shape((count, wide), bf16),
            compiler_params=params(),
            cost_estimate=pl.CostEstimate(
                flops=6 * count * model_width * hidden,
                bytes_accessed=6 * hidden * model_width,
                transcendentals=0,
            ),
            name="q_part",
        )(rank, rows_q, rows_x, w_gate, w_up, w_down, *parts)

    def weight_grads(blocks_x, blocks_q, start, out_type):
        counts = [b.shape[0] for b in blocks_x]
        if len(set(counts)) > 1:
            blocks_x, blocks_q = ([jnp.concatenate(b, axis=0)] for b in (blocks_x, blocks_q))
        count, rows = len(blocks_x), sum(counts)
        operands = [*blocks_x, *blocks_q, w_gate, w_up, w_down, *(start or ())]
        scratch = [pltpu.VMEM((rows, wide), bf16), pltpu.VMEM((rows, model_width), bf16)]
        scratch += [pltpu.VMEM((quarter, model_width), bf16)] * 3
        if start:
            scratch += [pltpu.VMEM((quarter, model_width), f32)] * 3
        scratch += [pltpu.SemaphoreType.DMA((len(operands),))]
        return pl.pallas_call(
            functools.partial(
                weight_kernel, blocks=count, rows=rows // count, with_start=start is not None
            ),
            out_shape=(shape((quarter, model_width), out_type),) * 3,
            in_specs=[smem] + [hbm] * len(operands),
            out_specs=(vmem,) * 3,
            scratch_shapes=scratch,
            compiler_params=params(),
            cost_estimate=pl.CostEstimate(
                flops=12 * rows * model_width * quarter,
                bytes_accessed=4 * rows * wide,
                transcendentals=rows * quarter,
            ),
            name="weight_grads",
        )(rank, *operands)

    half = dp_size // 2

    def replicas(rows):
        near = [rows]
        far = [swap(rows, half)]
        step = half // 2
        while step:
            near += [swap(b, step) for b in near]
            far += [swap(b, step) for b in far]
            step //= 2
        return near, far

    near_chunks_x = gather_near(token_x)
    near_chunks_q = gather_near(token_q)
    chunks_x = gather_far(token_x, near_chunks_x)
    chunks_q = gather_far(token_q, near_chunks_q)
    *sends_x, table = x_slots(chunks_x)
    other_x = exchange_inner(sends_x)
    sends_q = q_slots(table, chunks_q)
    other_q = exchange_inner(sends_q)
    same_x, same_q = sends_x[0], sends_q[0]
    near_sx, far_sx = replicas(same_x)
    near_sq, far_sq = replicas(same_q)
    near_ox, far_ox = replicas(other_x)
    near_oq, far_oq = replicas(other_q)

    same_parts = x_part(same_x, dp_size)
    same_back = q_part(same_q, same_x, same_parts)
    other_parts = x_part(other_x, dp_size)
    other_back = q_part(other_q, other_x, other_parts)
    backs = []
    for d in range(inner):
        source = same_back if d == 0 else other_back[(d - 1) * block : d * block]
        for s in range(outer):
            rows = source[s * capacity : (s + 1) * capacity]
            if d or s:
                home = lambda zz, i: ((zz - s) % outer, (i - d) % inner)
                rows = move(rows, home)
            backs.append(rows)
    sums = weight_grads(near_sx + near_ox, near_sq + near_oq, None, f32)
    sums = weight_grads(far_sx, far_sq, sums, f32)
    shares = weight_grads(far_ox, far_oq, sums, bf16)
    input_grad, prob_grad = pl.pallas_call(
        functools.partial(combine_kernel, routes=routes, outer=outer, inner=inner),
        grid=(1,),
        out_shape=(shape((tok_rows, model_width), bf16), shape((routes, tok_rows), f32)),
        in_specs=[
            smem,
            pl.BlockSpec((tok_rows, lanes), lambda j: (0, model_width // lanes)),
        ]
        + [pl.BlockSpec((capacity, wide), lambda j: (0, 0))] * len(backs),
        out_specs=(
            pl.BlockSpec((tok_rows, model_width), lambda j: (0, 0)),
            pl.BlockSpec((routes, tok_rows), lambda j: (0, 0)),
        ),
        compiler_params=params(),
        name="combine",
    )(spot, token_x, *backs)
    return (input_grad, prob_grad.T, *(share[None] for share in shares))


def outer_size(mesh):
    heights = {getattr(d, "coords", (0, 0, 0))[2] for d in mesh.devices.flat}
    return len(heights) if mesh.shape["ep"] % len(heights) == 0 else 1


def solution(mesh):
    def whole(*arrays):
        return on_device(*arrays, outer=outer_size(mesh))

    return jax.shard_map(
        whole,
        mesh=mesh,
        in_specs=(
            P(("ep", "dp"), None),
            P(("ep", "dp"), None),
            P(("ep", "dp"), None),
            P(("ep", "dp"), None),
            P(("ep", "dp"), None),
            P(),
            P("ep", None, None),
            P("ep", None, None),
            P("ep", None, None),
        ),
        out_specs=(
            P(("ep", "dp"), None),
            P(("ep", "dp"), None),
            P("ep", "dp", None),
            P("ep", "dp", None),
            P("ep", "dp", None),
        ),
        check_vma=False,
    )
```

profile of v0, /device:TPU:0, one launch (start us, length us, event | category | flops | bytes accessed | tf_op | source)
XLA Modules:
  0.0 240.4 jit_solution(13366104062875398205)
XLA Ops:
  0.6 2.6 %prep.1 = (bf16[128,1664]{1,0:T(8,128)(2,1)}, bf16[128,1536]{1,0:T(8,128)(2,1)}) custom-call(s32[8]{0:T(128)} %cap_ref.1, s32[4,128]{1,0:T(4,128)} %bitcast.30, s32[1,128]{1,0:T(1,128)} %order_ref.1, f32[4,128]{1,0:T(4,128)} %bitcast.31, f32[128,1536]{1,0:T(8,128)} %grad_ref.1, bf16[128,1536]{1,0:T(8,128)(2,1)} %tok_ref.1), custom_call_target="tpu_custom_call" | custom-call | tf_op jit(solution)/shard_map/prep/pallas_call | solution.py:312
  3.2 5.0 %collective-permute-start = (bf16[128,1664]{1,0:T(8,128)(2,1)}, bf16[128,1664]{1,0:T(8,128)(2,1)S(1)}, u32[]{:S(2)}, u32[]{:S(2)}) collective-permute-start(bf16[128,1664]{1,0:T(8,128)(2,1)} %get-tuple-element.29.refs_0_.facts_ref), channel_id=1, source_target_pairs={{0,8},{4,12},{8,16},{12,20},{16,24},{20,28},{1,9},{5,13},{9,17},{1... | collective-permute-start | bytes 1277960 | tf_op jit(solution)/shard_map/ppermute | solution.py:328
  8.2 1.3 collective-permute-start.1
  9.5 4.6 %collective-permute-start.5 = (bf16[128,1536]{1,0:T(8,128)(2,1)}, bf16[128,1536]{1,0:T(8,128)(2,1)S(1)}, u32[]{:S(2)}, u32[]{:S(2)}) collective-permute-start(bf16[128,1536]{1,0:T(8,128)(2,1)} %get-tuple-element.31.refs_0_), channel_id=1, source_target_pairs={{0,8},{4,12},{8,16},{12,20},{16,24},{20,28},{1,9},{5,13},{9,17},{1... | collective-permute-start | bytes 1179656 | tf_op jit(solution)/shard_map/ppermute | solution.py:328
  14.0 1.3 collective-permute-start.6
  15.3 3.3 %collective-permute-done.refs_1_ = bf16[128,1664]{1,0:T(8,128)(2,1)S(1)} collective-permute-done((bf16[128,1664]{1,0:T(8,128)(2,1)}, bf16[128,1664]{1,0:T(8,128)(2,1)S(1)}, u32[]{:S(2)}, u32[]{:S(2)}) %collective-permute-start) | collective-permute-done | bytes 426016 | tf_op jit(solution)/shard_map/ppermute | solution.py:328
  18.6 4.3 %collective-permute-done.1.refs_2_ = bf16[128,1664]{1,0:T(8,128)(2,1)S(1)} collective-permute-done((bf16[128,1664]{1,0:T(8,128)(2,1)}, bf16[128,1664]{1,0:T(8,128)(2,1)S(1)}, u32[]{:S(2)}, u32[]{:S(2)}) %collective-permute-start.1) | collective-permute-done | bytes 426016 | tf_op jit(solution)/shard_map/ppermute | solution.py:328
  23.0 1.3 collective-permute-start.4
  24.3 1.3 collective-permute-start.2
  25.6 0.7 collective-permute-start.3
  26.3 13.1 %collective-permute-done.6.refs_2_ = bf16[128,1536]{1,0:T(8,128)(2,1)S(1)} collective-permute-done((bf16[128,1536]{1,0:T(8,128)(2,1)}, bf16[128,1536]{1,0:T(8,128)(2,1)S(1)}, u32[]{:S(2)}, u32[]{:S(2)}) %collective-permute-start.6) | collective-permute-done | bytes 393248 | tf_op jit(solution)/shard_map/ppermute | solution.py:328
  39.5 0.9 broadcast_select_fusion.1
  40.4 1.3 collective-permute-start.9
  41.6 1.3 collective-permute-start.7
  43.0 1.4 collective-permute-start.8
  44.4 12.6 %collective-permute-done.2.refs_3_ = bf16[128,1664]{1,0:T(8,128)(2,1)S(1)} collective-permute-done((bf16[128,1664]{1,0:T(8,128)(2,1)S(1)}, bf16[128,1664]{1,0:T(8,128)(2,1)S(1)}, u32[]{:S(2)}, u32[]{:S(2)}) %collective-permute-start.2) | collective-permute-done | bytes 426016 | tf_op jit(solution)/shard_map/ppermute | solution.py:328
  57.0 0.8 copy-done.16
  57.9 6.0 %x_slots.1 = (bf16[320,1664]{1,0:T(8,128)(2,1)}, bf16[320,1664]{1,0:T(8,128)(2,1)}, bf16[512,640]{1,0:T(8,128)(2,1)}) custom-call(s32[1]{0:T(128)} %bitcast.place_ref, bf16[128,1664]{1,0:T(8,128)(2,1)} %get-tuple-element.29.refs_0_.facts_ref, bf16[128,1664]{1,0:T(8,128)(2,1)} %copy-done, bf16[128,1664]{1,0:T(8,128)(2,1)} %copy-done.1, ...), custom_call_target="tpu_custom_call" | custom-call | tf_op jit(solution)/shard_map/x_slots/pallas_call | solution.py:351
  63.9 1.3 collective-permute-done.7.refs_3_
  65.2 4.0 %q_slots.1 = (bf16[320,1536]{1,0:T(8,128)(2,1)}, bf16[320,1536]{1,0:T(8,128)(2,1)}) custom-call(s32[1]{0:T(128)} %bitcast.place_ref, bf16[512,640]{1,0:T(8,128)(2,1)} %get-tuple-element.30.table_ref, bf16[128,1536]{1,0:T(8,128)(2,1)} %get-tuple-element.31.refs_0_, bf16[128,1536]{1,0:T(8,128)(2,1)} %copy-done.2, bf16[128,1536]{1,0:T(8,128)(2,1)} %copy-done.3, ...), custom_call_target="tpu_custom_call" | custom-call | tf_op jit(solution)/shard_map/q_slots/pallas_call | solution.py:364
  69.2 1.5 collective-permute-start.25
  70.8 1.5 collective-permute-start.13
  72.8 8.4 %x_part.2 = (bf16[4,320,384]{2,1,0:T(8,128)(2,1)}, bf16[4,320,384]{2,1,0:T(8,128)(2,1)}, bf16[4,320,384]{2,1,0:T(8,128)(2,1)}) custom-call(s32[1]{0:T(128)} %bitcast.3.rank_ref, bf16[320,1664]{1,0:T(8,128)(2,1)} %get-tuple-element.33.x_ref.facts_ref.refs_0_, bf16[1536,1536]{1,0:T(8,128)(2,1)} %bitcast.11, bf16[1536,1536]{1,0:T(8,128)(2,1)} %bitcast.18), custom_call_target="tpu_custom_call" | custom-call | flops 3019898880 | bytes 10502144 | tf_op jit(solution)/shard_map/x_part/pallas_call | solution.py:385
  81.2 12.3 %q_part.2 = bf16[320,1664]{1,0:T(8,128)(2,1)} custom-call(s32[1]{0:T(128)} %bitcast.3.rank_ref, bf16[320,1536]{1,0:T(8,128)(2,1)} %get-tuple-element.32.q_ref.refs_4_, bf16[320,1664]{1,0:T(8,128)(2,1)} %get-tuple-element.33.x_ref.facts_ref.refs_0_, bf16[1536,1536]{1,0:T(8,128)(2,1)} %bitcast.12, bf16[1536,1536]{1,0:T(8,128)(2,1)} %bitcast.19, ...), custom_call_target="tpu_custom_call" | custom-call | flops 4529848320 | bytes 14155776 | tf_op jit(solution)/shard_map/q_part/pallas_call | solution.py:411
  93.6 2.0 fusion.1
  95.5 22.1 %collective-permute-done.14.x_ref.facts_ref.refs_2_ = bf16[320,1664]{1,0:T(8,128)(2,1)S(1)} collective-permute-done((bf16[320,1664]{1,0:T(8,128)(2,1)S(1)}, bf16[320,1664]{1,0:T(8,128)(2,1)S(1)}, u32[]{:S(2)}, u32[]{:S(2)}) %collective-permute-start.14) | collective-permute-done | bytes 1064992 | tf_op jit(solution)/shard_map/ppermute | solution.py:328
  118.7 8.4 %x_part.3 = (bf16[4,320,384]{2,1,0:T(8,128)(2,1)}, bf16[4,320,384]{2,1,0:T(8,128)(2,1)}, bf16[4,320,384]{2,1,0:T(8,128)(2,1)}) custom-call(s32[1]{0:T(128)} %bitcast.3.rank_ref, bf16[320,1664]{1,0:T(8,128)(2,1)} %copy-done.4, bf16[1536,1536]{1,0:T(8,128)(2,1)} %bitcast.13, bf16[1536,1536]{1,0:T(8,128)(2,1)} %bitcast.20), custom_call_target="tpu_custom_call" | custom-call | flops 3019898880 | bytes 10502144 | tf_op jit(solution)/shard_map/x_part/pallas_call | solution.py:385
  127.7 2.1 collective-permute-start.11
  129.8 12.3 %q_part.3 = bf16[320,1664]{1,0:T(8,128)(2,1)} custom-call(s32[1]{0:T(128)} %bitcast.3.rank_ref, bf16[320,1536]{1,0:T(8,128)(2,1)} %copy-done.11, bf16[320,1664]{1,0:T(8,128)(2,1)} %copy-done.4, bf16[1536,1536]{1,0:T(8,128)(2,1)} %bitcast.14, bf16[1536,1536]{1,0:T(8,128)(2,1)} %bitcast.21, bf16[1536,1536]{1,0:T(8,128)(2,1)} %bitcast.26, ...), custom_call_target="tpu_custom_call" | custom-call | flops 4529848320 | bytes 14155776 | tf_op jit(solution)/shard_map/q_part/pallas_call | solution.py:411
  142.7 1.5 fusion
  144.1 6.7 %collective-permute-done.12.refs_3_ = bf16[80,1664]{1,0:T(8,128)(2,1)S(1)} collective-permute-done((bf16[80,1664]{1,0:T(8,128)(2,1)S(1)}, bf16[80,1664]{1,0:T(8,128)(2,1)S(1)}, u32[]{:S(2)}, u32[]{:S(2)}) %collective-permute-start.12) | collective-permute-done | bytes 266272 | tf_op jit(solution)/shard_map/ppermute | solution.py:328
  150.8 1.5 collective-permute-start.15
  152.4 0.9 copy-done.27
  153.3 1.6 collective-permute-start.19
  155.3 2.0 collective-permute-done.15.refs_4_
  157.3 6.3 %collective-permute-start.21 = (bf16[320,1536]{1,0:T(8,128)(2,1)S(1)}, bf16[320,1536]{1,0:T(8,128)(2,1)S(1)}, u32[]{:S(2)}, u32[]{:S(2)}) collective-permute-start(bf16[320,1536]{1,0:T(8,128)(2,1)S(1)} %copy-done.12), channel_id=1, source_target_pairs={{0,2},{1,3},{2,0},{3,1},{4,6},{5,7},{6,4},{7,5},{8,10},{9,11},{10,... | collective-permute-start | bytes 2949128 | tf_op jit(solution)/shard_map/ppermute | solution.py:379
  163.5 1.1 collective-permute-done.16.refs_5_
  164.8 13.8 %collective-permute-done.17.refs_6_ = bf16[80,1664]{1,0:T(8,128)(2,1)S(1)} collective-permute-done((bf16[80,1664]{1,0:T(8,128)(2,1)S(1)}, bf16[80,1664]{1,0:T(8,128)(2,1)S(1)}, u32[]{:S(2)}, u32[]{:S(2)}) %collective-permute-start.17) | collective-permute-done | bytes 266272 | tf_op jit(solution)/shard_map/ppermute | solution.py:328
  178.7 0.7 copy-done.24
  179.4 10.3 %collective-permute-done.18.refs_7_ = bf16[80,1664]{1,0:T(8,128)(2,1)S(1)} collective-permute-done((bf16[80,1664]{1,0:T(8,128)(2,1)S(1)}, bf16[80,1664]{1,0:T(8,128)(2,1)S(1)}, u32[]{:S(2)}, u32[]{:S(2)}) %collective-permute-start.18) | collective-permute-done | bytes 266272 | tf_op jit(solution)/shard_map/ppermute | solution.py:328
  189.7 1.0 copy-done.28
  191.1 4.3 %combine.1 = (bf16[128,1536]{1,0:T(8,128)(2,1)}, f32[4,128]{1,0:T(4,128)}) custom-call(s32[1]{0:T(128)} %bitcast.place_ref, bf16[128,1664]{1,0:T(8,128)(2,1)} %get-tuple-element.29.refs_0_.facts_ref, bf16[80,1664]{1,0:T(8,128)(2,1)} %get-tuple-element.60.refs_0_, bf16[80,1664]{1,0:T(8,128)(2,1)} %copy-done.19, bf16[80,1664]{1,0:T(8,128)(2,1)} %copy-done.20, ...), custom_call_target="tpu_custom_call" | custom-call | tf_op jit(solution)/shard_map/combine/pallas_call | solution.py:512
  195.5 4.0 %collective-permute-done.21.refs_2_ = bf16[320,1536]{1,0:T(8,128)(2,1)S(1)} collective-permute-done((bf16[320,1536]{1,0:T(8,128)(2,1)S(1)}, bf16[320,1536]{1,0:T(8,128)(2,1)S(1)}, u32[]{:S(2)}, u32[]{:S(2)}) %collective-permute-start.21) | collective-permute-done | bytes 983072 | tf_op jit(solution)/shard_map/ppermute | solution.py:379
  200.0 16.5 %weight_grads.3 = (f32[384,1536]{1,0:T(8,128)}, f32[384,1536]{1,0:T(8,128)}, f32[384,1536]{1,0:T(8,128)}) custom-call(s32[1]{0:T(128)} %bitcast.3.rank_ref, bf16[320,1664]{1,0:T(8,128)(2,1)} %get-tuple-element.33.x_ref.facts_ref.refs_0_, bf16[320,1664]{1,0:T(8,128)(2,1)} %collective-permute-done.27.refs_1_, bf16[320,1664]{1,0:T(8,128)(2,1)} %copy-done.4, ...), custom_call_target="tpu_custom_call" | custom-call | flops 9059696640 | bytes 8519680 | tf_op jit(solution)/shard_map/weight_grads/pallas_call | solution.py:453
  216.6 1.0 copy-done.8
  217.6 10.9 %weight_grads.4 = (f32[384,1536]{1,0:T(8,128)}, f32[384,1536]{1,0:T(8,128)}, f32[384,1536]{1,0:T(8,128)}) custom-call(s32[1]{0:T(128)} %bitcast.3.rank_ref, bf16[320,1664]{1,0:T(8,128)(2,1)} %copy-done.6, bf16[320,1664]{1,0:T(8,128)(2,1)} %copy-done.8, bf16[320,1536]{1,0:T(8,128)(2,1)} %copy-done.10, bf16[320,1536]{1,0:T(8,128)(2,1)} %collective-permute-done.26.refs_3_, ...), custom_call_target="tpu_custom_call" | custom-call | flops 4529848320 | bytes 4259840 | tf_op jit(solution)/shard_map/weight_grads/pallas_call | solution.py:453
  228.6 0.9 copy-done.14
  229.9 10.4 %weight_grads.5 = (bf16[384,1536]{1,0:T(8,128)(2,1)}, bf16[384,1536]{1,0:T(8,128)(2,1)}, bf16[384,1536]{1,0:T(8,128)(2,1)}) custom-call(s32[1]{0:T(128)} %bitcast.3.rank_ref, bf16[320,1664]{1,0:T(8,128)(2,1)} %copy-done.7, bf16[320,1664]{1,0:T(8,128)(2,1)} %copy-done.9, bf16[320,1536]{1,0:T(8,128)(2,1)} %copy-done.13, bf16[320,1536]{1,0:T(8,128)(2,1)} %copy-done.14, ...), custom_call_target="tpu_custom_call" | custom-call | flops 4529848320 | bytes 4259840 | tf_op jit(solution)/shard_map/weight_grads/pallas_call | solution.py:453
  (87 shorter events, 4.9 us)
Async XLA Ops:
  3.2 15.5 %collective-permute-start = (bf16[128,1664]{1,0:T(8,128)(2,1)}, bf16[128,1664]{1,0:T(8,128)(2,1)S(1)}, u32[]{:S(2)}, u32[]{:S(2)}) collective-permute-start(bf16[128,1664]{1,0:T(8,128)(2,1)} %get-tuple-element.29.refs_0_.facts_ref), channel_id=1, source_target_pairs={{0,8},{4,12},{8,16},{12,20},{16,24},{20,28},{1,9},{5,13},{9,17},{1... | collective-permute-start | bytes 1277960 | tf_op jit(solution)/shard_map/ppermute | solution.py:328
  8.2 14.8 %collective-permute-start.1 = (bf16[128,1664]{1,0:T(8,128)(2,1)}, bf16[128,1664]{1,0:T(8,128)(2,1)S(1)}, u32[]{:S(2)}, u32[]{:S(2)}) collective-permute-start(bf16[128,1664]{1,0:T(8,128)(2,1)} %get-tuple-element.29.refs_0_.facts_ref), channel_id=1, source_target_pairs={{8,0},{12,4},{16,8},{20,12},{24,16},{28,20},{9,1},{13,5},{17,9},{2... | collective-permute-start | bytes 1277960 | tf_op jit(solution)/shard_map/ppermute | solution.py:328
  9.5 16.8 %collective-permute-start.5 = (bf16[128,1536]{1,0:T(8,128)(2,1)}, bf16[128,1536]{1,0:T(8,128)(2,1)S(1)}, u32[]{:S(2)}, u32[]{:S(2)}) collective-permute-start(bf16[128,1536]{1,0:T(8,128)(2,1)} %get-tuple-element.31.refs_0_), channel_id=1, source_target_pairs={{0,8},{4,12},{8,16},{12,20},{16,24},{20,28},{1,9},{5,13},{9,17},{1... | collective-permute-start | bytes 1179656 | tf_op jit(solution)/shard_map/ppermute | solution.py:328
  14.0 25.4 %collective-permute-start.6 = (bf16[128,1536]{1,0:T(8,128)(2,1)}, bf16[128,1536]{1,0:T(8,128)(2,1)S(1)}, u32[]{:S(2)}, u32[]{:S(2)}) collective-permute-start(bf16[128,1536]{1,0:T(8,128)(2,1)} %get-tuple-element.31.refs_0_), channel_id=1, source_target_pairs={{8,0},{12,4},{16,8},{20,12},{24,16},{28,20},{9,1},{13,5},{17,9},{2... | collective-permute-start | bytes 1179656 | tf_op jit(solution)/shard_map/ppermute | solution.py:328
  18.6 21.7 %copy-start = (bf16[128,1664]{1,0:T(8,128)(2,1)}, bf16[128,1664]{1,0:T(8,128)(2,1)S(1)}, u32[]{:S(2)}) copy-start(bf16[128,1664]{1,0:T(8,128)(2,1)S(1)} %collective-permute-done.refs_1_) | copy-start | bytes 1277956
  23.0 17.4 %copy-start.1 = (bf16[128,1664]{1,0:T(8,128)(2,1)}, bf16[128,1664]{1,0:T(8,128)(2,1)S(1)}, u32[]{:S(2)}) copy-start(bf16[128,1664]{1,0:T(8,128)(2,1)S(1)} %collective-permute-done.1.refs_2_) | copy-start | bytes 1277956
  23.0 19.9 %collective-permute-start.4 = (bf16[128,1664]{1,0:T(8,128)(2,1)S(1)}, bf16[128,1664]{1,0:T(8,128)(2,1)S(1)}, u32[]{:S(2)}, u32[]{:S(2)}) collective-permute-start(bf16[128,1664]{1,0:T(8,128)(2,1)S(1)} %broadcast_select_fusion), channel_id=1, source_target_pairs={{8,24},{12,28},{16,0},{20,4},{9,25},{13,29},{17,1},{21,5},{10,26},... | collective-permute-start | bytes 1277960 | tf_op jit(solution)/shard_map/ppermute | solution.py:328
  24.3 32.7 %collective-permute-start.2 = (bf16[128,1664]{1,0:T(8,128)(2,1)S(1)}, bf16[128,1664]{1,0:T(8,128)(2,1)S(1)}, u32[]{:S(2)}, u32[]{:S(2)}) collective-permute-start(bf16[128,1664]{1,0:T(8,128)(2,1)S(1)} %collective-permute-done.1.refs_2_), channel_id=1, source_target_pairs={{8,0},{12,4},{16,8},{20,12},{9,1},{13,5},{17,9},{21,13},{10,2},{14... | collective-permute-start | bytes 1277960 | tf_op jit(solution)/shard_map/ppermute | solution.py:328
  25.6 31.4 %collective-permute-start.3 = (bf16[128,1664]{1,0:T(8,128)(2,1)S(1)}, bf16[128,1664]{1,0:T(8,128)(2,1)S(1)}, u32[]{:S(2)}, u32[]{:S(2)}) collective-permute-start(bf16[128,1664]{1,0:T(8,128)(2,1)S(1)} %collective-permute-done.refs_1_), channel_id=1, source_target_pairs={{8,16},{12,20},{16,24},{20,28},{9,17},{13,21},{17,25},{21,29},{10,... | collective-permute-start | bytes 1277960 | tf_op jit(solution)/shard_map/ppermute | solution.py:328
  26.3 37.6 %copy-start.2 = (bf16[128,1536]{1,0:T(8,128)(2,1)}, bf16[128,1536]{1,0:T(8,128)(2,1)S(1)}, u32[]{:S(2)}) copy-start(bf16[128,1536]{1,0:T(8,128)(2,1)S(1)} %collective-permute-done.5.refs_1_) | copy-start | bytes 1179652
  39.5 24.4 %copy-start.3 = (bf16[128,1536]{1,0:T(8,128)(2,1)}, bf16[128,1536]{1,0:T(8,128)(2,1)S(1)}, u32[]{:S(2)}) copy-start(bf16[128,1536]{1,0:T(8,128)(2,1)S(1)} %collective-permute-done.6.refs_2_) | copy-start | bytes 1179652
  40.4 23.5 %collective-permute-start.9 = (bf16[128,1536]{1,0:T(8,128)(2,1)}, bf16[128,1536]{1,0:T(8,128)(2,1)S(1)}, u32[]{:S(2)}, u32[]{:S(2)}) collective-permute-start(bf16[128,1536]{1,0:T(8,128)(2,1)} %broadcast_select_fusion.1), channel_id=1, source_target_pairs={{8,24},{12,28},{16,0},{20,4},{9,25},{13,29},{17,1},{21,5},{10,26},... | collective-permute-start | bytes 1179656 | tf_op jit(solution)/shard_map/ppermute | solution.py:328
  41.6 23.5 %collective-permute-start.7 = (bf16[128,1536]{1,0:T(8,128)(2,1)S(1)}, bf16[128,1536]{1,0:T(8,128)(2,1)}, u32[]{:S(2)}, u32[]{:S(2)}) collective-permute-start(bf16[128,1536]{1,0:T(8,128)(2,1)S(1)} %collective-permute-done.6.refs_2_), channel_id=1, source_target_pairs={{8,0},{12,4},{16,8},{20,12},{9,1},{13,5},{17,9},{21,13},{10,2},{14... | collective-permute-start | bytes 1179656 | tf_op jit(solution)/shard_map/ppermute | solution.py:328
  43.0 14.0 %copy-start.15 = (bf16[128,1664]{1,0:T(8,128)(2,1)}, bf16[128,1664]{1,0:T(8,128)(2,1)S(1)}, u32[]{:S(2)}) copy-start(bf16[128,1664]{1,0:T(8,128)(2,1)S(1)} %collective-permute-done.4.refs_5_) | copy-start | bytes 1277956
  43.0 22.2 %collective-permute-start.8 = (bf16[128,1536]{1,0:T(8,128)(2,1)S(1)}, bf16[128,1536]{1,0:T(8,128)(2,1)}, u32[]{:S(2)}, u32[]{:S(2)}) collective-permute-start(bf16[128,1536]{1,0:T(8,128)(2,1)S(1)} %collective-permute-done.5.refs_1_), channel_id=1, source_target_pairs={{8,16},{12,20},{16,24},{20,28},{9,17},{13,21},{17,25},{21,29},{10,... | collective-permute-start | bytes 1179656 | tf_op jit(solution)/shard_map/ppermute | solution.py:328
  65.2 7.1 %copy-start.26 = (bf16[320,1664]{1,0:T(8,128)(2,1)S(1)}, bf16[320,1664]{1,0:T(8,128)(2,1)}, u32[]{:S(2)}) copy-start(bf16[320,1664]{1,0:T(8,128)(2,1)} %get-tuple-element.38) | copy-start | bytes 3194884
  69.2 83.1 %collective-permute-start.29 = (bf16[320,1536]{1,0:T(8,128)(2,1)}, bf16[320,1536]{1,0:T(8,128)(2,1)S(1)}, u32[]{:S(2)}, u32[]{:S(2)}) collective-permute-start(bf16[320,1536]{1,0:T(8,128)(2,1)} %get-tuple-element.32.q_ref.refs_4_), channel_id=1, source_target_pairs={{0,1},{1,0},{2,3},{3,2},{4,5},{5,4},{6,7},{7,6},{8,9},{9,8},{10,11... | collective-permute-start | bytes 2949128 | tf_op jit(solution)/shard_map/ppermute | solution.py:379
  69.2 84.1 %collective-permute-start.25 = (bf16[320,1536]{1,0:T(8,128)(2,1)}, bf16[320,1536]{1,0:T(8,128)(2,1)S(1)}, u32[]{:S(2)}, u32[]{:S(2)}) collective-permute-start(bf16[320,1536]{1,0:T(8,128)(2,1)} %get-tuple-element.32.q_ref.refs_4_), channel_id=1, source_target_pairs={{0,2},{1,3},{2,0},{3,1},{4,6},{5,7},{6,4},{7,5},{8,10},{9,11},{10,... | collective-permute-start | bytes 2949128 | tf_op jit(solution)/shard_map/ppermute | solution.py:379
  70.8 56.9 %collective-permute-start.13 = (bf16[320,1536]{1,0:T(8,128)(2,1)}, bf16[320,1536]{1,0:T(8,128)(2,1)S(1)}, u32[]{:S(2)}, u32[]{:S(2)}) collective-permute-start(bf16[320,1536]{1,0:T(8,128)(2,1)} %get-tuple-element.37), channel_id=1, source_target_pairs={{0,4},{4,0},{8,12},{12,8},{16,20},{20,16},{24,28},{28,24},{1,5},{5... | collective-permute-start | bytes 2949128 | tf_op jit(solution)/shard_map/ppermute | solution.py:328
  72.3 45.4 %collective-permute-start.14 = (bf16[320,1664]{1,0:T(8,128)(2,1)S(1)}, bf16[320,1664]{1,0:T(8,128)(2,1)S(1)}, u32[]{:S(2)}, u32[]{:S(2)}) collective-permute-start(bf16[320,1664]{1,0:T(8,128)(2,1)S(1)} %copy-done.26), channel_id=1, source_target_pairs={{0,4},{4,0},{8,12},{12,8},{16,20},{20,16},{24,28},{28,24},{1,5},{5... | collective-permute-start | bytes 3194888 | tf_op jit(solution)/shard_map/ppermute | solution.py:328
  72.8 82.1 %collective-permute-start.27 = (bf16[320,1664]{1,0:T(8,128)(2,1)}, bf16[320,1664]{1,0:T(8,128)(2,1)}, u32[]{:S(2)}, u32[]{:S(2)}) collective-permute-start(bf16[320,1664]{1,0:T(8,128)(2,1)} %get-tuple-element.33.x_ref.facts_ref.refs_0_), channel_id=1, source_target_pairs={{0,1},{1,0},{2,3},{3,2},{4,5},{5,4},{6,7},{7,6},{8,9},{9,8},{10,11... | collective-permute-start | bytes 3194888 | tf_op jit(solution)/shard_map/ppermute | solution.py:379
  117.7 9.4 %collective-permute-start.10 = (bf16[80,1664]{1,0:T(8,128)(2,1)S(1)}, bf16[80,1664]{1,0:T(8,128)(2,1)S(1)}, u32[]{:S(2)}, u32[]{:S(2)}) collective-permute-start(bf16[80,1664]{1,0:T(8,128)(2,1)S(1)} %get-tuple-element.59), channel_id=1, source_target_pairs={{0,24},{4,28},{8,0},{12,4},{16,8},{20,12},{24,16},{28,20},{1,25},{... | collective-permute-start | bytes 798728 | tf_op jit(solution)/shard_map/ppermute | solution.py:328
  127.1 15.1 %copy-start.19 = (bf16[80,1664]{1,0:T(8,128)(2,1)}, bf16[80,1664]{1,0:T(8,128)(2,1)S(1)}, u32[]{:S(2)}) copy-start(bf16[80,1664]{1,0:T(8,128)(2,1)S(1)} %collective-permute-done.10.refs_1_) | copy-start | bytes 798724
  127.1 27.9 %collective-permute-start.23 = (bf16[320,1664]{1,0:T(8,128)(2,1)}, bf16[320,1664]{1,0:T(8,128)(2,1)S(1)}, u32[]{:S(2)}, u32[]{:S(2)}) collective-permute-start(bf16[320,1664]{1,0:T(8,128)(2,1)} %get-tuple-element.33.x_ref.facts_ref.refs_0_), channel_id=1, source_target_pairs={{0,2},{1,3},{2,0},{3,1},{4,6},{5,7},{6,4},{7,5},{8,10},{9,11},{10,... | collective-permute-start | bytes 3194888 | tf_op jit(solution)/shard_map/ppermute | solution.py:379
  127.7 2.1 copy-start.11
  127.7 14.5 %collective-permute-start.11 = (bf16[80,1664]{1,0:T(8,128)(2,1)S(1)}, bf16[80,1664]{1,0:T(8,128)(2,1)S(1)}, u32[]{:S(2)}, u32[]{:S(2)}) collective-permute-start(bf16[80,1664]{1,0:T(8,128)(2,1)S(1)} %get-tuple-element.58), channel_id=1, source_target_pairs={{0,16},{4,20},{8,24},{12,28},{16,0},{20,4},{24,8},{28,12},{1,17},{... | collective-permute-start | bytes 798728 | tf_op jit(solution)/shard_map/ppermute | solution.py:328
  142.1 10.2 %copy-start.12 = (bf16[320,1536]{1,0:T(8,128)(2,1)S(1)}, bf16[320,1536]{1,0:T(8,128)(2,1)}, u32[]{:S(2)}) copy-start(bf16[320,1536]{1,0:T(8,128)(2,1)} %copy-done.11) | copy-start | bytes 2949124
  142.2 11.2 %copy-start.5 = (bf16[320,1664]{1,0:T(8,128)(2,1)S(1)}, bf16[320,1664]{1,0:T(8,128)(2,1)}, u32[]{:S(2)}) copy-start(bf16[320,1664]{1,0:T(8,128)(2,1)} %copy-done.4) | copy-start | bytes 3194884
  142.2 8.7 %collective-permute-start.12 = (bf16[80,1664]{1,0:T(8,128)(2,1)S(1)}, bf16[80,1664]{1,0:T(8,128)(2,1)S(1)}, u32[]{:S(2)}, u32[]{:S(2)}) collective-permute-start(bf16[80,1664]{1,0:T(8,128)(2,1)S(1)} %get-tuple-element.57), channel_id=1, source_target_pairs={{0,8},{4,12},{8,16},{12,20},{16,24},{20,28},{24,0},{28,4},{1,9},{5... | collective-permute-start | bytes 798728 | tf_op jit(solution)/shard_map/ppermute | solution.py:328
  150.8 40.3 %copy-start.21 = (bf16[80,1664]{1,0:T(8,128)(2,1)}, bf16[80,1664]{1,0:T(8,128)(2,1)S(1)}, u32[]{:S(2)}) copy-start(bf16[80,1664]{1,0:T(8,128)(2,1)S(1)} %collective-permute-done.12.refs_3_) | copy-start | bytes 798724
  150.8 6.4 %collective-permute-start.15 = (bf16[80,1664]{1,0:T(8,128)(2,1)S(1)}, bf16[80,1664]{1,0:T(8,128)(2,1)S(1)}, u32[]{:S(2)}, u32[]{:S(2)}) collective-permute-start(bf16[80,1664]{1,0:T(8,128)(2,1)S(1)} %get-tuple-element.56), channel_id=1, source_target_pairs={{0,4},{4,0},{8,12},{12,8},{16,20},{20,16},{24,28},{28,24},{1,5},{5... | collective-permute-start | bytes 798728 | tf_op jit(solution)/shard_map/ppermute | solution.py:328
  152.4 37.3 %collective-permute-start.30 = (bf16[320,1536]{1,0:T(8,128)(2,1)S(1)}, bf16[320,1536]{1,0:T(8,128)(2,1)S(1)}, u32[]{:S(2)}, u32[]{:S(2)}) collective-permute-start(bf16[320,1536]{1,0:T(8,128)(2,1)S(1)} %copy-done.12), channel_id=1, source_target_pairs={{0,1},{1,0},{2,3},{3,2},{4,5},{5,4},{6,7},{7,6},{8,9},{9,8},{10,11... | collective-permute-start | bytes 2949128 | tf_op jit(solution)/shard_map/ppermute | solution.py:379
  153.3 42.1 %copy-start.10 = (bf16[320,1536]{1,0:T(8,128)(2,1)}, bf16[320,1536]{1,0:T(8,128)(2,1)S(1)}, u32[]{:S(2)}) copy-start(bf16[320,1536]{1,0:T(8,128)(2,1)S(1)} %collective-permute-done.25.refs_2_) | copy-start | bytes 2949124
  153.3 46.2 %collective-permute-start.19 = (bf16[320,1664]{1,0:T(8,128)(2,1)S(1)}, bf16[320,1664]{1,0:T(8,128)(2,1)S(1)}, u32[]{:S(2)}, u32[]{:S(2)}) collective-permute-start(bf16[320,1664]{1,0:T(8,128)(2,1)S(1)} %copy-done.5), channel_id=1, source_target_pairs={{0,2},{1,3},{2,0},{3,1},{4,6},{5,7},{6,4},{7,5},{8,10},{9,11},{10,... | collective-permute-start | bytes 3194888 | tf_op jit(solution)/shard_map/ppermute | solution.py:379
  154.9 45.1 %collective-permute-start.28 = (bf16[320,1664]{1,0:T(8,128)(2,1)S(1)}, bf16[320,1664]{1,0:T(8,128)(2,1)}, u32[]{:S(2)}, u32[]{:S(2)}) collective-permute-start(bf16[320,1664]{1,0:T(8,128)(2,1)S(1)} %copy-done.5), channel_id=1, source_target_pairs={{0,1},{1,0},{2,3},{3,2},{4,5},{5,4},{6,7},{7,6},{8,9},{9,8},{10,11... | collective-permute-start | bytes 3194888 | tf_op jit(solution)/shard_map/ppermute | solution.py:379
  154.9 40.5 %copy-start.6 = (bf16[320,1664]{1,0:T(8,128)(2,1)}, bf16[320,1664]{1,0:T(8,128)(2,1)S(1)}, u32[]{:S(2)}) copy-start(bf16[320,1664]{1,0:T(8,128)(2,1)S(1)} %collective-permute-done.23.refs_0_) | copy-start | bytes 3194884
  154.9 9.7 %collective-permute-start.16 = (bf16[80,1664]{1,0:T(8,128)(2,1)S(1)}, bf16[80,1664]{1,0:T(8,128)(2,1)S(1)}, u32[]{:S(2)}, u32[]{:S(2)}) collective-permute-start(bf16[80,1664]{1,0:T(8,128)(2,1)S(1)} %get-tuple-element.55), channel_id=1, source_target_pairs={{0,28},{4,24},{8,4},{12,0},{16,12},{20,8},{24,20},{28,16},{1,29},{... | collective-permute-start | bytes 798728 | tf_op jit(solution)/shard_map/ppermute | solution.py:328
  157.3 33.9 %copy-start.22 = (bf16[80,1664]{1,0:T(8,128)(2,1)}, bf16[80,1664]{1,0:T(8,128)(2,1)S(1)}, u32[]{:S(2)}) copy-start(bf16[80,1664]{1,0:T(8,128)(2,1)S(1)} %collective-permute-done.15.refs_4_) | copy-start | bytes 798724
  157.3 42.2 %collective-permute-start.21 = (bf16[320,1536]{1,0:T(8,128)(2,1)S(1)}, bf16[320,1536]{1,0:T(8,128)(2,1)S(1)}, u32[]{:S(2)}, u32[]{:S(2)}) collective-permute-start(bf16[320,1536]{1,0:T(8,128)(2,1)S(1)} %copy-done.12), channel_id=1, source_target_pairs={{0,2},{1,3},{2,0},{3,1},{4,6},{5,7},{6,4},{7,5},{8,10},{9,11},{10,... | collective-permute-start | bytes 2949128 | tf_op jit(solution)/shard_map/ppermute | solution.py:379
  164.6 14.0 %copy-start.23 = (bf16[80,1664]{1,0:T(8,128)(2,1)}, bf16[80,1664]{1,0:T(8,128)(2,1)S(1)}, u32[]{:S(2)}) copy-start(bf16[80,1664]{1,0:T(8,128)(2,1)S(1)} %collective-permute-done.16.refs_5_) | copy-start | bytes 798724
  164.6 14.0 %collective-permute-start.17 = (bf16[80,1664]{1,0:T(8,128)(2,1)S(1)}, bf16[80,1664]{1,0:T(8,128)(2,1)S(1)}, u32[]{:S(2)}, u32[]{:S(2)}) collective-permute-start(bf16[80,1664]{1,0:T(8,128)(2,1)S(1)} %get-tuple-element.54), channel_id=1, source_target_pairs={{0,20},{4,16},{8,28},{12,24},{16,4},{20,0},{24,12},{28,8},{1,21},{... | collective-permute-start | bytes 798728 | tf_op jit(solution)/shard_map/ppermute | solution.py:328
  178.7 11.0 %collective-permute-start.18 = (bf16[80,1664]{1,0:T(8,128)(2,1)S(1)}, bf16[80,1664]{1,0:T(8,128)(2,1)S(1)}, u32[]{:S(2)}, u32[]{:S(2)}) collective-permute-start(bf16[80,1664]{1,0:T(8,128)(2,1)S(1)} %get-tuple-element.53), channel_id=1, source_target_pairs={{0,12},{4,8},{8,20},{12,16},{16,28},{20,24},{24,4},{28,0},{1,13},{... | collective-permute-start | bytes 798728 | tf_op jit(solution)/shard_map/ppermute | solution.py:328
  189.7 26.9 %collective-permute-start.24 = (bf16[320,1664]{1,0:T(8,128)(2,1)S(1)}, bf16[320,1664]{1,0:T(8,128)(2,1)S(1)}, u32[]{:S(2)}, u32[]{:S(2)}) collective-permute-start(bf16[320,1664]{1,0:T(8,128)(2,1)S(1)} %collective-permute-done.23.refs_0_), channel_id=1, source_target_pairs={{0,1},{1,0},{2,3},{3,2},{4,5},{5,4},{6,7},{7,6},{8,9},{9,8},{10,11... | collective-permute-start | bytes 3194888 | tf_op jit(solution)/shard_map/ppermute | solution.py:379
  190.7 25.9 %collective-permute-start.26 = (bf16[320,1536]{1,0:T(8,128)(2,1)S(1)}, bf16[320,1536]{1,0:T(8,128)(2,1)}, u32[]{:S(2)}, u32[]{:S(2)}) collective-permute-start(bf16[320,1536]{1,0:T(8,128)(2,1)S(1)} %collective-permute-done.25.refs_2_), channel_id=1, source_target_pairs={{0,1},{1,0},{2,3},{3,2},{4,5},{5,4},{6,7},{7,6},{8,9},{9,8},{10,11... | collective-permute-start | bytes 2949128 | tf_op jit(solution)/shard_map/ppermute | solution.py:379
  199.5 17.1 %copy-start.13 = (bf16[320,1536]{1,0:T(8,128)(2,1)}, bf16[320,1536]{1,0:T(8,128)(2,1)S(1)}, u32[]{:S(2)}) copy-start(bf16[320,1536]{1,0:T(8,128)(2,1)S(1)} %collective-permute-done.21.refs_2_) | copy-start | bytes 2949124
  199.5 29.0 %collective-permute-start.22 = (bf16[320,1536]{1,0:T(8,128)(2,1)S(1)}, bf16[320,1536]{1,0:T(8,128)(2,1)S(1)}, u32[]{:S(2)}, u32[]{:S(2)}) collective-permute-start(bf16[320,1536]{1,0:T(8,128)(2,1)S(1)} %collective-permute-done.21.refs_2_), channel_id=1, source_target_pairs={{0,1},{1,0},{2,3},{3,2},{4,5},{5,4},{6,7},{7,6},{8,9},{9,8},{10,11... | collective-permute-start | bytes 2949128 | tf_op jit(solution)/shard_map/ppermute | solution.py:379
  199.5 17.1 %copy-start.7 = (bf16[320,1664]{1,0:T(8,128)(2,1)}, bf16[320,1664]{1,0:T(8,128)(2,1)S(1)}, u32[]{:S(2)}) copy-start(bf16[320,1664]{1,0:T(8,128)(2,1)S(1)} %collective-permute-done.19.refs_0_) | copy-start | bytes 3194884
  199.5 29.0 %collective-permute-start.20 = (bf16[320,1664]{1,0:T(8,128)(2,1)S(1)}, bf16[320,1664]{1,0:T(8,128)(2,1)S(1)}, u32[]{:S(2)}, u32[]{:S(2)}) collective-permute-start(bf16[320,1664]{1,0:T(8,128)(2,1)S(1)} %collective-permute-done.19.refs_0_), channel_id=1, source_target_pairs={{0,1},{1,0},{2,3},{3,2},{4,5},{5,4},{6,7},{7,6},{8,9},{9,8},{10,11... | collective-permute-start | bytes 3194888 | tf_op jit(solution)/shard_map/ppermute | solution.py:379
  (12 other events, 13.3 us)
where the time goes:
time: 241 us; the launch traced here: 240 us
  Pallas kernels  96.2 us (40%)
  waiting for transfers between devices  94.7 us (39%)
  starting transfers between devices  37.5 us (16%)
  local copies, waits for them, and re-layouts  9.91 us (4%)
    ppermute x19, waiting for transfers between devices, move(): return lax.ppermute(rows, 'ep', pairs)  90.6 us
    pallas_call x3, Pallas kernels, weight_grads(): pl.pallas_call(functools.partial(weight_kernel, blocks=count, rows=rows /...  37.8 us
    ppermute x19, starting transfers between devices, move(): return lax.ppermute(rows, 'ep', pairs)  26.5 us
    pallas_call x2, Pallas kernels, q_part(): pl.pallas_call(q_kernel, grid_spec=pltpu.PrefetchScalarGridSpec(num_scala...  24.7 us
    pallas_call x2, Pallas kernels, x_part(): pl.pallas_call(x_kernel, grid_spec=pltpu.PrefetchScalarGridSpec(num_scala...  16.8 us
    ppermute x12, starting transfers between devices, swap(): return lax.ppermute(rows, 'dp', [(d, d ^ step) for d in range(dp_size)])  11 us
    unnamed x58, local copies, waits for them, and re-layouts  6.45 us
    pallas_call x1, Pallas kernels, x_slots(): pl.pallas_call(functools.partial(x_slots_kernel, outer=outer, inner=inner...  5.98 us
  transfers between devices with their start and end apart: 31, of which 12 were waited for; matrix products, arithmetic and copies ran while one was open for 2% of the time, Pallas kernels for 33%

commit v1 on v0

--- a/solution.py
+++ b/solution.py
@@ -1,4 +1,5 @@
 import functools
+import math
 
 import jax
 import jax.numpy as jnp
@@ -156,34 +157,31 @@
     return scale, scale * lane_sum(values, 0, 2)
 
 
-def x_kernel(rank_ref, x_ref, gate_ref, up_ref, gated_ref, slope_ref, act_ref):
-    del rank_ref
-    width = gate_ref.shape[1]
+def expert_kernel(x_ref, q_ref, gate_ref, up_ref, down_ref, gate_delta_ref, up_delta_ref,
+                  act_ref, *refs):
+    outs, (sum_ref, prob_ref) = refs[:-2], refs[-2:]
+    step = pl.program_id(0)
+    width = q_ref.shape[1]
     x = x_ref[:, :width]
+    scale, weight = slot_facts(x_ref[:, width:])
     gate_pre = contract_last(x, gate_ref[...])
     up_pre = contract_last(x, up_ref[...])
+    back_proj = contract_last(q_ref[...], down_ref[...])
     squash = jax.nn.sigmoid(sharpness * gate_pre)
     gated = gate_pre * squash
     more = up_pre + 1.0
-    gated_ref[0] = gated.astype(jnp.bfloat16)
-    slope_ref[0] = (more * (squash + sharpness * gated * (1.0 - squash))).astype(jnp.bfloat16)
-    act_ref[0] = (more * gated).astype(jnp.bfloat16)
-
-
-def q_kernel(rank_ref, q_ref, facts_ref, gate_ref, up_ref, down_ref, gated_ref, slope_ref, act_ref,
-             out_ref, sum_ref, prob_ref):
-    del rank_ref
-    step = pl.program_id(0)
-    width = q_ref.shape[1]
-    scale, weight = slot_facts(facts_ref[...])
-    back_proj = contract_last(q_ref[...], down_ref[...])
+    activated = more * gated
     delta = weight * back_proj
-    up_delta = (delta * gated_ref[0].astype(jnp.float32)).astype(jnp.bfloat16)
-    gate_delta = (delta * slope_ref[0].astype(jnp.float32)).astype(jnp.bfloat16)
+    up_delta = (delta * gated).astype(jnp.bfloat16)
+    slope = more * (squash + sharpness * gated * (1.0 - squash))
+    gate_delta = (delta * slope).astype(jnp.bfloat16)
+    gate_delta_ref[...] = gate_delta
+    up_delta_ref[...] = up_delta
+    act_ref[...] = (activated * weight).astype(jnp.bfloat16)
     share = jnp.dot(gate_delta, gate_ref[...], preferred_element_type=jnp.float32) + jnp.dot(
         up_delta, up_ref[...], preferred_element_type=jnp.float32
     )
-    term = jnp.sum(act_ref[0].astype(jnp.float32) * back_proj, axis=1, keepdims=True)
+    term = jnp.sum(activated * back_proj, axis=1, keepdims=True)
 
     @pl.when(step == 0)
     def _():
@@ -197,22 +195,25 @@
 
     @pl.when(step == pl.num_programs(0) - 1)
     def _():
-        out_ref[:, :width] = sum_ref[...].astype(jnp.bfloat16)
-        high, low = high_low(scale * prob_ref[...])
-        lane = iota((out_ref.shape[0], lanes), 1)
-        out_ref[:, width:] = jnp.where(
-            lane == 0, high.astype(jnp.float32), jnp.where(lane == 1, low.astype(jnp.float32), 0.0)
-        ).astype(jnp.bfloat16)
-
-
-def weight_kernel(rank_ref, *refs, blocks, rows, with_start):
+        high, low = (h.astype(jnp.float32) for h in high_low(scale * prob_ref[...]))
+        lane = iota((sum_ref.shape[0], lanes), 1)
+        facts = jnp.where(lane == 0, high, jnp.where(lane == 1, low, 0.0))
+        rows = outs[0].shape[0]
+        for i, out in enumerate(outs):
+            part = slice(i * rows, (i + 1) * rows)
+            out[:, :width] = sum_ref[part, :].astype(jnp.bfloat16)
+            out[:, width:] = facts[part].astype(jnp.bfloat16)
+
+
+def weight_kernel(rank_ref, *refs, blocks, ready, rows, with_start):
     x_hbm, refs = refs[:blocks], refs[blocks:]
     q_hbm, refs = refs[:blocks], refs[blocks:]
+    delta_hbm, refs = refs[: 3 * ready], refs[3 * ready :]
     weights_hbm, refs = refs[:3], refs[3:]
     starts, refs = (refs[:3], refs[3:]) if with_start else ((), refs)
     outs, refs = refs[:3], refs[3:]
-    x, q, refs = refs[0], refs[1], refs[2:]
-    weights, refs = refs[:3], refs[3:]
+    x, q, gate_up, down, refs = *refs[:4], refs[4:]
+    parts, refs = refs[:3], refs[3:]
     held = refs[:3] if with_start else ()
     sems = refs[-1]
     copies = []
@@ -223,35 +224,41 @@
         copies.append(copy)
         return copy
 
-    quarter = weights[0].shape[0]
+    quarter = down.shape[0]
     mine = pl.ds(rank_ref[0] * quarter, quarter)
-    first = [fetch(w.at[mine, :], v) for w, v in zip(weights_hbm, weights)]
-    first += [fetch(x_hbm[b], x.at[pl.ds(b * rows, rows)]) for b in range(blocks)]
-    second = [fetch(q_hbm[b], q.at[pl.ds(b * rows, rows)]) for b in range(blocks)]
-    third = [fetch(s, h) for s, h in zip(starts, held)]
+    known = ready * rows
+    first = [fetch(weights_hbm[0].at[mine, :], gate_up.at[pl.ds(0, quarter)])]
+    first += [fetch(weights_hbm[1].at[mine, :], gate_up.at[pl.ds(quarter, quarter)])]
+    first += [fetch(x_hbm[b], x.at[pl.ds(b * rows, rows)]) for b in range(ready, blocks)]
+    second = [fetch(weights_hbm[2].at[mine, :], down)]
+    second += [fetch(q_hbm[b], q.at[pl.ds(b * rows, rows)]) for b in range(ready, blocks)]
+    third = []
+    for b in range(ready):
+        part = pl.ds(b * rows, rows)
+        third += [fetch(x_hbm[b], x.at[part]), fetch(q_hbm[b], q.at[part])]
+        for i in range(3):
+            third += [fetch(delta_hbm[3 * b + i].at[:, mine], parts[i].at[part, :])]
+    third += [fetch(s, h) for s, h in zip(starts, held)]
     for copy in first:
         copy.wait()
     width = q.shape[1]
-    gate_pre = contract_last(x[:, :width], weights[0][...])
-    up_pre = contract_last(x[:, :width], weights[1][...])
+    pre = contract_last(x[known:, :width], gate_up[...])
     for copy in second:
         copy.wait()
-    back_proj = contract_last(q[...], weights[2][...])
-    _, weight = slot_facts(x[:, width:])
+    back_proj = contract_last(q[known:], down[...])
+    _, weight = slot_facts(x[known:, width:])
+    gate_pre, more = pre[:, :quarter], pre[:, quarter:] + 1.0
     squash = jax.nn.sigmoid(sharpness * gate_pre)
     gated = gate_pre * squash
-    more = up_pre + 1.0
     delta = weight * back_proj
-    up_delta = (delta * gated).astype(jnp.bfloat16)
     slope = more * (squash + sharpness * gated * (1.0 - squash))
-    gate_delta = (delta * slope).astype(jnp.bfloat16)
-    act_scaled = (more * gated * weight).astype(jnp.bfloat16)
+    parts[0][known:, :] = (delta * slope).astype(jnp.bfloat16)
+    parts[1][known:, :] = (delta * gated).astype(jnp.bfloat16)
+    parts[2][known:, :] = (more * gated * weight).astype(jnp.bfloat16)
     for copy in third:
         copy.wait()
-    for i, (left, right) in enumerate(
-        ((gate_delta, x[:, :width]), (up_delta, x[:, :width]), (act_scaled, q[...]))
-    ):
-        total = contract_first(left, right)
+    for i, right in enumerate((x[:, :width], x[:, :width], q[...])):
+        total = contract_first(parts[i][...], right)
         if with_start:
             total = total + held[i][...]
         outs[i][...] = total.astype(outs[i].dtype)
@@ -378,81 +385,66 @@
     def swap(rows, step):
         return lax.ppermute(rows, "dp", [(d, d ^ step) for d in range(dp_size)])
 
-    def x_part(rows, tiles):
-        count = rows.shape[0]
-        turn = lambda j, r: ((r[0] + j) % dp_size, 0)
-        out = pl.BlockSpec((1, count, quarter), lambda j, r: (j, 0, 0))
-        return pl.pallas_call(
-            x_kernel,
-            grid_spec=pltpu.PrefetchScalarGridSpec(
-                num_scalar_prefetch=1,
-                grid=(tiles,),
-                in_specs=[
-                    pl.BlockSpec((count, wide), lambda j, r: (0, 0)),
-                    pl.BlockSpec((quarter, model_width), turn),
-                    pl.BlockSpec((quarter, model_width), turn),
-                ],
-                out_specs=(out,) * 3,
-            ),
-            out_shape=(shape((tiles, count, quarter), bf16),) * 3,
+    def expert_part(rows_x, rows_q):
+        count = rows_q.shape[0]
+        tiles = next(n for n in (3, 4, 2, 1) if hidden % (n * lanes) == 0)
+        size = hidden // tiles
+        weights = pl.BlockSpec((size, model_width), lambda j: (j, 0))
+        units = pl.BlockSpec((count, size), lambda j: (0, j))
+        pieces = count // capacity
+        results = pl.pallas_call(
+            expert_kernel,
+            grid=(tiles,),
+            in_specs=[
+                pl.BlockSpec((count, wide), lambda j: (0, 0)),
+                pl.BlockSpec((count, model_width), lambda j: (0, 0)),
+                weights,
+                weights,
+                weights,
+            ],
+            out_specs=[units] * 3 + [pl.BlockSpec((capacity, wide), lambda j: (0, 0))] * pieces,
+            scratch_shapes=[
+                pltpu.VMEM((count, model_width), f32),
+                pltpu.VMEM((count, 1), f32),
+            ],
+            out_shape=[shape((count, hidden), bf16)] * 3
+            + [shape((capacity, wide), bf16)] * pieces,
             compiler_params=params(),
             cost_estimate=pl.CostEstimate(
-                flops=4 * count * model_width * quarter * tiles,
-                bytes_accessed=2 * count * wide + 4 * tiles * quarter * model_width,
-                transcendentals=tiles * count * quarter,
+                flops=10 * count * model_width * hidden,
+                bytes_accessed=6 * hidden * model_width,
+                transcendentals=count * hidden,
             ),
-            name="x_part",
-        )(rank, rows, w_gate, w_up)
-
-    def q_part(rows_q, rows_x, parts):
-        count = rows_q.shape[0]
-        turn = lambda j, r: ((r[0] + j) % dp_size, 0)
-        tile = pl.BlockSpec((1, count, quarter), lambda j, r: (j, 0, 0))
-        return pl.pallas_call(
-            q_kernel,
-            grid_spec=pltpu.PrefetchScalarGridSpec(
-                num_scalar_prefetch=1,
-                grid=(dp_size,),
-                in_specs=[
-                    pl.BlockSpec((count, model_width), lambda j, r: (0, 0)),
-                    pl.BlockSpec((count, lanes), lambda j, r: (0, model_width // lanes)),
-                    pl.BlockSpec((quarter, model_width), turn),
-                    pl.BlockSpec((quarter, model_width), turn),
-                    pl.BlockSpec((quarter, model_width), turn),
-                    tile,
-                    tile,
-                    tile,
-                ],
-                out_specs=pl.BlockSpec((count, wide), lambda j, r: (0, 0)),
-                scratch_shapes=[
-                    pltpu.VMEM((count, model_width), f32),
-                    pltpu.VMEM((count, 1), f32),
-                ],
-            ),
-            out_shape=shape((count, wide), bf16),
-            compiler_params=params(),
-            cost_estimate=pl.CostEstimate(
-                flops=6 * count * model_width * hidden,
-                bytes_accessed=6 * hidden * model_width,
-                transcendentals=0,
-            ),
-            name="q_part",
-        )(rank, rows_q, rows_x, w_gate, w_up, w_down, *parts)
-
-    def weight_grads(blocks_x, blocks_q, start, out_type):
+            name="expert_part",
+        )(rows_x, rows_q, w_gate, w_up, w_down)
+        return results[:3], results[3:]
+
+    def weight_grads(blocks_x, blocks_q, deltas, start, out_type):
         counts = [b.shape[0] for b in blocks_x]
         if len(set(counts)) > 1:
-            blocks_x, blocks_q = ([jnp.concatenate(b, axis=0)] for b in (blocks_x, blocks_q))
-        count, rows = len(blocks_x), sum(counts)
-        operands = [*blocks_x, *blocks_q, w_gate, w_up, w_down, *(start or ())]
+            size = math.gcd(*counts)
+            cut = lambda bs: [b[i : i + size] for b in bs for i in range(0, b.shape[0], size)]
+            blocks_x, blocks_q = cut(blocks_x), cut(blocks_q)
+            if deltas:
+                columns = [cut(c) for c in zip(*deltas)]
+                deltas = list(zip(*columns))
+        count, rows, ready = len(blocks_x), sum(counts), len(deltas)
+        operands = [*blocks_x, *blocks_q, *sum(map(list, deltas), [])]
+        operands += [w_gate, w_up, w_down, *(start or ())]
         scratch = [pltpu.VMEM((rows, wide), bf16), pltpu.VMEM((rows, model_width), bf16)]
-        scratch += [pltpu.VMEM((quarter, model_width), bf16)] * 3
+        scratch += [pltpu.VMEM((2 * quarter, model_width), bf16)]
+        scratch += [pltpu.VMEM((quarter, model_width), bf16)]
+        scratch += [pltpu.VMEM((rows, quarter), bf16)] * 3
         if start:
             scratch += [pltpu.VMEM((quarter, model_width), f32)] * 3
         scratch += [pltpu.SemaphoreType.DMA((len(operands),))]
         return pl.pallas_call(
             functools.partial(
-                weight_kernel, blocks=count, rows=rows // count, with_start=start is not None
+                weight_kernel,
+                blocks=count,
+                ready=ready,
+                rows=rows // count,
+                with_start=start is not None,
             ),
             out_shape=(shape((quarter, model_width), out_type),) * 3,
             in_specs=[smem] + [hbm] * len(operands),
@@ -493,22 +485,24 @@
     near_ox, far_ox = replicas(other_x)
     near_oq, far_oq = replicas(other_q)
 
-    same_parts = x_part(same_x, dp_size)
-    same_back = q_part(same_q, same_x, same_parts)
-    other_parts = x_part(other_x, dp_size)
-    other_back = q_part(other_q, other_x, other_parts)
+    same_deltas, same_back = expert_part(same_x, same_q)
+    other_deltas, other_back = expert_part(other_x, other_q)
     backs = []
-    for d in range(inner):
-        source = same_back if d == 0 else other_back[(d - 1) * block : d * block]
-        for s in range(outer):
-            rows = source[s * capacity : (s + 1) * capacity]
-            if d or s:
-                home = lambda zz, i: ((zz - s) % outer, (i - d) % inner)
-                rows = move(rows, home)
-            backs.append(rows)
-    sums = weight_grads(near_sx + near_ox, near_sq + near_oq, None, f32)
-    sums = weight_grads(far_sx, far_sq, sums, f32)
-    shares = weight_grads(far_ox, far_oq, sums, bf16)
+    for i, rows in enumerate([*same_back, *other_back]):
+        d, s = i // outer, i % outer
+        if i:
+            home = lambda zz, ii: ((zz - s) % outer, (ii - d) % inner)
+            rows = move(rows, home)
+        backs.append(rows)
+    sums = weight_grads(
+        [near_sx[0], near_ox[0], *near_sx[1:], *near_ox[1:]],
+        [near_sq[0], near_oq[0], *near_sq[1:], *near_oq[1:]],
+        [same_deltas, other_deltas],
+        None,
+        f32,
+    )
+    sums = weight_grads(far_sx, far_sq, [], sums, f32)
+    shares = weight_grads(far_ox, far_oq, [], sums, bf16)
     input_grad, prob_grad = pl.pallas_call(
         functools.partial(combine_kernel, routes=routes, outer=outer, inner=inner),
         grid=(1,),

time: 241 us -> 233 us (0.967)
  Pallas kernels: 96.2 us -> 80.5 us
  waiting for transfers between devices: 94.7 us -> 108 us
  local copies, waits for them, and re-layouts: 9.91 us -> 4.82 us
    pallas_call x7 -> x5, Pallas kernels: 79.4 us -> 63.7 us  [the longest x3 35 us: weight_grads(): pl.pallas_call(functools.partial(weight_kernel, blocks=count, ready=ready...]
    ppermute x12, waiting for transfers between devices: 4.06 us -> 18.6 us  [swap(): return lax.ppermute(rows, 'dp', [(d, d ^ step) for d in range(dp_size)])]
    ppermute x12, starting transfers between devices: 11 us -> 5.06 us  [swap(): return lax.ppermute(rows, 'dp', [(d, d ^ step) for d in range(dp_size)])]
    ppermute x19, starting transfers between devices: 26.5 us -> 32.2 us  [move(): return lax.ppermute(rows, 'ep', pairs)]
    slice x2 -> x0, local copies, waits for them, and re-layouts: 3.46 us -> none  [on_device(): rows = source[s * capacity:(s + 1) * capacity]]
    unnamed x58 -> x52, local copies, waits for them, and re-layouts: 6.45 us -> 4.82 us
  transfers between devices with their start and end apart: 31 -> 31, of which waited for: 12 -> 13; matrix products, arithmetic and copies ran while one was open for 2% -> 0% of each run, Pallas kernels for 33% -> 27%
where the time goes in v1:
time: 233 us; the launch traced here: 232 us
  waiting for transfers between devices  108 us (46%)
  Pallas kernels  80.5 us (35%)
  starting transfers between devices  37.2 us (16%)
  local copies, waits for them, and re-layouts  4.82 us (2%)
    ppermute x19, waiting for transfers between devices, move(): return lax.ppermute(rows, 'ep', pairs)  89.7 us
    pallas_call x3, Pallas kernels, weight_grads(): pl.pallas_call(functools.partial(weight_kernel, blocks=count, ready=ready...  35 us
    ppermute x19, starting transfers between devices, move(): return lax.ppermute(rows, 'ep', pairs)  32.2 us
    pallas_call x2, Pallas kernels, expert_part(): pl.pallas_call(expert_kernel, grid=(tiles,), in_specs=[pl.BlockSpec((coun...  28.7 us
    ppermute x12, waiting for transfers between devices, swap(): return lax.ppermute(rows, 'dp', [(d, d ^ step) for d in range(dp_size)])  18.6 us
    pallas_call x1, Pallas kernels, x_slots(): pl.pallas_call(functools.partial(x_slots_kernel, outer=outer, inner=inner...  5.95 us
    ppermute x12, starting transfers between devices, swap(): return lax.ppermute(rows, 'dp', [(d, d ^ step) for d in range(dp_size)])  5.06 us
    unnamed x52, local copies, waits for them, and re-layouts  4.82 us
  transfers between devices with their start and end apart: 31, of which 13 were waited for; matrix products, arithmetic and copies ran while one was open for 0% of the time, Pallas kernels for 27%

profile of v1, /device:TPU:0, one launch (start us, length us, event | category | flops | bytes accessed | tf_op | source)
XLA Modules:
  0.0 232.1 jit_solution(12318288552727292414)
XLA Ops:
  0.6 2.6 %prep.1 = (bf16[128,1664]{1,0:T(8,128)(2,1)}, bf16[128,1536]{1,0:T(8,128)(2,1)}) custom-call(s32[8]{0:T(128)} %cap_ref.1, s32[4,128]{1,0:T(4,128)} %bitcast.26, s32[1,128]{1,0:T(1,128)} %order_ref.1, f32[4,128]{1,0:T(4,128)} %bitcast.27, f32[128,1536]{1,0:T(8,128)} %grad_ref.1, bf16[128,1536]{1,0:T(8,128)(2,1)} %tok_ref.1), custom_call_target="tpu_custom_call" | custom-call | tf_op jit(solution)/shard_map/prep/pallas_call | solution.py:319
  3.2 5.0 %collective-permute-start = (bf16[128,1664]{1,0:T(8,128)(2,1)}, bf16[128,1664]{1,0:T(8,128)(2,1)S(1)}, u32[]{:S(2)}, u32[]{:S(2)}) collective-permute-start(bf16[128,1664]{1,0:T(8,128)(2,1)} %get-tuple-element.37.refs_0_.facts_ref), channel_id=1, source_target_pairs={{0,8},{4,12},{8,16},{12,20},{16,24},{20,28},{1,9},{5,13},{9,17},{1... | collective-permute-start | bytes 1277960 | tf_op jit(solution)/shard_map/ppermute | solution.py:335
  8.2 1.3 collective-permute-start.1
  9.5 4.6 %collective-permute-start.5 = (bf16[128,1536]{1,0:T(8,128)(2,1)}, bf16[128,1536]{1,0:T(8,128)(2,1)S(1)}, u32[]{:S(2)}, u32[]{:S(2)}) collective-permute-start(bf16[128,1536]{1,0:T(8,128)(2,1)} %get-tuple-element.40.refs_0_), channel_id=1, source_target_pairs={{0,8},{4,12},{8,16},{12,20},{16,24},{20,28},{1,9},{5,13},{9,17},{1... | collective-permute-start | bytes 1179656 | tf_op jit(solution)/shard_map/ppermute | solution.py:335
  14.0 1.3 collective-permute-start.6
  15.4 3.3 %collective-permute-done.refs_1_ = bf16[128,1664]{1,0:T(8,128)(2,1)S(1)} collective-permute-done((bf16[128,1664]{1,0:T(8,128)(2,1)}, bf16[128,1664]{1,0:T(8,128)(2,1)S(1)}, u32[]{:S(2)}, u32[]{:S(2)}) %collective-permute-start) | collective-permute-done | bytes 426016 | tf_op jit(solution)/shard_map/ppermute | solution.py:335
  18.6 4.3 %collective-permute-done.1.refs_2_ = bf16[128,1664]{1,0:T(8,128)(2,1)S(1)} collective-permute-done((bf16[128,1664]{1,0:T(8,128)(2,1)}, bf16[128,1664]{1,0:T(8,128)(2,1)S(1)}, u32[]{:S(2)}, u32[]{:S(2)}) %collective-permute-start.1) | collective-permute-done | bytes 426016 | tf_op jit(solution)/shard_map/ppermute | solution.py:335
  23.0 1.3 collective-permute-start.4
  24.3 1.3 collective-permute-start.2
  25.6 0.7 collective-permute-start.3
  26.3 13.1 %collective-permute-done.6.refs_2_ = bf16[128,1536]{1,0:T(8,128)(2,1)S(1)} collective-permute-done((bf16[128,1536]{1,0:T(8,128)(2,1)}, bf16[128,1536]{1,0:T(8,128)(2,1)S(1)}, u32[]{:S(2)}, u32[]{:S(2)}) %collective-permute-start.6) | collective-permute-done | bytes 393248 | tf_op jit(solution)/shard_map/ppermute | solution.py:335
  39.5 1.3 collective-permute-start.9
  40.8 1.3 collective-permute-start.7
  42.2 0.7 collective-permute-start.8
  42.9 14.1 %collective-permute-done.2.refs_3_ = bf16[128,1664]{1,0:T(8,128)(2,1)S(1)} collective-permute-done((bf16[128,1664]{1,0:T(8,128)(2,1)S(1)}, bf16[128,1664]{1,0:T(8,128)(2,1)S(1)}, u32[]{:S(2)}, u32[]{:S(2)}) %collective-permute-start.2) | collective-permute-done | bytes 426016 | tf_op jit(solution)/shard_map/ppermute | solution.py:335
  57.0 0.7 copy-done.10
  57.9 6.0 %x_slots.1 = (bf16[320,1664]{1,0:T(8,128)(2,1)}, bf16[320,1664]{1,0:T(8,128)(2,1)}, bf16[512,640]{1,0:T(8,128)(2,1)}) custom-call(s32[1]{0:T(128)} %bitcast.place_ref, bf16[128,1664]{1,0:T(8,128)(2,1)} %get-tuple-element.37.refs_0_.facts_ref, bf16[128,1664]{1,0:T(8,128)(2,1)} %copy-done, bf16[128,1664]{1,0:T(8,128)(2,1)} %copy-done.1, ...), custom_call_target="tpu_custom_call" | custom-call | tf_op jit(solution)/shard_map/x_slots/pallas_call | solution.py:358
  63.9 1.2 collective-permute-done.7.refs_3_
  65.1 0.7 copy-done.13
  66.0 4.0 %q_slots.1 = (bf16[320,1536]{1,0:T(8,128)(2,1)}, bf16[320,1536]{1,0:T(8,128)(2,1)}) custom-call(s32[1]{0:T(128)} %bitcast.place_ref, bf16[512,640]{1,0:T(8,128)(2,1)} %get-tuple-element.39.table_ref, bf16[128,1536]{1,0:T(8,128)(2,1)} %get-tuple-element.40.refs_0_, bf16[128,1536]{1,0:T(8,128)(2,1)} %copy-done.2, bf16[128,1536]{1,0:T(8,128)(2,1)} %copy-done.3, ...), custom_call_target="tpu_custom_call" | custom-call | tf_op jit(solution)/shard_map/q_slots/pallas_call | solution.py:371
  70.0 1.5 collective-permute-start.14
  71.5 0.5 collective-permute-start.13
  72.0 14.4 %expert_part.2 = (bf16[320,1536]{1,0:T(8,128)(2,1)}, bf16[320,1536]{1,0:T(8,128)(2,1)}, bf16[320,1536]{1,0:T(8,128)(2,1)}, bf16[80,1664]{1,0:T(8,128)(2,1)}, bf1...) custom-call(bf16[320,1664]{1,0:T(8,128)(2,1)} %get-tuple-element.38.x_ref.refs_0_, ...), custom_call_target="tpu_custom_call" | custom-call | flops 7549747200 | bytes 14155776 | tf_op jit(solution)/shard_map/expert_part/pallas_call | solution.py:395
  86.8 2.9 %collective-permute-start.11 = (bf16[80,1664]{1,0:T(8,128)(2,1)}, bf16[80,1664]{1,0:T(8,128)(2,1)}, u32[]{:S(2)}, u32[]{:S(2)}) collective-permute-start(bf16[80,1664]{1,0:T(8,128)(2,1)} %get-tuple-element.44), channel_id=1, source_target_pairs={{0,16},{4,20},{8,24},{12,28},{16,0},{20,4},{24,8},{28,12},{1,17},{... | collective-permute-start | bytes 798728 | tf_op jit(solution)/shard_map/ppermute | solution.py:335
  89.6 4.2 %collective-permute-done.10.refs_1_ = bf16[80,1664]{1,0:T(8,128)(2,1)S(1)} collective-permute-done((bf16[80,1664]{1,0:T(8,128)(2,1)}, bf16[80,1664]{1,0:T(8,128)(2,1)S(1)}, u32[]{:S(2)}, u32[]{:S(2)}) %collective-permute-start.10) | collective-permute-done | bytes 266272 | tf_op jit(solution)/shard_map/ppermute | solution.py:335
  93.9 11.9 %collective-permute-done.11.refs_2_ = bf16[80,1664]{1,0:T(8,128)(2,1)} collective-permute-done((bf16[80,1664]{1,0:T(8,128)(2,1)}, bf16[80,1664]{1,0:T(8,128)(2,1)}, u32[]{:S(2)}, u32[]{:S(2)}) %collective-permute-start.11) | collective-permute-done | bytes 266272 | tf_op jit(solution)/shard_map/ppermute | solution.py:335
  105.8 1.5 collective-permute-start.23
  107.3 0.5 collective-permute-start.25
  107.8 7.6 %collective-permute-done.13.x_ref.refs_1_ = bf16[320,1664]{1,0:T(8,128)(2,1)S(1)} collective-permute-done((bf16[320,1664]{1,0:T(8,128)(2,1)S(1)}, bf16[320,1664]{1,0:T(8,128)(2,1)S(1)}, u32[]{:S(2)}, u32[]{:S(2)}) %collective-permute-start.13) | collective-permute-done | bytes 1064992 | tf_op jit(solution)/shard_map/ppermute | solution.py:335
  115.4 1.6 collective-permute-start.12
  117.1 14.3 %expert_part.3 = (bf16[320,1536]{1,0:T(8,128)(2,1)}, bf16[320,1536]{1,0:T(8,128)(2,1)}, bf16[320,1536]{1,0:T(8,128)(2,1)}, bf16[80,1664]{1,0:T(8,128)(2,1)}, bf1...) custom-call(bf16[320,1664]{1,0:T(8,128)(2,1)} %copy-done.21, ...), custom_call_target="tpu_custom_call" | custom-call | flops 7549747200 | bytes 14155776 | tf_op jit(solution)/shard_map/expert_part/pallas_call | solution.py:395
  131.4 1.5 collective-permute-start.15
  132.9 17.4 %collective-permute-done.25.refs_2_ = bf16[320,1536]{1,0:T(8,128)(2,1)} collective-permute-done((bf16[320,1536]{1,0:T(8,128)(2,1)S(1)}, bf16[320,1536]{1,0:T(8,128)(2,1)}, u32[]{:S(2)}, u32[]{:S(2)}) %collective-permute-start.25) | collective-permute-done | bytes 983072 | tf_op jit(solution)/shard_map/ppermute | solution.py:386
  150.3 1.5 collective-permute-start.19
  151.8 4.0 %collective-permute-start.16 = (bf16[80,1664]{1,0:T(8,128)(2,1)}, bf16[80,1664]{1,0:T(8,128)(2,1)S(1)}, u32[]{:S(2)}, u32[]{:S(2)}) collective-permute-start(bf16[80,1664]{1,0:T(8,128)(2,1)} %get-tuple-element.49), channel_id=1, source_target_pairs={{0,28},{4,24},{8,4},{12,0},{16,12},{20,8},{24,20},{28,16},{1,29},{... | collective-permute-start | bytes 798728 | tf_op jit(solution)/shard_map/ppermute | solution.py:335
  156.3 6.1 %collective-permute-done.16.refs_5_ = bf16[80,1664]{1,0:T(8,128)(2,1)S(1)} collective-permute-done((bf16[80,1664]{1,0:T(8,128)(2,1)}, bf16[80,1664]{1,0:T(8,128)(2,1)S(1)}, u32[]{:S(2)}, u32[]{:S(2)}) %collective-permute-start.16) | collective-permute-done | bytes 266272 | tf_op jit(solution)/shard_map/ppermute | solution.py:335
  162.4 1.2 collective-permute-start.17
  163.6 14.4 %collective-permute-done.17.refs_6_ = bf16[80,1664]{1,0:T(8,128)(2,1)S(1)} collective-permute-done((bf16[80,1664]{1,0:T(8,128)(2,1)}, bf16[80,1664]{1,0:T(8,128)(2,1)S(1)}, u32[]{:S(2)}, u32[]{:S(2)}) %collective-permute-start.17) | collective-permute-done | bytes 266272 | tf_op jit(solution)/shard_map/ppermute | solution.py:335
  178.0 0.7 copy-done.19
  178.7 9.3 %collective-permute-done.18.refs_7_ = bf16[80,1664]{1,0:T(8,128)(2,1)} collective-permute-done((bf16[80,1664]{1,0:T(8,128)(2,1)}, bf16[80,1664]{1,0:T(8,128)(2,1)}, u32[]{:S(2)}, u32[]{:S(2)}) %collective-permute-start.18) | collective-permute-done | bytes 266272 | tf_op jit(solution)/shard_map/ppermute | solution.py:335
  188.0 0.5 collective-permute-start.26
  188.5 4.3 %combine.1 = (bf16[128,1536]{1,0:T(8,128)(2,1)}, f32[4,128]{1,0:T(4,128)}) custom-call(s32[1]{0:T(128)} %bitcast.place_ref, bf16[128,1664]{1,0:T(8,128)(2,1)} %get-tuple-element.37.refs_0_.facts_ref, bf16[80,1664]{1,0:T(8,128)(2,1)} %get-tuple-element.42.refs_0_, bf16[80,1664]{1,0:T(8,128)(2,1)} %copy-done.15, ...), custom_call_target="tpu_custom_call" | custom-call | tf_op jit(solution)/shard_map/combine/pallas_call | solution.py:506
  192.8 1.2 collective-permute-done.21.refs_2_
  194.5 12.8 %weight_grads.3 = (f32[384,1536]{1,0:T(8,128)}, f32[384,1536]{1,0:T(8,128)}, f32[384,1536]{1,0:T(8,128)}) custom-call(s32[1]{0:T(128)} %bitcast.7.rank_ref, bf16[320,1664]{1,0:T(8,128)(2,1)} %get-tuple-element.38.x_ref.refs_0_, bf16[320,1664]{1,0:T(8,128)(2,1)} %copy-done.21, bf16[320,1664]{1,0:T(8,128)(2,1)} %copy-done.22, ...), custom_call_target="tpu_custom_call" | custom-call | flops 9059696640 | bytes 8519680 | tf_op jit(solution)/shard_map/weight_grads/pallas_call | solution.py:441
  207.4 1.0 copy-done.6
  208.4 11.4 %weight_grads.4 = (f32[384,1536]{1,0:T(8,128)}, f32[384,1536]{1,0:T(8,128)}, f32[384,1536]{1,0:T(8,128)}) custom-call(s32[1]{0:T(128)} %bitcast.7.rank_ref, bf16[320,1664]{1,0:T(8,128)(2,1)} %copy-done.4, bf16[320,1664]{1,0:T(8,128)(2,1)} %copy-done.6, bf16[320,1536]{1,0:T(8,128)(2,1)} %collective-permute-done.25.refs_2_, ...), custom_call_target="tpu_custom_call" | custom-call | flops 4529848320 | bytes 4259840 | tf_op jit(solution)/shard_map/weight_grads/pallas_call | solution.py:441
  219.8 0.9 copy-done.8
  221.1 10.8 %weight_grads.5 = (bf16[384,1536]{1,0:T(8,128)(2,1)}, bf16[384,1536]{1,0:T(8,128)(2,1)}, bf16[384,1536]{1,0:T(8,128)(2,1)}) custom-call(s32[1]{0:T(128)} %bitcast.7.rank_ref, bf16[320,1664]{1,0:T(8,128)(2,1)} %copy-done.5, bf16[320,1664]{1,0:T(8,128)(2,1)} %copy-done.7, bf16[320,1536]{1,0:T(8,128)(2,1)} %collective-permute-done.21.refs_2_, ...), custom_call_target="tpu_custom_call" | custom-call | flops 4529848320 | bytes 4259840 | tf_op jit(solution)/shard_map/weight_grads/pallas_call | solution.py:441
  (77 shorter events, 2.2 us)
Async XLA Ops:
  3.2 15.5 %collective-permute-start = (bf16[128,1664]{1,0:T(8,128)(2,1)}, bf16[128,1664]{1,0:T(8,128)(2,1)S(1)}, u32[]{:S(2)}, u32[]{:S(2)}) collective-permute-start(bf16[128,1664]{1,0:T(8,128)(2,1)} %get-tuple-element.37.refs_0_.facts_ref), channel_id=1, source_target_pairs={{0,8},{4,12},{8,16},{12,20},{16,24},{20,28},{1,9},{5,13},{9,17},{1... | collective-permute-start | bytes 1277960 | tf_op jit(solution)/shard_map/ppermute | solution.py:335
  8.2 14.8 %collective-permute-start.1 = (bf16[128,1664]{1,0:T(8,128)(2,1)}, bf16[128,1664]{1,0:T(8,128)(2,1)S(1)}, u32[]{:S(2)}, u32[]{:S(2)}) collective-permute-start(bf16[128,1664]{1,0:T(8,128)(2,1)} %get-tuple-element.37.refs_0_.facts_ref), channel_id=1, source_target_pairs={{8,0},{12,4},{16,8},{20,12},{24,16},{28,20},{9,1},{13,5},{17,9},{2... | collective-permute-start | bytes 1277960 | tf_op jit(solution)/shard_map/ppermute | solution.py:335
  9.5 16.8 %collective-permute-start.5 = (bf16[128,1536]{1,0:T(8,128)(2,1)}, bf16[128,1536]{1,0:T(8,128)(2,1)S(1)}, u32[]{:S(2)}, u32[]{:S(2)}) collective-permute-start(bf16[128,1536]{1,0:T(8,128)(2,1)} %get-tuple-element.40.refs_0_), channel_id=1, source_target_pairs={{0,8},{4,12},{8,16},{12,20},{16,24},{20,28},{1,9},{5,13},{9,17},{1... | collective-permute-start | bytes 1179656 | tf_op jit(solution)/shard_map/ppermute | solution.py:335
  14.0 25.4 %collective-permute-start.6 = (bf16[128,1536]{1,0:T(8,128)(2,1)}, bf16[128,1536]{1,0:T(8,128)(2,1)S(1)}, u32[]{:S(2)}, u32[]{:S(2)}) collective-permute-start(bf16[128,1536]{1,0:T(8,128)(2,1)} %get-tuple-element.40.refs_0_), channel_id=1, source_target_pairs={{8,0},{12,4},{16,8},{20,12},{24,16},{28,20},{9,1},{13,5},{17,9},{2... | collective-permute-start | bytes 1179656 | tf_op jit(solution)/shard_map/ppermute | solution.py:335
  18.6 20.9 %copy-start = (bf16[128,1664]{1,0:T(8,128)(2,1)}, bf16[128,1664]{1,0:T(8,128)(2,1)S(1)}, u32[]{:S(2)}) copy-start(bf16[128,1664]{1,0:T(8,128)(2,1)S(1)} %collective-permute-done.refs_1_) | copy-start | bytes 1277956
  23.0 16.6 %copy-start.1 = (bf16[128,1664]{1,0:T(8,128)(2,1)}, bf16[128,1664]{1,0:T(8,128)(2,1)S(1)}, u32[]{:S(2)}) copy-start(bf16[128,1664]{1,0:T(8,128)(2,1)S(1)} %collective-permute-done.1.refs_2_) | copy-start | bytes 1277956
  23.0 19.1 %collective-permute-start.4 = (bf16[128,1664]{1,0:T(8,128)(2,1)S(1)}, bf16[128,1664]{1,0:T(8,128)(2,1)S(1)}, u32[]{:S(2)}, u32[]{:S(2)}) collective-permute-start(bf16[128,1664]{1,0:T(8,128)(2,1)S(1)} %broadcast_select_fusion), channel_id=1, source_target_pairs={{8,24},{12,28},{16,0},{20,4},{9,25},{13,29},{17,1},{21,5},{10,26},... | collective-permute-start | bytes 1277960 | tf_op jit(solution)/shard_map/ppermute | solution.py:335
  24.3 32.7 %collective-permute-start.2 = (bf16[128,1664]{1,0:T(8,128)(2,1)S(1)}, bf16[128,1664]{1,0:T(8,128)(2,1)S(1)}, u32[]{:S(2)}, u32[]{:S(2)}) collective-permute-start(bf16[128,1664]{1,0:T(8,128)(2,1)S(1)} %collective-permute-done.1.refs_2_), channel_id=1, source_target_pairs={{8,0},{12,4},{16,8},{20,12},{9,1},{13,5},{17,9},{21,13},{10,2},{14... | collective-permute-start | bytes 1277960 | tf_op jit(solution)/shard_map/ppermute | solution.py:335
  25.6 31.4 %collective-permute-start.3 = (bf16[128,1664]{1,0:T(8,128)(2,1)S(1)}, bf16[128,1664]{1,0:T(8,128)(2,1)S(1)}, u32[]{:S(2)}, u32[]{:S(2)}) collective-permute-start(bf16[128,1664]{1,0:T(8,128)(2,1)S(1)} %collective-permute-done.refs_1_), channel_id=1, source_target_pairs={{8,16},{12,20},{16,24},{20,28},{9,17},{13,21},{17,25},{21,29},{10,... | collective-permute-start | bytes 1277960 | tf_op jit(solution)/shard_map/ppermute | solution.py:335
  26.3 37.5 %copy-start.2 = (bf16[128,1536]{1,0:T(8,128)(2,1)}, bf16[128,1536]{1,0:T(8,128)(2,1)S(1)}, u32[]{:S(2)}) copy-start(bf16[128,1536]{1,0:T(8,128)(2,1)S(1)} %collective-permute-done.5.refs_1_) | copy-start | bytes 1179652
  39.5 24.4 %copy-start.3 = (bf16[128,1536]{1,0:T(8,128)(2,1)}, bf16[128,1536]{1,0:T(8,128)(2,1)S(1)}, u32[]{:S(2)}) copy-start(bf16[128,1536]{1,0:T(8,128)(2,1)S(1)} %collective-permute-done.6.refs_2_) | copy-start | bytes 1179652
  39.5 24.3 %collective-permute-start.9 = (bf16[128,1536]{1,0:T(8,128)(2,1)S(1)}, bf16[128,1536]{1,0:T(8,128)(2,1)S(1)}, u32[]{:S(2)}, u32[]{:S(2)}) collective-permute-start(bf16[128,1536]{1,0:T(8,128)(2,1)S(1)} %broadcast_select_fusion.1), channel_id=1, source_target_pairs={{8,24},{12,28},{16,0},{20,4},{9,25},{13,29},{17,1},{21,5},{10,26},... | collective-permute-start | bytes 1179656 | tf_op jit(solution)/shard_map/ppermute | solution.py:335
  40.8 24.2 %collective-permute-start.7 = (bf16[128,1536]{1,0:T(8,128)(2,1)S(1)}, bf16[128,1536]{1,0:T(8,128)(2,1)S(1)}, u32[]{:S(2)}, u32[]{:S(2)}) collective-permute-start(bf16[128,1536]{1,0:T(8,128)(2,1)S(1)} %collective-permute-done.6.refs_2_), channel_id=1, source_target_pairs={{8,0},{12,4},{16,8},{20,12},{9,1},{13,5},{17,9},{21,13},{10,2},{14... | collective-permute-start | bytes 1179656 | tf_op jit(solution)/shard_map/ppermute | solution.py:335
  42.1 14.8 %copy-start.9 = (bf16[128,1664]{1,0:T(8,128)(2,1)}, bf16[128,1664]{1,0:T(8,128)(2,1)S(1)}, u32[]{:S(2)}) copy-start(bf16[128,1664]{1,0:T(8,128)(2,1)S(1)} %collective-permute-done.4.refs_5_) | copy-start | bytes 1277956
  42.2 22.9 %collective-permute-start.8 = (bf16[128,1536]{1,0:T(8,128)(2,1)S(1)}, bf16[128,1536]{1,0:T(8,128)(2,1)S(1)}, u32[]{:S(2)}, u32[]{:S(2)}) collective-permute-start(bf16[128,1536]{1,0:T(8,128)(2,1)S(1)} %collective-permute-done.5.refs_1_), channel_id=1, source_target_pairs={{8,16},{12,20},{16,24},{20,28},{9,17},{13,21},{17,25},{21,29},{10,... | collective-permute-start | bytes 1179656 | tf_op jit(solution)/shard_map/ppermute | solution.py:335
  66.0 5.5 %copy-start.23 = (bf16[320,1664]{1,0:T(8,128)(2,1)S(1)}, bf16[320,1664]{1,0:T(8,128)(2,1)}, u32[]{:S(2)}) copy-start(bf16[320,1664]{1,0:T(8,128)(2,1)} %get-tuple-element.46) | copy-start | bytes 3194884
  70.0 37.3 %collective-permute-start.14 = (bf16[320,1536]{1,0:T(8,128)(2,1)}, bf16[320,1536]{1,0:T(8,128)(2,1)S(1)}, u32[]{:S(2)}, u32[]{:S(2)}) collective-permute-start(bf16[320,1536]{1,0:T(8,128)(2,1)} %get-tuple-element.47), channel_id=1, source_target_pairs={{0,4},{4,0},{8,12},{12,8},{16,20},{20,16},{24,28},{28,24},{1,5},{5... | collective-permute-start | bytes 2949128 | tf_op jit(solution)/shard_map/ppermute | solution.py:335
  71.5 43.9 %collective-permute-start.13 = (bf16[320,1664]{1,0:T(8,128)(2,1)S(1)}, bf16[320,1664]{1,0:T(8,128)(2,1)S(1)}, u32[]{:S(2)}, u32[]{:S(2)}) collective-permute-start(bf16[320,1664]{1,0:T(8,128)(2,1)S(1)} %copy-done.23), channel_id=1, source_target_pairs={{0,4},{4,0},{8,12},{12,8},{16,20},{20,16},{24,28},{28,24},{1,5},{5... | collective-permute-start | bytes 3194888 | tf_op jit(solution)/shard_map/ppermute | solution.py:335
  72.0 17.6 %copy-start.20 = (bf16[320,1664]{1,0:T(8,128)(2,1)S(1)}, bf16[320,1664]{1,0:T(8,128)(2,1)}, u32[]{:S(2)}) copy-start(bf16[320,1664]{1,0:T(8,128)(2,1)} %get-tuple-element.38.x_ref.refs_0_) | copy-start | bytes 3194884
  72.0 21.8 %copy-start.24 = (bf16[320,1536]{1,0:T(8,128)(2,1)S(1)}, bf16[320,1536]{1,0:T(8,128)(2,1)}, u32[]{:S(2)}) copy-start(bf16[320,1536]{1,0:T(8,128)(2,1)} %get-tuple-element.41.q_ref.refs_4_) | copy-start | bytes 2949124
  86.5 7.4 %collective-permute-start.10 = (bf16[80,1664]{1,0:T(8,128)(2,1)}, bf16[80,1664]{1,0:T(8,128)(2,1)S(1)}, u32[]{:S(2)}, u32[]{:S(2)}) collective-permute-start(bf16[80,1664]{1,0:T(8,128)(2,1)} %get-tuple-element.43), channel_id=1, source_target_pairs={{0,24},{4,28},{8,0},{12,4},{16,8},{20,12},{24,16},{28,20},{1,25},{... | collective-permute-start | bytes 798728 | tf_op jit(solution)/shard_map/ppermute | solution.py:335
  86.8 19.0 %collective-permute-start.11 = (bf16[80,1664]{1,0:T(8,128)(2,1)}, bf16[80,1664]{1,0:T(8,128)(2,1)}, u32[]{:S(2)}, u32[]{:S(2)}) collective-permute-start(bf16[80,1664]{1,0:T(8,128)(2,1)} %get-tuple-element.44), channel_id=1, source_target_pairs={{0,16},{4,20},{8,24},{12,28},{16,0},{20,4},{24,8},{28,12},{1,17},{... | collective-permute-start | bytes 798728 | tf_op jit(solution)/shard_map/ppermute | solution.py:335
  89.6 62.2 %collective-permute-start.27 = (bf16[320,1664]{1,0:T(8,128)(2,1)S(1)}, bf16[320,1664]{1,0:T(8,128)(2,1)S(1)}, u32[]{:S(2)}, u32[]{:S(2)}) collective-permute-start(bf16[320,1664]{1,0:T(8,128)(2,1)S(1)} %copy-done.20), channel_id=1, source_target_pairs={{0,1},{1,0},{2,3},{3,2},{4,5},{5,4},{6,7},{7,6},{8,9},{9,8},{10,11... | collective-permute-start | bytes 3194888 | tf_op jit(solution)/shard_map/ppermute | solution.py:386
  93.9 37.5 %copy-start.15 = (bf16[80,1664]{1,0:T(8,128)(2,1)}, bf16[80,1664]{1,0:T(8,128)(2,1)S(1)}, u32[]{:S(2)}) copy-start(bf16[80,1664]{1,0:T(8,128)(2,1)S(1)} %collective-permute-done.10.refs_1_) | copy-start | bytes 798724
  93.9 39.1 %collective-permute-start.29 = (bf16[320,1536]{1,0:T(8,128)(2,1)S(1)}, bf16[320,1536]{1,0:T(8,128)(2,1)}, u32[]{:S(2)}, u32[]{:S(2)}) collective-permute-start(bf16[320,1536]{1,0:T(8,128)(2,1)S(1)} %copy-done.24), channel_id=1, source_target_pairs={{0,1},{1,0},{2,3},{3,2},{4,5},{5,4},{6,7},{7,6},{8,9},{9,8},{10,11... | collective-permute-start | bytes 2949128 | tf_op jit(solution)/shard_map/ppermute | solution.py:386
  105.8 46.1 %collective-permute-start.23 = (bf16[320,1664]{1,0:T(8,128)(2,1)S(1)}, bf16[320,1664]{1,0:T(8,128)(2,1)S(1)}, u32[]{:S(2)}, u32[]{:S(2)}) collective-permute-start(bf16[320,1664]{1,0:T(8,128)(2,1)S(1)} %copy-done.20), channel_id=1, source_target_pairs={{0,2},{1,3},{2,0},{3,1},{4,6},{5,7},{6,4},{7,5},{8,10},{9,11},{10,... | collective-permute-start | bytes 3194888 | tf_op jit(solution)/shard_map/ppermute | solution.py:386
  107.3 9.8 %copy-start.25 = (bf16[320,1536]{1,0:T(8,128)(2,1)}, bf16[320,1536]{1,0:T(8,128)(2,1)S(1)}, u32[]{:S(2)}) copy-start(bf16[320,1536]{1,0:T(8,128)(2,1)S(1)} %collective-permute-done.14.q_ref.refs_5_) | copy-start | bytes 2949124
  107.3 43.0 %collective-permute-start.25 = (bf16[320,1536]{1,0:T(8,128)(2,1)S(1)}, bf16[320,1536]{1,0:T(8,128)(2,1)}, u32[]{:S(2)}, u32[]{:S(2)}) collective-permute-start(bf16[320,1536]{1,0:T(8,128)(2,1)S(1)} %copy-done.24), channel_id=1, source_target_pairs={{0,2},{1,3},{2,0},{3,1},{4,6},{5,7},{6,4},{7,5},{8,10},{9,11},{10,... | collective-permute-start | bytes 2949128 | tf_op jit(solution)/shard_map/ppermute | solution.py:386
  115.4 1.7 copy-start.21
  115.4 15.9 %collective-permute-start.12 = (bf16[80,1664]{1,0:T(8,128)(2,1)}, bf16[80,1664]{1,0:T(8,128)(2,1)S(1)}, u32[]{:S(2)}, u32[]{:S(2)}) collective-permute-start(bf16[80,1664]{1,0:T(8,128)(2,1)} %get-tuple-element.45), channel_id=1, source_target_pairs={{0,8},{4,12},{8,16},{12,20},{16,24},{20,28},{24,0},{28,4},{1,9},{5... | collective-permute-start | bytes 798728 | tf_op jit(solution)/shard_map/ppermute | solution.py:335
  131.4 1.6 copy-start.16
  131.4 24.5 %collective-permute-start.15 = (bf16[80,1664]{1,0:T(8,128)(2,1)}, bf16[80,1664]{1,0:T(8,128)(2,1)S(1)}, u32[]{:S(2)}, u32[]{:S(2)}) collective-permute-start(bf16[80,1664]{1,0:T(8,128)(2,1)} %get-tuple-element.48), channel_id=1, source_target_pairs={{0,4},{4,0},{8,12},{12,8},{16,20},{20,16},{24,28},{28,24},{1,5},{5... | collective-permute-start | bytes 798728 | tf_op jit(solution)/shard_map/ppermute | solution.py:335
  132.9 55.1 %collective-permute-start.30 = (bf16[320,1536]{1,0:T(8,128)(2,1)}, bf16[320,1536]{1,0:T(8,128)(2,1)}, u32[]{:S(2)}, u32[]{:S(2)}) collective-permute-start(bf16[320,1536]{1,0:T(8,128)(2,1)} %copy-done.25), channel_id=1, source_target_pairs={{0,1},{1,0},{2,3},{3,2},{4,5},{5,4},{6,7},{7,6},{8,9},{9,8},{10,11... | collective-permute-start | bytes 2949128 | tf_op jit(solution)/shard_map/ppermute | solution.py:386
  150.3 43.7 %collective-permute-start.19 = (bf16[320,1664]{1,0:T(8,128)(2,1)}, bf16[320,1664]{1,0:T(8,128)(2,1)S(1)}, u32[]{:S(2)}, u32[]{:S(2)}) collective-permute-start(bf16[320,1664]{1,0:T(8,128)(2,1)} %copy-done.21), channel_id=1, source_target_pairs={{0,2},{1,3},{2,0},{3,1},{4,6},{5,7},{6,4},{7,5},{8,10},{9,11},{10,... | collective-permute-start | bytes 3194888 | tf_op jit(solution)/shard_map/ppermute | solution.py:386
  151.8 36.2 %copy-start.22 = (bf16[320,1664]{1,0:T(8,128)(2,1)}, bf16[320,1664]{1,0:T(8,128)(2,1)S(1)}, u32[]{:S(2)}) copy-start(bf16[320,1664]{1,0:T(8,128)(2,1)S(1)} %collective-permute-done.27.refs_2_) | copy-start | bytes 3194884
  151.8 42.7 %collective-permute-start.28 = (bf16[320,1664]{1,0:T(8,128)(2,1)}, bf16[320,1664]{1,0:T(8,128)(2,1)}, u32[]{:S(2)}, u32[]{:S(2)}) collective-permute-start(bf16[320,1664]{1,0:T(8,128)(2,1)} %copy-done.21), channel_id=1, source_target_pairs={{0,1},{1,0},{2,3},{3,2},{4,5},{5,4},{6,7},{7,6},{8,9},{9,8},{10,11... | collective-permute-start | bytes 3194888 | tf_op jit(solution)/shard_map/ppermute | solution.py:386
  151.8 41.0 %copy-start.4 = (bf16[320,1664]{1,0:T(8,128)(2,1)}, bf16[320,1664]{1,0:T(8,128)(2,1)S(1)}, u32[]{:S(2)}) copy-start(bf16[320,1664]{1,0:T(8,128)(2,1)S(1)} %collective-permute-done.23.refs_0_) | copy-start | bytes 3194884
  151.8 10.5 %collective-permute-start.16 = (bf16[80,1664]{1,0:T(8,128)(2,1)}, bf16[80,1664]{1,0:T(8,128)(2,1)S(1)}, u32[]{:S(2)}, u32[]{:S(2)}) collective-permute-start(bf16[80,1664]{1,0:T(8,128)(2,1)} %get-tuple-element.49), channel_id=1, source_target_pairs={{0,28},{4,24},{8,4},{12,0},{16,12},{20,8},{24,20},{28,16},{1,29},{... | collective-permute-start | bytes 798728 | tf_op jit(solution)/shard_map/ppermute | solution.py:335
  155.8 32.7 %copy-start.17 = (bf16[80,1664]{1,0:T(8,128)(2,1)}, bf16[80,1664]{1,0:T(8,128)(2,1)S(1)}, u32[]{:S(2)}) copy-start(bf16[80,1664]{1,0:T(8,128)(2,1)S(1)} %collective-permute-done.15.refs_4_) | copy-start | bytes 798724
  155.8 38.2 %collective-permute-start.21 = (bf16[320,1536]{1,0:T(8,128)(2,1)}, bf16[320,1536]{1,0:T(8,128)(2,1)}, u32[]{:S(2)}, u32[]{:S(2)}) collective-permute-start(bf16[320,1536]{1,0:T(8,128)(2,1)} %copy-done.25), channel_id=1, source_target_pairs={{0,2},{1,3},{2,0},{3,1},{4,6},{5,7},{6,4},{7,5},{8,10},{9,11},{10,... | collective-permute-start | bytes 2949128 | tf_op jit(solution)/shard_map/ppermute | solution.py:386
  162.4 15.6 %copy-start.18 = (bf16[80,1664]{1,0:T(8,128)(2,1)}, bf16[80,1664]{1,0:T(8,128)(2,1)S(1)}, u32[]{:S(2)}) copy-start(bf16[80,1664]{1,0:T(8,128)(2,1)S(1)} %collective-permute-done.16.refs_5_) | copy-start | bytes 798724
  162.4 15.6 %collective-permute-start.17 = (bf16[80,1664]{1,0:T(8,128)(2,1)}, bf16[80,1664]{1,0:T(8,128)(2,1)S(1)}, u32[]{:S(2)}, u32[]{:S(2)}) collective-permute-start(bf16[80,1664]{1,0:T(8,128)(2,1)} %get-tuple-element.50), channel_id=1, source_target_pairs={{0,20},{4,16},{8,28},{12,24},{16,4},{20,0},{24,12},{28,8},{1,21},{... | collective-permute-start | bytes 798728 | tf_op jit(solution)/shard_map/ppermute | solution.py:335
  178.0 10.0 %collective-permute-start.18 = (bf16[80,1664]{1,0:T(8,128)(2,1)}, bf16[80,1664]{1,0:T(8,128)(2,1)}, u32[]{:S(2)}, u32[]{:S(2)}) collective-permute-start(bf16[80,1664]{1,0:T(8,128)(2,1)} %get-tuple-element.51), channel_id=1, source_target_pairs={{0,12},{4,8},{8,20},{12,16},{16,28},{20,24},{24,4},{28,0},{1,13},{... | collective-permute-start | bytes 798728 | tf_op jit(solution)/shard_map/ppermute | solution.py:335
  188.0 19.4 %collective-permute-start.24 = (bf16[320,1664]{1,0:T(8,128)(2,1)S(1)}, bf16[320,1664]{1,0:T(8,128)(2,1)S(1)}, u32[]{:S(2)}, u32[]{:S(2)}) collective-permute-start(bf16[320,1664]{1,0:T(8,128)(2,1)S(1)} %collective-permute-done.23.refs_0_), channel_id=1, source_target_pairs={{0,1},{1,0},{2,3},{3,2},{4,5},{5,4},{6,7},{7,6},{8,9},{9,8},{10,11... | collective-permute-start | bytes 3194888 | tf_op jit(solution)/shard_map/ppermute | solution.py:386
  188.0 19.4 %collective-permute-start.26 = (bf16[320,1536]{1,0:T(8,128)(2,1)}, bf16[320,1536]{1,0:T(8,128)(2,1)}, u32[]{:S(2)}, u32[]{:S(2)}) collective-permute-start(bf16[320,1536]{1,0:T(8,128)(2,1)} %collective-permute-done.25.refs_2_), channel_id=1, source_target_pairs={{0,1},{1,0},{2,3},{3,2},{4,5},{5,4},{6,7},{7,6},{8,9},{9,8},{10,11... | collective-permute-start | bytes 2949128 | tf_op jit(solution)/shard_map/ppermute | solution.py:386
  194.0 25.8 %collective-permute-start.22 = (bf16[320,1536]{1,0:T(8,128)(2,1)}, bf16[320,1536]{1,0:T(8,128)(2,1)S(1)}, u32[]{:S(2)}, u32[]{:S(2)}) collective-permute-start(bf16[320,1536]{1,0:T(8,128)(2,1)} %collective-permute-done.21.refs_2_), channel_id=1, source_target_pairs={{0,1},{1,0},{2,3},{3,2},{4,5},{5,4},{6,7},{7,6},{8,9},{9,8},{10,11... | collective-permute-start | bytes 2949128 | tf_op jit(solution)/shard_map/ppermute | solution.py:386
  194.0 13.4 %copy-start.5 = (bf16[320,1664]{1,0:T(8,128)(2,1)}, bf16[320,1664]{1,0:T(8,128)(2,1)S(1)}, u32[]{:S(2)}) copy-start(bf16[320,1664]{1,0:T(8,128)(2,1)S(1)} %collective-permute-done.19.refs_0_) | copy-start | bytes 3194884
  194.0 25.8 %collective-permute-start.20 = (bf16[320,1664]{1,0:T(8,128)(2,1)S(1)}, bf16[320,1664]{1,0:T(8,128)(2,1)S(1)}, u32[]{:S(2)}, u32[]{:S(2)}) collective-permute-start(bf16[320,1664]{1,0:T(8,128)(2,1)S(1)} %collective-permute-done.19.refs_0_), channel_id=1, source_target_pairs={{0,1},{1,0},{2,3},{3,2},{4,5},{5,4},{6,7},{7,6},{8,9},{9,8},{10,11... | collective-permute-start | bytes 3194888 | tf_op jit(solution)/shard_map/ppermute | solution.py:386
  (9 other events, 8.5 us)

commit v2 on v1

--- a/solution.py
+++ b/solution.py
@@ -12,8 +12,6 @@
 sharpness = 1.702
 lanes = 128
 
-params = functools.partial(pltpu.CompilerParams, vmem_limit_bytes=56 * 1024 * 1024)
-
 
 def contract_last(first_op, second_op):
     return lax.dot_general(
@@ -49,7 +47,8 @@
     ]
 
 
-def prep_kernel(cap_ref, ids_ref, order_ref, probs_ref, grad_ref, tok_ref, x_ref, q_ref, *, experts):
+def prep_kernel(cap_ref, ids_ref, order_ref, probs_ref, grad_ref, tok_ref, x_ref, q_ref, facts_ref,
+                *, experts):
     rows, width = tok_ref.shape
     routes = ids_ref.shape[0]
     lane = iota((rows, lanes), 1)
@@ -80,7 +79,9 @@
     facts = jnp.where(lane == 4 * routes, high, facts)
     facts = jnp.where(lane == 4 * routes + 1, low, facts)
     x_ref[:, :width] = tok_ref[...]
-    x_ref[:, width:] = facts.astype(jnp.bfloat16)
+    facts = facts.astype(jnp.bfloat16)
+    x_ref[:, width:] = facts
+    facts_ref[...] = facts
 
 
 def chunks_of(place_ref, refs, outer, inner):
@@ -109,7 +110,7 @@
     chunk = (iota((count, 1), 0) // (count // outer)).astype(jnp.float32)
     slot = iota((count, inner * block), 1).astype(jnp.float32)
     table = jnp.zeros((count, inner * block), jnp.float32)
-    chance = jnp.zeros((count, inner * block), jnp.float32)
+    chances = [jnp.zeros((count, 1), jnp.float32)] * inner
     for k in range(routes):
         expert = facts[:, k : k + 1]
         rank = facts[:, routes + k : routes + k + 1]
@@ -119,27 +120,22 @@
         for d in range(inner):
             mine = (expert == partner(place_ref[0], 0, d, outer, inner)) & (rank >= 0.0)
             column = jnp.where(mine, d * block + chunk * capacity + rank, column)
-        hit = (slot == column).astype(jnp.float32)
-        table = table + hit
-        chance = chance + hit * prob
+            chances[d] = jnp.where(mine, prob, chances[d])
+        table = table + (slot == column).astype(jnp.float32)
     table = table.astype(jnp.bfloat16)
     outs[-1][...] = table
-    chance_high, chance_low = high_low(chance)
     lane = iota((count, lanes), 1)
     scales = jnp.where(
         lane == 2,
         facts[:, 4 * routes : 4 * routes + 1],
         jnp.where(lane == 3, facts[:, 4 * routes + 1 : 4 * routes + 2], 0.0),
-    ).astype(jnp.bfloat16)
-    kept = (
-        contract_first(chance_high, (lane == 0).astype(jnp.bfloat16))
-        + contract_first(chance_low, (lane == 1).astype(jnp.bfloat16))
-        + contract_first(table, scales)
-    ).astype(jnp.bfloat16)
+    )
     for d in range(inner):
-        part = slice(d * block, (d + 1) * block)
-        outs[d][:, :width] = contract_first(table[:, part], rows[:, :width]).astype(jnp.bfloat16)
-        outs[d][:, width:] = kept[part]
+        part = table[:, d * block : (d + 1) * block]
+        high, low = (h.astype(jnp.float32) for h in high_low(chances[d]))
+        kept = jnp.where(lane == 0, high, jnp.where(lane == 1, low, scales)).astype(jnp.bfloat16)
+        outs[d][:, :width] = contract_first(part, rows[:, :width]).astype(jnp.bfloat16)
+        outs[d][:, width:] = contract_first(part, kept).astype(jnp.bfloat16)
 
 
 def q_slots_kernel(place_ref, table_ref, *refs, outer, inner):
@@ -157,94 +153,125 @@
     return scale, scale * lane_sum(values, 0, 2)
 
 
-def expert_kernel(x_ref, q_ref, gate_ref, up_ref, down_ref, gate_delta_ref, up_delta_ref,
-                  act_ref, *refs):
-    outs, (sum_ref, prob_ref) = refs[:-2], refs[-2:]
-    step = pl.program_id(0)
-    width = q_ref.shape[1]
-    x = x_ref[:, :width]
-    scale, weight = slot_facts(x_ref[:, width:])
-    gate_pre = contract_last(x, gate_ref[...])
-    up_pre = contract_last(x, up_ref[...])
-    back_proj = contract_last(q_ref[...], down_ref[...])
-    squash = jax.nn.sigmoid(sharpness * gate_pre)
-    gated = gate_pre * squash
-    more = up_pre + 1.0
-    activated = more * gated
-    delta = weight * back_proj
-    up_delta = (delta * gated).astype(jnp.bfloat16)
-    slope = more * (squash + sharpness * gated * (1.0 - squash))
-    gate_delta = (delta * slope).astype(jnp.bfloat16)
-    gate_delta_ref[...] = gate_delta
-    up_delta_ref[...] = up_delta
-    act_ref[...] = (activated * weight).astype(jnp.bfloat16)
-    share = jnp.dot(gate_delta, gate_ref[...], preferred_element_type=jnp.float32) + jnp.dot(
-        up_delta, up_ref[...], preferred_element_type=jnp.float32
-    )
-    term = jnp.sum(activated * back_proj, axis=1, keepdims=True)
-
-    @pl.when(step == 0)
-    def _():
-        sum_ref[...] = share
-        prob_ref[...] = term
-
-    @pl.when(step > 0)
-    def _():
+class Copies:
+    def __init__(self, sems):
+        self.sems, self.count = sems, 0
+
+    def start(self, source, target):
+        copy = pltpu.make_async_copy(source, target, self.sems.at[self.count])
+        copy.start()
+        self.count += 1
+        return copy
+
+
+def wait_all(copies):
+    for copy in copies:
+        copy.wait()
+
+
+def expert_kernel(rank_ref, x_hbm, q_hbm, *refs, tiles):
+    weights_hbm, refs = refs[:3], refs[3:]
+    owns_hbm, refs = refs[:3], refs[3:]
+    *refs, x, q, gate, up, down, every_gate, every_up, every_act, sum_ref, prob_ref, sems, own_sems = refs
+    outs_hbm, outs = refs[: len(refs) // 2], refs[len(refs) // 2 :]
+    weights, alls = (gate, up, down), (every_gate, every_up, every_act)
+    size, width = gate.shape[1:]
+    copies = Copies(own_sems)
+
+    def tile_copy(i, tile):
+        part = pl.ds(tile * size, size)
+        return pltpu.make_async_copy(
+            weights_hbm[i].at[part, :], weights[i].at[tile], sems.at[i, tile]
+        )
+
+    loads = [copies.start(x_hbm, x)]
+    tile_copy(0, 0).start()
+    tile_copy(1, 0).start()
+    loads.append(copies.start(q_hbm, q))
+    tile_copy(2, 0).start()
+    for tile in range(1, tiles):
+        for i in range(3):
+            tile_copy(i, tile).start()
+    loads[0].wait()
+    scale, weight = slot_facts(x[:, width:])
+    sum_ref[...] = jnp.zeros_like(sum_ref)
+    prob_ref[...] = jnp.zeros_like(prob_ref)
+    loads[1].wait()
+
+    def step(tile, carry):
+        units = pl.ds(pl.multiple_of(tile * size, lanes), size)
+        rows = x[:, :width]
+        tile_copy(0, tile).wait()
+        gate_pre = contract_last(rows, gate[tile])
+        tile_copy(1, tile).wait()
+        up_pre = contract_last(rows, up[tile])
+        tile_copy(2, tile).wait()
+        back_proj = contract_last(q[...], down[tile])
+        squash = jax.nn.sigmoid(sharpness * gate_pre)
+        gated = gate_pre * squash
+        more = up_pre + 1.0
+        activated = more * gated
+        delta = weight * back_proj
+        up_delta = (delta * gated).astype(jnp.bfloat16)
+        slope = more * (squash + sharpness * gated * (1.0 - squash))
+        gate_delta = (delta * slope).astype(jnp.bfloat16)
+        every_gate[:, units] = gate_delta
+        every_up[:, units] = up_delta
+        every_act[:, units] = (activated * weight).astype(jnp.bfloat16)
+        share = jnp.dot(gate_delta, gate[tile], preferred_element_type=jnp.float32)
+        share = share + jnp.dot(up_delta, up[tile], preferred_element_type=jnp.float32)
         sum_ref[...] += share
-        prob_ref[...] += term
-
-    @pl.when(step == pl.num_programs(0) - 1)
-    def _():
-        high, low = (h.astype(jnp.float32) for h in high_low(scale * prob_ref[...]))
-        lane = iota((sum_ref.shape[0], lanes), 1)
-        facts = jnp.where(lane == 0, high, jnp.where(lane == 1, low, 0.0))
-        rows = outs[0].shape[0]
-        for i, out in enumerate(outs):
-            part = slice(i * rows, (i + 1) * rows)
-            out[:, :width] = sum_ref[part, :].astype(jnp.bfloat16)
-            out[:, width:] = facts[part].astype(jnp.bfloat16)
+        prob_ref[...] += jnp.sum(activated * back_proj, axis=1, keepdims=True)
+        return carry
+
+    lax.fori_loop(0, tiles, step, 0)
+    high, low = (h.astype(jnp.float32) for h in high_low(scale * prob_ref[...]))
+    lane = iota((sum_ref.shape[0], lanes), 1)
+    facts = jnp.where(lane == 0, high, jnp.where(lane == 1, low, 0.0))
+    stores = []
+    for i, (out, out_hbm) in enumerate(zip(outs, outs_hbm)):
+        rows = out.shape[0]
+        part = slice(i * rows, (i + 1) * rows)
+        out[:, :width] = sum_ref[part, :].astype(jnp.bfloat16)
+        out[:, width:] = facts[part].astype(jnp.bfloat16)
+        stores.append(copies.start(out, out_hbm))
+    quarter = owns_hbm[0].shape[1]
+    mine = pl.ds(pl.multiple_of(rank_ref[0] * quarter, lanes), quarter)
+    stores += [copies.start(every.at[:, mine], own) for every, own in zip(alls, owns_hbm)]
+    wait_all(stores)
 
 
 def weight_kernel(rank_ref, *refs, blocks, ready, rows, with_start):
     x_hbm, refs = refs[:blocks], refs[blocks:]
     q_hbm, refs = refs[:blocks], refs[blocks:]
-    delta_hbm, refs = refs[: 3 * ready], refs[3 * ready :]
+    deltas_hbm, refs = refs[: 3 * ready], refs[3 * ready :]
     weights_hbm, refs = refs[:3], refs[3:]
-    starts, refs = (refs[:3], refs[3:]) if with_start else ((), refs)
-    outs, refs = refs[:3], refs[3:]
+    starts_hbm, refs = (refs[:3], refs[3:]) if with_start else ((), refs)
+    outs_hbm, refs = refs[:3], refs[3:]
     x, q, gate_up, down, refs = *refs[:4], refs[4:]
-    parts, refs = refs[:3], refs[3:]
-    held = refs[:3] if with_start else ()
-    sems = refs[-1]
-    copies = []
-
-    def fetch(source, target):
-        copy = pltpu.make_async_copy(source, target, sems.at[len(copies)])
-        copy.start()
-        copies.append(copy)
-        return copy
-
+    parts, sums, sems = refs[:3], refs[3:6], refs[6]
+    copies = Copies(sems)
     quarter = down.shape[0]
     mine = pl.ds(rank_ref[0] * quarter, quarter)
     known = ready * rows
-    first = [fetch(weights_hbm[0].at[mine, :], gate_up.at[pl.ds(0, quarter)])]
-    first += [fetch(weights_hbm[1].at[mine, :], gate_up.at[pl.ds(quarter, quarter)])]
-    first += [fetch(x_hbm[b], x.at[pl.ds(b * rows, rows)]) for b in range(ready, blocks)]
-    second = [fetch(weights_hbm[2].at[mine, :], down)]
-    second += [fetch(q_hbm[b], q.at[pl.ds(b * rows, rows)]) for b in range(ready, blocks)]
+    place = lambda b: pl.ds(b * rows, rows)
+    first = [copies.start(x_hbm[b], x.at[place(b)]) for b in range(ready, blocks)]
+    for i in range(2):
+        target = gate_up.at[pl.ds(i * quarter, quarter)]
+        first.append(copies.start(weights_hbm[i].at[mine, :], target))
+    second = [copies.start(q_hbm[b], q.at[place(b)]) for b in range(ready, blocks)]
+    second.append(copies.start(weights_hbm[2].at[mine, :], down))
     third = []
     for b in range(ready):
-        part = pl.ds(b * rows, rows)
-        third += [fetch(x_hbm[b], x.at[part]), fetch(q_hbm[b], q.at[part])]
-        for i in range(3):
-            third += [fetch(delta_hbm[3 * b + i].at[:, mine], parts[i].at[part, :])]
-    third += [fetch(s, h) for s, h in zip(starts, held)]
-    for copy in first:
-        copy.wait()
+        third += [copies.start(x_hbm[b], x.at[place(b)]), copies.start(q_hbm[b], q.at[place(b)])]
+        third += [
+            copies.start(deltas_hbm[3 * b + i], parts[i].at[place(b)]) for i in range(3)
+        ]
+    third += [copies.start(s, h) for s, h in zip(starts_hbm, sums)]
+    wait_all(first)
     width = q.shape[1]
     pre = contract_last(x[known:, :width], gate_up[...])
-    for copy in second:
-        copy.wait()
+    wait_all(second)
     back_proj = contract_last(q[known:], down[...])
     _, weight = slot_facts(x[known:, width:])
     gate_pre, more = pre[:, :quarter], pre[:, quarter:] + 1.0
@@ -255,13 +282,15 @@
     parts[0][known:, :] = (delta * slope).astype(jnp.bfloat16)
     parts[1][known:, :] = (delta * gated).astype(jnp.bfloat16)
     parts[2][known:, :] = (more * gated * weight).astype(jnp.bfloat16)
-    for copy in third:
-        copy.wait()
+    wait_all(third)
+    stores = []
     for i, right in enumerate((x[:, :width], x[:, :width], q[...])):
         total = contract_first(parts[i][...], right)
         if with_start:
-            total = total + held[i][...]
-        outs[i][...] = total.astype(outs[i].dtype)
+            total = total + sums[i][...].astype(jnp.float32)
+        sums[i][...] = total.astype(jnp.bfloat16)
+        stores.append(copies.start(sums[i], outs_hbm[i]))
+    wait_all(stores)
 
 
 def combine_kernel(place_ref, facts_ref, *refs, routes, outer, inner):
@@ -316,12 +345,16 @@
     smem = pl.BlockSpec(memory_space=pltpu.SMEM)
     hbm = pl.BlockSpec(memory_space=pltpu.HBM)
 
-    token_x, token_q = pl.pallas_call(
+    token_x, token_q, token_facts = pl.pallas_call(
         functools.partial(prep_kernel, experts=ep_size),
-        out_shape=(shape((tok_rows, wide), bf16), shape((tok_rows, model_width), bf16)),
+        out_shape=(
+            shape((tok_rows, wide), bf16),
+            shape((tok_rows, model_width), bf16),
+            shape((tok_rows, lanes), bf16),
+        ),
         in_specs=[smem] + [vmem] * 5,
-        out_specs=(vmem,) * 2,
-        compiler_params=params(),
+        out_specs=(vmem,) * 3,
+        compiler_params=pltpu.CompilerParams(vmem_limit_bytes=24 << 20),
         name="prep",
     )(cap_counts, expert_ids.T, priority, probs.T, grad_out, tokens)
 
@@ -363,7 +396,7 @@
             + (shape((outer * tok_rows, inner * block), bf16),),
             in_specs=[smem] + [vmem] * len(chunks),
             out_specs=(vmem,) * (inner + 1),
-            compiler_params=params(),
+            compiler_params=pltpu.CompilerParams(vmem_limit_bytes=24 << 20),
             name="x_slots",
         )(spot, *chunks)
 
@@ -373,7 +406,7 @@
             out_shape=(shape((block, model_width), bf16),) * inner,
             in_specs=[smem] + [vmem] * (1 + len(chunks)),
             out_specs=(vmem,) * inner,
-            compiler_params=params(),
+            compiler_params=pltpu.CompilerParams(vmem_limit_bytes=24 << 20),
             name="q_slots",
         )(spot, table, *chunks)
 
@@ -388,38 +421,31 @@
     def expert_part(rows_x, rows_q):
         count = rows_q.shape[0]
         tiles = next(n for n in (3, 4, 2, 1) if hidden % (n * lanes) == 0)
+        pieces = count // capacity
         size = hidden // tiles
-        weights = pl.BlockSpec((size, model_width), lambda j: (j, 0))
-        units = pl.BlockSpec((count, size), lambda j: (0, j))
-        pieces = count // capacity
         results = pl.pallas_call(
-            expert_kernel,
-            grid=(tiles,),
-            in_specs=[
-                pl.BlockSpec((count, wide), lambda j: (0, 0)),
-                pl.BlockSpec((count, model_width), lambda j: (0, 0)),
-                weights,
-                weights,
-                weights,
-            ],
-            out_specs=[units] * 3 + [pl.BlockSpec((capacity, wide), lambda j: (0, 0))] * pieces,
-            scratch_shapes=[
-                pltpu.VMEM((count, model_width), f32),
-                pltpu.VMEM((count, 1), f32),
-            ],
-            out_shape=[shape((count, hidden), bf16)] * 3
+            functools.partial(expert_kernel, tiles=tiles),
+            in_specs=[smem] + [hbm] * 5,
+            out_specs=[hbm] * (3 + pieces),
+            scratch_shapes=[pltpu.VMEM((capacity, wide), bf16)] * pieces
+            + [pltpu.VMEM((count, wide), bf16), pltpu.VMEM((count, model_width), bf16)]
+            + [pltpu.VMEM((tiles, size, model_width), bf16)] * 3
+            + [pltpu.VMEM((count, hidden), bf16)] * 3
+            + [pltpu.VMEM((count, model_width), f32), pltpu.VMEM((count, 1), f32)]
+            + [pltpu.SemaphoreType.DMA((3, tiles)), pltpu.SemaphoreType.DMA((pieces + 5,))],
+            out_shape=[shape((count, quarter), bf16)] * 3
             + [shape((capacity, wide), bf16)] * pieces,
-            compiler_params=params(),
+            compiler_params=pltpu.CompilerParams(vmem_limit_bytes=48 << 20),
             cost_estimate=pl.CostEstimate(
                 flops=10 * count * model_width * hidden,
                 bytes_accessed=6 * hidden * model_width,
                 transcendentals=count * hidden,
             ),
             name="expert_part",
-        )(rows_x, rows_q, w_gate, w_up, w_down)
+        )(rank, rows_x, rows_q, w_gate, w_up, w_down)
         return results[:3], results[3:]
 
-    def weight_grads(blocks_x, blocks_q, deltas, start, out_type):
+    def weight_grads(blocks_x, blocks_q, deltas, start):
         counts = [b.shape[0] for b in blocks_x]
         if len(set(counts)) > 1:
             size = math.gcd(*counts)
@@ -435,9 +461,8 @@
         scratch += [pltpu.VMEM((2 * quarter, model_width), bf16)]
         scratch += [pltpu.VMEM((quarter, model_width), bf16)]
         scratch += [pltpu.VMEM((rows, quarter), bf16)] * 3
-        if start:
-            scratch += [pltpu.VMEM((quarter, model_width), f32)] * 3
-        scratch += [pltpu.SemaphoreType.DMA((len(operands),))]
+        scratch += [pltpu.VMEM((quarter, model_width), bf16)] * 3
+        scratch += [pltpu.SemaphoreType.DMA((len(operands) + 3,))]
         return pl.pallas_call(
             functools.partial(
                 weight_kernel,
@@ -446,11 +471,11 @@
                 rows=rows // count,
                 with_start=start is not None,
             ),
-            out_shape=(shape((quarter, model_width), out_type),) * 3,
+            out_shape=(shape((quarter, model_width), bf16),) * 3,
             in_specs=[smem] + [hbm] * len(operands),
-            out_specs=(vmem,) * 3,
+            out_specs=(hbm,) * 3,
             scratch_shapes=scratch,
-            compiler_params=params(),
+            compiler_params=pltpu.CompilerParams(vmem_limit_bytes=48 << 20),
             cost_estimate=pl.CostEstimate(
                 flops=12 * rows * model_width * quarter,
                 bytes_accessed=4 * rows * wide,
@@ -494,31 +519,18 @@
             home = lambda zz, ii: ((zz - s) % outer, (ii - d) % inner)
             rows = move(rows, home)
         backs.append(rows)
-    sums = weight_grads(
-        [near_sx[0], near_ox[0], *near_sx[1:], *near_ox[1:]],
-        [near_sq[0], near_oq[0], *near_sq[1:], *near_oq[1:]],
-        [same_deltas, other_deltas],
-        None,
-        f32,
-    )
-    sums = weight_grads(far_sx, far_sq, [], sums, f32)
-    shares = weight_grads(far_ox, far_oq, [], sums, bf16)
+    sums = weight_grads(near_sx, near_sq, [same_deltas], None)
+    sums = weight_grads(near_ox, near_oq, [other_deltas], sums)
+    sums = weight_grads(far_sx, far_sq, [], sums)
+    shares = weight_grads(far_ox, far_oq, [], sums)
     input_grad, prob_grad = pl.pallas_call(
         functools.partial(combine_kernel, routes=routes, outer=outer, inner=inner),
-        grid=(1,),
         out_shape=(shape((tok_rows, model_width), bf16), shape((routes, tok_rows), f32)),
-        in_specs=[
-            smem,
-            pl.BlockSpec((tok_rows, lanes), lambda j: (0, model_width // lanes)),
-        ]
-        + [pl.BlockSpec((capacity, wide), lambda j: (0, 0))] * len(backs),
-        out_specs=(
-            pl.BlockSpec((tok_rows, model_width), lambda j: (0, 0)),
-            pl.BlockSpec((routes, tok_rows), lambda j: (0, 0)),
-        ),
-        compiler_params=params(),
+        in_specs=[smem] + [vmem] * (1 + len(backs)),
+        out_specs=(vmem,) * 2,
+        compiler_params=pltpu.CompilerParams(vmem_limit_bytes=24 << 20),
         name="combine",
-    )(spot, token_x, *backs)
+    )(spot, token_facts, *backs)
     return (input_grad, prob_grad.T, *(share[None] for share in shares))
 
 

time: 233 us -> 257 us (1.10)
  local copies, waits for them, and re-layouts: 4.82 us -> 20.4 us
  starting transfers between devices: 37.2 us -> 52.3 us
  Pallas kernels: 80.5 us -> 72.9 us
    ppermute x12, waiting for transfers between devices: 18.6 us -> 36.5 us  [swap(): return lax.ppermute(rows, 'dp', [(d, d ^ step) for d in range(dp_size)])]
    ppermute x19, waiting for transfers between devices: 89.7 us -> 72.6 us  [move(): return lax.ppermute(rows, 'ep', pairs)]
    unnamed x52 -> x56, local copies, waits for them, and re-layouts: 4.82 us -> 20.4 us
    ppermute x19, starting transfers between devices: 32.2 us -> 46.1 us  [move(): return lax.ppermute(rows, 'ep', pairs)]
    pallas_call x2, Pallas kernels: 28.7 us -> 24.3 us  [expert_part(): pl.pallas_call(functools.partial(expert_kernel, tiles=tiles), in_specs=[s...]
    pallas_call x3 -> x4, Pallas kernels: 35 us -> 38.8 us  [weight_grads(): pl.pallas_call(functools.partial(weight_kernel, blocks=count, ready=ready...]
    pallas_call x1, Pallas kernels: 5.95 us -> 2.8 us  [x_slots(): pl.pallas_call(functools.partial(x_slots_kernel, outer=outer, inner=inner...]
  transfers between devices with their start and end apart: 31 -> 31, of which waited for: 13 -> 14; matrix products, arithmetic and copies ran while one was open for 0% -> 0% of each run, Pallas kernels for 27% -> 23%
where the time goes in v2:
time: 257 us
  waiting for transfers between devices  109 us (42%)
  Pallas kernels  72.9 us (28%)
  starting transfers between devices  52.3 us (20%)
  local copies, waits for them, and re-layouts  20.4 us (8%)
    ppermute x19, waiting for transfers between devices, move(): return lax.ppermute(rows, 'ep', pairs)  72.6 us
    ppermute x19, starting transfers between devices, move(): return lax.ppermute(rows, 'ep', pairs)  46.1 us
    pallas_call x4, Pallas kernels, weight_grads(): pl.pallas_call(functools.partial(weight_kernel, blocks=count, ready=ready...  38.8 us
    ppermute x12, waiting for transfers between devices, swap(): return lax.ppermute(rows, 'dp', [(d, d ^ step) for d in range(dp_size)])  36.5 us
    pallas_call x2, Pallas kernels, expert_part(): pl.pallas_call(functools.partial(expert_kernel, tiles=tiles), in_specs=[s...  24.3 us
    unnamed x56, local copies, waits for them, and re-layouts  20.4 us
    ppermute x12, starting transfers between devices, swap(): return lax.ppermute(rows, 'dp', [(d, d ^ step) for d in range(dp_size)])  6.16 us
  transfers between devices with their start and end apart: 31, of which 14 were waited for; matrix products, arithmetic and copies ran while one was open for 0% of the time, Pallas kernels for 23%

profile of v2, /device:TPU:0, one launch (start us, length us, event | category | flops | bytes accessed | tf_op | source)
XLA Modules:
  0.0 256.6 jit_solution(2369288001096912024)
XLA Ops:
  0.6 1.1 copy-done.6
  5.4 1.6 prep.1
  7.0 5.0 %collective-permute-start = (bf16[128,1664]{1,0:T(8,128)(2,1)S(1)}, bf16[128,1664]{1,0:T(8,128)(2,1)S(1)}, u32[]{:S(2)}, u32[]{:S(2)}) collective-permute-start(bf16[128,1664]{1,0:T(8,128)(2,1)S(1)} %get-tuple-element.42.refs_0_), channel_id=1, source_target_pairs={{0,8},{4,12},{8,16},{12,20},{16,24},{20,28},{1,9},{5,13},{9,17},{1... | collective-permute-start | bytes 1277960 | tf_op jit(solution)/shard_map/ppermute | solution.py:368
  12.0 1.3 collective-permute-start.1
  13.3 4.6 %collective-permute-start.5 = (bf16[128,1536]{1,0:T(8,128)(2,1)}, bf16[128,1536]{1,0:T(8,128)(2,1)S(1)}, u32[]{:S(2)}, u32[]{:S(2)}) collective-permute-start(bf16[128,1536]{1,0:T(8,128)(2,1)} %get-tuple-element.45.refs_0_), channel_id=1, source_target_pairs={{0,8},{4,12},{8,16},{12,20},{16,24},{20,28},{1,9},{5,13},{9,17},{1... | collective-permute-start | bytes 1179656 | tf_op jit(solution)/shard_map/ppermute | solution.py:368
  17.9 1.3 collective-permute-start.6
  19.2 3.0 %collective-permute-done.refs_1_ = bf16[128,1664]{1,0:T(8,128)(2,1)S(1)} collective-permute-done((bf16[128,1664]{1,0:T(8,128)(2,1)S(1)}, bf16[128,1664]{1,0:T(8,128)(2,1)S(1)}, u32[]{:S(2)}, u32[]{:S(2)}) %collective-permute-start) | collective-permute-done | bytes 426016 | tf_op jit(solution)/shard_map/ppermute | solution.py:368
  22.2 4.4 %collective-permute-done.1.refs_2_ = bf16[128,1664]{1,0:T(8,128)(2,1)S(1)} collective-permute-done((bf16[128,1664]{1,0:T(8,128)(2,1)S(1)}, bf16[128,1664]{1,0:T(8,128)(2,1)S(1)}, u32[]{:S(2)}, u32[]{:S(2)}) %collective-permute-start.1) | collective-permute-done | bytes 426016 | tf_op jit(solution)/shard_map/ppermute | solution.py:368
  26.6 1.3 collective-permute-start.4
  27.9 1.3 collective-permute-start.2
  29.9 13.2 %collective-permute-done.6.refs_2_ = bf16[128,1536]{1,0:T(8,128)(2,1)S(1)} collective-permute-done((bf16[128,1536]{1,0:T(8,128)(2,1)}, bf16[128,1536]{1,0:T(8,128)(2,1)S(1)}, u32[]{:S(2)}, u32[]{:S(2)}) %collective-permute-start.6) | collective-permute-done | bytes 393248 | tf_op jit(solution)/shard_map/ppermute | solution.py:368
  43.9 1.3 collective-permute-start.9
  45.2 1.3 collective-permute-start.7
  46.5 1.4 collective-permute-start.8
  47.9 12.7 %collective-permute-done.2.refs_3_ = bf16[128,1664]{1,0:T(8,128)(2,1)S(1)} collective-permute-done((bf16[128,1664]{1,0:T(8,128)(2,1)S(1)}, bf16[128,1664]{1,0:T(8,128)(2,1)S(1)}, u32[]{:S(2)}, u32[]{:S(2)}) %collective-permute-start.2) | collective-permute-done | bytes 426016 | tf_op jit(solution)/shard_map/ppermute | solution.py:368
  60.6 2.8 %x_slots.1 = (bf16[320,1664]{1,0:T(8,128)(2,1)S(1)}, bf16[320,1664]{1,0:T(8,128)(2,1)S(1)}, bf16[512,640]{1,0:T(8,128)(2,1)S(1)}) custom-call(s32[1]{0:T(128)} %bitcast.place_ref, bf16[128,1664]{1,0:T(8,128)(2,1)S(1)} %get-tuple-element.42.refs_0_, bf16[128,1664]{1,0:T(8,128)(2,1)S(1)} %collective-permute-done.refs_1_, ...), custom_call_target="tpu_custom_call" | custom-call | tf_op jit(solution)/shard_map/x_slots/pallas_call | solution.py:391
  63.4 5.4 %collective-permute-done.7.refs_3_ = bf16[128,1536]{1,0:T(8,128)(2,1)} collective-permute-done((bf16[128,1536]{1,0:T(8,128)(2,1)S(1)}, bf16[128,1536]{1,0:T(8,128)(2,1)}, u32[]{:S(2)}, u32[]{:S(2)}) %collective-permute-start.7) | collective-permute-done | bytes 393248 | tf_op jit(solution)/shard_map/ppermute | solution.py:368
  68.8 2.6 %q_slots.1 = (bf16[320,1536]{1,0:T(8,128)(2,1)S(1)}, bf16[320,1536]{1,0:T(8,128)(2,1)S(1)}) custom-call(s32[1]{0:T(128)} %bitcast.place_ref, bf16[512,640]{1,0:T(8,128)(2,1)S(1)} %get-tuple-element.44.table_ref, bf16[128,1536]{1,0:T(8,128)(2,1)} %get-tuple-element.45.refs_0_, bf16[128,1536]{1,0:T(8,128)(2,1)S(1)} %collective-permute-done.5.refs_1_, ...), custom_call_target="tpu_custom_call" | custom-call | tf_op jit(solution)/shard_map/q_slots/pallas_call | solution.py:404
  71.5 1.5 collective-permute-start.14
  73.6 12.1 %expert_part.2 = (bf16[320,384]{1,0:T(8,128)(2,1)S(1)}, bf16[320,384]{1,0:T(8,128)(2,1)S(1)}, bf16[320,384]{1,0:T(8,128)(2,1)S(1)}, bf16[80,1664]{1,0:T(8,128)(2...) custom-call(s32[1]{0:T(128)} %bitcast.3.rank_ref, ...), custom_call_target="tpu_custom_call" | custom-call | flops 7549747200 | bytes 14155776 | tf_op jit(solution)/shard_map/expert_part/pallas_call | solution.py:426
  88.2 2.8 %collective-permute-start.11 = (bf16[80,1664]{1,0:T(8,128)(2,1)S(1)}, bf16[80,1664]{1,0:T(8,128)(2,1)S(1)}, u32[]{:S(2)}, u32[]{:S(2)}) collective-permute-start(bf16[80,1664]{1,0:T(8,128)(2,1)S(1)} %get-tuple-element.49), channel_id=1, source_target_pairs={{0,16},{4,20},{8,24},{12,28},{16,0},{20,4},{24,8},{28,12},{1,17},{... | collective-permute-start | bytes 798728 | tf_op jit(solution)/shard_map/ppermute | solution.py:368
  90.9 5.1 %collective-permute-done.10.refs_1_ = bf16[80,1664]{1,0:T(8,128)(2,1)S(1)} collective-permute-done((bf16[80,1664]{1,0:T(8,128)(2,1)S(1)}, bf16[80,1664]{1,0:T(8,128)(2,1)S(1)}, u32[]{:S(2)}, u32[]{:S(2)}) %collective-permute-start.10) | collective-permute-done | bytes 266272 | tf_op jit(solution)/shard_map/ppermute | solution.py:368
  96.0 14.1 %collective-permute-start.12 = (bf16[80,1664]{1,0:T(8,128)(2,1)S(1)}, bf16[80,1664]{1,0:T(8,128)(2,1)S(1)}, u32[]{:S(2)}, u32[]{:S(2)}) collective-permute-start(bf16[80,1664]{1,0:T(8,128)(2,1)S(1)} %get-tuple-element.50), channel_id=1, source_target_pairs={{0,8},{4,12},{8,16},{12,20},{16,24},{20,28},{24,0},{28,4},{1,9},{5... | collective-permute-start | bytes 798728 | tf_op jit(solution)/shard_map/ppermute | solution.py:368
  110.2 4.0 %collective-permute-done.11.refs_2_ = bf16[80,1664]{1,0:T(8,128)(2,1)S(1)} collective-permute-done((bf16[80,1664]{1,0:T(8,128)(2,1)S(1)}, bf16[80,1664]{1,0:T(8,128)(2,1)S(1)}, u32[]{:S(2)}, u32[]{:S(2)}) %collective-permute-start.11) | collective-permute-done | bytes 266272 | tf_op jit(solution)/shard_map/ppermute | solution.py:368
  114.2 1.5 collective-permute-start.25
  116.2 2.3 collective-permute-done.13.x_hbm.refs_0_
  118.5 1.5 collective-permute-start.19
  120.0 12.1 %expert_part.3 = (bf16[320,384]{1,0:T(8,128)(2,1)S(1)}, bf16[320,384]{1,0:T(8,128)(2,1)S(1)}, bf16[320,384]{1,0:T(8,128)(2,1)S(1)}, bf16[80,1664]{1,0:T(8,128)(2...) custom-call(s32[1]{0:T(128)} %bitcast.3.rank_ref, ...), custom_call_target="tpu_custom_call" | custom-call | flops 7549747200 | bytes 14155776 | tf_op jit(solution)/shard_map/expert_part/pallas_call | solution.py:426
  134.3 4.7 %collective-permute-done.25.refs_2_ = bf16[320,1536]{1,0:T(8,128)(2,1)} collective-permute-done((bf16[320,1536]{1,0:T(8,128)(2,1)S(1)}, bf16[320,1536]{1,0:T(8,128)(2,1)}, u32[]{:S(2)}, u32[]{:S(2)}) %collective-permute-start.25) | collective-permute-done | bytes 983072 | tf_op jit(solution)/shard_map/ppermute | solution.py:419
  138.9 1.5 collective-permute-start.15
  140.4 1.5 collective-permute-start.21
  142.0 19.7 %collective-permute-done.23.refs_0_ = bf16[320,1664]{1,0:T(8,128)(2,1)S(1)} collective-permute-done((bf16[320,1664]{1,0:T(8,128)(2,1)S(1)}, bf16[320,1664]{1,0:T(8,128)(2,1)S(1)}, u32[]{:S(2)}, u32[]{:S(2)}) %collective-permute-start.23) | collective-permute-done | bytes 1064992 | tf_op jit(solution)/shard_map/ppermute | solution.py:419
  161.6 1.7 collective-permute-start.16
  163.4 3.0 %collective-permute-start.17 = (bf16[80,1664]{1,0:T(8,128)(2,1)S(1)}, bf16[80,1664]{1,0:T(8,128)(2,1)S(1)}, u32[]{:S(2)}, u32[]{:S(2)}) collective-permute-start(bf16[80,1664]{1,0:T(8,128)(2,1)S(1)} %get-tuple-element.55), channel_id=1, source_target_pairs={{0,20},{4,16},{8,28},{12,24},{16,4},{20,0},{24,12},{28,8},{1,21},{... | collective-permute-start | bytes 798728 | tf_op jit(solution)/shard_map/ppermute | solution.py:368
  166.4 6.5 %collective-permute-done.16.refs_5_ = bf16[80,1664]{1,0:T(8,128)(2,1)S(1)} collective-permute-done((bf16[80,1664]{1,0:T(8,128)(2,1)S(1)}, bf16[80,1664]{1,0:T(8,128)(2,1)S(1)}, u32[]{:S(2)}, u32[]{:S(2)}) %collective-permute-start.16) | collective-permute-done | bytes 266272 | tf_op jit(solution)/shard_map/ppermute | solution.py:368
  172.9 6.7 %collective-permute-done.17.refs_6_ = bf16[80,1664]{1,0:T(8,128)(2,1)S(1)} collective-permute-done((bf16[80,1664]{1,0:T(8,128)(2,1)S(1)}, bf16[80,1664]{1,0:T(8,128)(2,1)S(1)}, u32[]{:S(2)}, u32[]{:S(2)}) %collective-permute-start.17) | collective-permute-done | bytes 266272 | tf_op jit(solution)/shard_map/ppermute | solution.py:368
  180.3 1.2 collective-permute-start.18
  181.4 9.4 %collective-permute-done.18.refs_7_ = bf16[80,1664]{1,0:T(8,128)(2,1)S(1)} collective-permute-done((bf16[80,1664]{1,0:T(8,128)(2,1)S(1)}, bf16[80,1664]{1,0:T(8,128)(2,1)S(1)}, u32[]{:S(2)}, u32[]{:S(2)}) %collective-permute-start.18) | collective-permute-done | bytes 266272 | tf_op jit(solution)/shard_map/ppermute | solution.py:368
  191.6 1.0 copy-done.2
  193.1 12.1 %collective-permute-done.21.refs_2_ = bf16[320,1536]{1,0:T(8,128)(2,1)} collective-permute-done((bf16[320,1536]{1,0:T(8,128)(2,1)S(1)}, bf16[320,1536]{1,0:T(8,128)(2,1)}, u32[]{:S(2)}, u32[]{:S(2)}) %collective-permute-start.21) | collective-permute-done | bytes 983072 | tf_op jit(solution)/shard_map/ppermute | solution.py:419
  208.5 8.7 %weight_grads.4 = (bf16[384,1536]{1,0:T(8,128)(2,1)S(1)}, bf16[384,1536]{1,0:T(8,128)(2,1)}, bf16[384,1536]{1,0:T(8,128)(2,1)}) custom-call(s32[1]{0:T(128)} %bitcast.3.rank_ref, bf16[320,1664]{1,0:T(8,128)(2,1)S(1)} %get-tuple-element.43.x_hbm.refs_0_, bf16[320,1664]{1,0:T(8,128)(2,1)S(1)} %collective-permute-done.29.refs_1_, ...), custom_call_target="tpu_custom_call" | custom-call | flops 4529848320 | bytes 4259840 | tf_op jit(solution)/shard_map/weight_grads/pallas_call | solution.py:466
  217.2 1.0 copy-done
  218.2 1.0 copy-done.9
  220.2 2.8 %combine.1 = (bf16[128,1536]{1,0:T(8,128)(2,1)}, f32[4,128]{1,0:T(4,128)}) custom-call(s32[1]{0:T(128)} %bitcast.place_ref, bf16[128,128]{1,0:T(8,128)(2,1)S(1)} %get-tuple-element.41.facts_ref, bf16[80,1664]{1,0:T(8,128)(2,1)S(1)} %get-tuple-element.47.refs_0_, bf16[80,1664]{1,0:T(8,128)(2,1)S(1)} %collective-permute-done.10.refs_1_, ...), custom_call_target="tpu_custom_call" | custom-call | tf_op jit(solution)/shard_map/combine/pallas_call | solution.py:526
  223.1 8.9 %weight_grads.5 = (bf16[384,1536]{1,0:T(8,128)(2,1)S(1)}, bf16[384,1536]{1,0:T(8,128)(2,1)}, bf16[384,1536]{1,0:T(8,128)(2,1)}) custom-call(s32[1]{0:T(128)} %bitcast.3.rank_ref, bf16[320,1664]{1,0:T(8,128)(2,1)S(1)} %collective-permute-done.13.x_hbm.refs_0_, bf16[320,1664]{1,0:T(8,128)(2,1)S(1)} %collective-permute-done.27.refs_1_, ...), custom_call_target="tpu_custom_call" | custom-call | flops 4529848320 | bytes 4259840 | tf_op jit(solution)/shard_map/weight_grads/pallas_call | solution.py:466
  233.9 1.2 copy-done.5
  235.1 10.9 %weight_grads.6 = (bf16[384,1536]{1,0:T(8,128)(2,1)S(1)}, bf16[384,1536]{1,0:T(8,128)(2,1)}, bf16[384,1536]{1,0:T(8,128)(2,1)}) custom-call(s32[1]{0:T(128)} %bitcast.3.rank_ref, bf16[320,1664]{1,0:T(8,128)(2,1)S(1)} %collective-permute-done.23.refs_0_, bf16[320,1664]{1,0:T(8,128)(2,1)S(1)} %collective-permute-done.24.refs_1_, ...), custom_call_target="tpu_custom_call" | custom-call | flops 4529848320 | bytes 4259840 | tf_op jit(solution)/shard_map/weight_grads/pallas_call | solution.py:466
  246.1 10.4 %weight_grads.7 = (bf16[384,1536]{1,0:T(8,128)(2,1)}, bf16[384,1536]{1,0:T(8,128)(2,1)}, bf16[384,1536]{1,0:T(8,128)(2,1)}) custom-call(s32[1]{0:T(128)} %bitcast.3.rank_ref, bf16[320,1664]{1,0:T(8,128)(2,1)S(1)} %collective-permute-done.19.refs_0_, bf16[320,1664]{1,0:T(8,128)(2,1)S(1)} %collective-permute-done.20.refs_1_, ...), custom_call_target="tpu_custom_call" | custom-call | flops 4529848320 | bytes 4259840 | tf_op jit(solution)/shard_map/weight_grads/pallas_call | solution.py:466
  (82 shorter events, 19.1 us)
Async XLA Ops:
  0.6 1.1 copy-start.6
  1.8 1.0 copy-start.7
  7.0 15.1 %collective-permute-start = (bf16[128,1664]{1,0:T(8,128)(2,1)S(1)}, bf16[128,1664]{1,0:T(8,128)(2,1)S(1)}, u32[]{:S(2)}, u32[]{:S(2)}) collective-permute-start(bf16[128,1664]{1,0:T(8,128)(2,1)S(1)} %get-tuple-element.42.refs_0_), channel_id=1, source_target_pairs={{0,8},{4,12},{8,16},{12,20},{16,24},{20,28},{1,9},{5,13},{9,17},{1... | collective-permute-start | bytes 1277960 | tf_op jit(solution)/shard_map/ppermute | solution.py:368
  12.0 14.6 %collective-permute-start.1 = (bf16[128,1664]{1,0:T(8,128)(2,1)S(1)}, bf16[128,1664]{1,0:T(8,128)(2,1)S(1)}, u32[]{:S(2)}, u32[]{:S(2)}) collective-permute-start(bf16[128,1664]{1,0:T(8,128)(2,1)S(1)} %get-tuple-element.42.refs_0_), channel_id=1, source_target_pairs={{8,0},{12,4},{16,8},{20,12},{24,16},{28,20},{9,1},{13,5},{17,9},{2... | collective-permute-start | bytes 1277960 | tf_op jit(solution)/shard_map/ppermute | solution.py:368
  13.3 16.6 %collective-permute-start.5 = (bf16[128,1536]{1,0:T(8,128)(2,1)}, bf16[128,1536]{1,0:T(8,128)(2,1)S(1)}, u32[]{:S(2)}, u32[]{:S(2)}) collective-permute-start(bf16[128,1536]{1,0:T(8,128)(2,1)} %get-tuple-element.45.refs_0_), channel_id=1, source_target_pairs={{0,8},{4,12},{8,16},{12,20},{16,24},{20,28},{1,9},{5,13},{9,17},{1... | collective-permute-start | bytes 1179656 | tf_op jit(solution)/shard_map/ppermute | solution.py:368
  17.9 25.2 %collective-permute-start.6 = (bf16[128,1536]{1,0:T(8,128)(2,1)}, bf16[128,1536]{1,0:T(8,128)(2,1)S(1)}, u32[]{:S(2)}, u32[]{:S(2)}) collective-permute-start(bf16[128,1536]{1,0:T(8,128)(2,1)} %get-tuple-element.45.refs_0_), channel_id=1, source_target_pairs={{8,0},{12,4},{16,8},{20,12},{24,16},{28,20},{9,1},{13,5},{17,9},{2... | collective-permute-start | bytes 1179656 | tf_op jit(solution)/shard_map/ppermute | solution.py:368
  26.6 19.8 %collective-permute-start.4 = (bf16[128,1664]{1,0:T(8,128)(2,1)S(1)}, bf16[128,1664]{1,0:T(8,128)(2,1)S(1)}, u32[]{:S(2)}, u32[]{:S(2)}) collective-permute-start(bf16[128,1664]{1,0:T(8,128)(2,1)S(1)} %broadcast_select_fusion), channel_id=1, source_target_pairs={{8,24},{12,28},{16,0},{20,4},{9,25},{13,29},{17,1},{21,5},{10,26},... | collective-permute-start | bytes 1277960 | tf_op jit(solution)/shard_map/ppermute | solution.py:368
  27.9 32.7 %collective-permute-start.2 = (bf16[128,1664]{1,0:T(8,128)(2,1)S(1)}, bf16[128,1664]{1,0:T(8,128)(2,1)S(1)}, u32[]{:S(2)}, u32[]{:S(2)}) collective-permute-start(bf16[128,1664]{1,0:T(8,128)(2,1)S(1)} %collective-permute-done.1.refs_2_), channel_id=1, source_target_pairs={{8,0},{12,4},{16,8},{20,12},{9,1},{13,5},{17,9},{21,13},{10,2},{14... | collective-permute-start | bytes 1277960 | tf_op jit(solution)/shard_map/ppermute | solution.py:368
  29.2 31.4 %collective-permute-start.3 = (bf16[128,1664]{1,0:T(8,128)(2,1)S(1)}, bf16[128,1664]{1,0:T(8,128)(2,1)S(1)}, u32[]{:S(2)}, u32[]{:S(2)}) collective-permute-start(bf16[128,1664]{1,0:T(8,128)(2,1)S(1)} %collective-permute-done.refs_1_), channel_id=1, source_target_pairs={{8,16},{12,20},{16,24},{20,28},{9,17},{13,21},{17,25},{21,29},{10,... | collective-permute-start | bytes 1277960 | tf_op jit(solution)/shard_map/ppermute | solution.py:368
  43.9 19.5 %collective-permute-start.9 = (bf16[128,1536]{1,0:T(8,128)(2,1)}, bf16[128,1536]{1,0:T(8,128)(2,1)}, u32[]{:S(2)}, u32[]{:S(2)}) collective-permute-start(bf16[128,1536]{1,0:T(8,128)(2,1)} %broadcast_select_fusion.1), channel_id=1, source_target_pairs={{8,24},{12,28},{16,0},{20,4},{9,25},{13,29},{17,1},{21,5},{10,26},... | collective-permute-start | bytes 1179656 | tf_op jit(solution)/shard_map/ppermute | solution.py:368
  45.2 23.6 %collective-permute-start.7 = (bf16[128,1536]{1,0:T(8,128)(2,1)S(1)}, bf16[128,1536]{1,0:T(8,128)(2,1)}, u32[]{:S(2)}, u32[]{:S(2)}) collective-permute-start(bf16[128,1536]{1,0:T(8,128)(2,1)S(1)} %collective-permute-done.6.refs_2_), channel_id=1, source_target_pairs={{8,0},{12,4},{16,8},{20,12},{9,1},{13,5},{17,9},{21,13},{10,2},{14... | collective-permute-start | bytes 1179656 | tf_op jit(solution)/shard_map/ppermute | solution.py:368
  46.5 22.3 %collective-permute-start.8 = (bf16[128,1536]{1,0:T(8,128)(2,1)S(1)}, bf16[128,1536]{1,0:T(8,128)(2,1)}, u32[]{:S(2)}, u32[]{:S(2)}) collective-permute-start(bf16[128,1536]{1,0:T(8,128)(2,1)S(1)} %collective-permute-done.5.refs_1_), channel_id=1, source_target_pairs={{8,16},{12,20},{16,24},{20,28},{9,17},{13,21},{17,25},{21,29},{10,... | collective-permute-start | bytes 1179656 | tf_op jit(solution)/shard_map/ppermute | solution.py:368
  71.4 44.3 %collective-permute-start.30 = (bf16[320,1536]{1,0:T(8,128)(2,1)S(1)}, bf16[320,1536]{1,0:T(8,128)(2,1)S(1)}, u32[]{:S(2)}, u32[]{:S(2)}) collective-permute-start(bf16[320,1536]{1,0:T(8,128)(2,1)S(1)} %get-tuple-element.46.q_hbm.refs_2_), channel_id=1, source_target_pairs={{0,1},{1,0},{2,3},{3,2},{4,5},{5,4},{6,7},{7,6},{8,9},{9,8},{10,11... | collective-permute-start | bytes 2949128 | tf_op jit(solution)/shard_map/ppermute | solution.py:419
  71.5 44.7 %collective-permute-start.14 = (bf16[320,1536]{1,0:T(8,128)(2,1)S(1)}, bf16[320,1536]{1,0:T(8,128)(2,1)S(1)}, u32[]{:S(2)}, u32[]{:S(2)}) collective-permute-start(bf16[320,1536]{1,0:T(8,128)(2,1)S(1)} %get-tuple-element.52), channel_id=1, source_target_pairs={{0,4},{4,0},{8,12},{12,8},{16,20},{20,16},{24,28},{28,24},{1,5},{5... | collective-permute-start | bytes 2949128 | tf_op jit(solution)/shard_map/ppermute | solution.py:368
  73.1 45.4 %collective-permute-start.13 = (bf16[320,1664]{1,0:T(8,128)(2,1)S(1)}, bf16[320,1664]{1,0:T(8,128)(2,1)S(1)}, u32[]{:S(2)}, u32[]{:S(2)}) collective-permute-start(bf16[320,1664]{1,0:T(8,128)(2,1)S(1)} %get-tuple-element.51), channel_id=1, source_target_pairs={{0,4},{4,0},{8,12},{12,8},{16,20},{20,16},{24,28},{28,24},{1,5},{5... | collective-permute-start | bytes 3194888 | tf_op jit(solution)/shard_map/ppermute | solution.py:368
  87.8 8.2 %collective-permute-start.10 = (bf16[80,1664]{1,0:T(8,128)(2,1)S(1)}, bf16[80,1664]{1,0:T(8,128)(2,1)S(1)}, u32[]{:S(2)}, u32[]{:S(2)}) collective-permute-start(bf16[80,1664]{1,0:T(8,128)(2,1)S(1)} %get-tuple-element.48), channel_id=1, source_target_pairs={{0,24},{4,28},{8,0},{12,4},{16,8},{20,12},{24,16},{28,20},{1,25},{... | collective-permute-start | bytes 798728 | tf_op jit(solution)/shard_map/ppermute | solution.py:368
  88.2 26.0 %collective-permute-start.11 = (bf16[80,1664]{1,0:T(8,128)(2,1)S(1)}, bf16[80,1664]{1,0:T(8,128)(2,1)S(1)}, u32[]{:S(2)}, u32[]{:S(2)}) collective-permute-start(bf16[80,1664]{1,0:T(8,128)(2,1)S(1)} %get-tuple-element.49), channel_id=1, source_target_pairs={{0,16},{4,20},{8,24},{12,28},{16,0},{20,4},{24,8},{28,12},{1,17},{... | collective-permute-start | bytes 798728 | tf_op jit(solution)/shard_map/ppermute | solution.py:368
  96.0 18.2 %collective-permute-start.12 = (bf16[80,1664]{1,0:T(8,128)(2,1)S(1)}, bf16[80,1664]{1,0:T(8,128)(2,1)S(1)}, u32[]{:S(2)}, u32[]{:S(2)}) collective-permute-start(bf16[80,1664]{1,0:T(8,128)(2,1)S(1)} %get-tuple-element.50), channel_id=1, source_target_pairs={{0,8},{4,12},{8,16},{12,20},{16,24},{20,28},{24,0},{28,4},{1,9},{5... | collective-permute-start | bytes 798728 | tf_op jit(solution)/shard_map/ppermute | solution.py:368
  114.2 26.2 %collective-permute-start.29 = (bf16[320,1664]{1,0:T(8,128)(2,1)S(1)}, bf16[320,1664]{1,0:T(8,128)(2,1)S(1)}, u32[]{:S(2)}, u32[]{:S(2)}) collective-permute-start(bf16[320,1664]{1,0:T(8,128)(2,1)S(1)} %get-tuple-element.43.x_hbm.refs_0_), channel_id=1, source_target_pairs={{0,1},{1,0},{2,3},{3,2},{4,5},{5,4},{6,7},{7,6},{8,9},{9,8},{10,11... | collective-permute-start | bytes 3194888 | tf_op jit(solution)/shard_map/ppermute | solution.py:419
  114.2 24.7 %collective-permute-start.25 = (bf16[320,1536]{1,0:T(8,128)(2,1)S(1)}, bf16[320,1536]{1,0:T(8,128)(2,1)}, u32[]{:S(2)}, u32[]{:S(2)}) collective-permute-start(bf16[320,1536]{1,0:T(8,128)(2,1)S(1)} %get-tuple-element.46.q_hbm.refs_2_), channel_id=1, source_target_pairs={{0,2},{1,3},{2,0},{3,1},{4,6},{5,7},{6,4},{7,5},{8,10},{9,11},{10,... | collective-permute-start | bytes 2949128 | tf_op jit(solution)/shard_map/ppermute | solution.py:419
  115.7 45.9 %collective-permute-start.23 = (bf16[320,1664]{1,0:T(8,128)(2,1)S(1)}, bf16[320,1664]{1,0:T(8,128)(2,1)S(1)}, u32[]{:S(2)}, u32[]{:S(2)}) collective-permute-start(bf16[320,1664]{1,0:T(8,128)(2,1)S(1)} %get-tuple-element.43.x_hbm.refs_0_), channel_id=1, source_target_pairs={{0,2},{1,3},{2,0},{3,1},{4,6},{5,7},{6,4},{7,5},{8,10},{9,11},{10,... | collective-permute-start | bytes 3194888 | tf_op jit(solution)/shard_map/ppermute | solution.py:419
  116.2 75.3 %collective-permute-start.28 = (bf16[320,1536]{1,0:T(8,128)(2,1)S(1)}, bf16[320,1536]{1,0:T(8,128)(2,1)S(1)}, u32[]{:S(2)}, u32[]{:S(2)}) collective-permute-start(bf16[320,1536]{1,0:T(8,128)(2,1)S(1)} %collective-permute-done.14.q_hbm.refs_2_), channel_id=1, source_target_pairs={{0,1},{1,0},{2,3},{3,2},{4,5},{5,4},{6,7},{7,6},{8,9},{9,8},{10,11... | collective-permute-start | bytes 2949128 | tf_op jit(solution)/shard_map/ppermute | solution.py:419
  118.5 86.7 %collective-permute-start.19 = (bf16[320,1664]{1,0:T(8,128)(2,1)S(1)}, bf16[320,1664]{1,0:T(8,128)(2,1)S(1)}, u32[]{:S(2)}, u32[]{:S(2)}) collective-permute-start(bf16[320,1664]{1,0:T(8,128)(2,1)S(1)} %collective-permute-done.13.x_hbm.refs_0_), channel_id=1, source_target_pairs={{0,2},{1,3},{2,0},{3,1},{4,6},{5,7},{6,4},{7,5},{8,10},{9,11},{10,... | collective-permute-start | bytes 3194888 | tf_op jit(solution)/shard_map/ppermute | solution.py:419
  138.9 24.4 %collective-permute-start.15 = (bf16[80,1664]{1,0:T(8,128)(2,1)S(1)}, bf16[80,1664]{1,0:T(8,128)(2,1)S(1)}, u32[]{:S(2)}, u32[]{:S(2)}) collective-permute-start(bf16[80,1664]{1,0:T(8,128)(2,1)S(1)} %get-tuple-element.53), channel_id=1, source_target_pairs={{0,4},{4,0},{8,12},{12,8},{16,20},{20,16},{24,28},{28,24},{1,5},{5... | collective-permute-start | bytes 798728 | tf_op jit(solution)/shard_map/ppermute | solution.py:368
  140.4 64.8 %collective-permute-start.21 = (bf16[320,1536]{1,0:T(8,128)(2,1)S(1)}, bf16[320,1536]{1,0:T(8,128)(2,1)}, u32[]{:S(2)}, u32[]{:S(2)}) collective-permute-start(bf16[320,1536]{1,0:T(8,128)(2,1)S(1)} %collective-permute-done.14.q_hbm.refs_2_), channel_id=1, source_target_pairs={{0,2},{1,3},{2,0},{3,1},{4,6},{5,7},{6,4},{7,5},{8,10},{9,11},{10,... | collective-permute-start | bytes 2949128 | tf_op jit(solution)/shard_map/ppermute | solution.py:419
  161.6 11.2 %collective-permute-start.16 = (bf16[80,1664]{1,0:T(8,128)(2,1)S(1)}, bf16[80,1664]{1,0:T(8,128)(2,1)S(1)}, u32[]{:S(2)}, u32[]{:S(2)}) collective-permute-start(bf16[80,1664]{1,0:T(8,128)(2,1)S(1)} %get-tuple-element.54), channel_id=1, source_target_pairs={{0,28},{4,24},{8,4},{12,0},{16,12},{20,8},{24,20},{28,16},{1,29},{... | collective-permute-start | bytes 798728 | tf_op jit(solution)/shard_map/ppermute | solution.py:368
  163.4 16.2 %collective-permute-start.17 = (bf16[80,1664]{1,0:T(8,128)(2,1)S(1)}, bf16[80,1664]{1,0:T(8,128)(2,1)S(1)}, u32[]{:S(2)}, u32[]{:S(2)}) collective-permute-start(bf16[80,1664]{1,0:T(8,128)(2,1)S(1)} %get-tuple-element.55), channel_id=1, source_target_pairs={{0,20},{4,16},{8,28},{12,24},{16,4},{20,0},{24,12},{28,8},{1,21},{... | collective-permute-start | bytes 798728 | tf_op jit(solution)/shard_map/ppermute | solution.py:368
  172.9 50.1 %collective-permute-start.27 = (bf16[320,1664]{1,0:T(8,128)(2,1)S(1)}, bf16[320,1664]{1,0:T(8,128)(2,1)S(1)}, u32[]{:S(2)}, u32[]{:S(2)}) collective-permute-start(bf16[320,1664]{1,0:T(8,128)(2,1)S(1)} %collective-permute-done.13.x_hbm.refs_0_), channel_id=1, source_target_pairs={{0,1},{1,0},{2,3},{3,2},{4,5},{5,4},{6,7},{7,6},{8,9},{9,8},{10,11... | collective-permute-start | bytes 3194888 | tf_op jit(solution)/shard_map/ppermute | solution.py:419
  180.3 10.6 %collective-permute-start.18 = (bf16[80,1664]{1,0:T(8,128)(2,1)S(1)}, bf16[80,1664]{1,0:T(8,128)(2,1)S(1)}, u32[]{:S(2)}, u32[]{:S(2)}) collective-permute-start(bf16[80,1664]{1,0:T(8,128)(2,1)S(1)} %get-tuple-element.56), channel_id=1, source_target_pairs={{0,12},{4,8},{8,20},{12,16},{16,28},{20,24},{24,4},{28,0},{1,13},{... | collective-permute-start | bytes 798728 | tf_op jit(solution)/shard_map/ppermute | solution.py:368
  190.8 0.7 copy-start.10
  191.5 42.4 %collective-permute-start.24 = (bf16[320,1664]{1,0:T(8,128)(2,1)S(1)}, bf16[320,1664]{1,0:T(8,128)(2,1)S(1)}, u32[]{:S(2)}, u32[]{:S(2)}) collective-permute-start(bf16[320,1664]{1,0:T(8,128)(2,1)S(1)} %collective-permute-done.23.refs_0_), channel_id=1, source_target_pairs={{0,1},{1,0},{2,3},{3,2},{4,5},{5,4},{6,7},{7,6},{8,9},{9,8},{10,11... | collective-permute-start | bytes 3194888 | tf_op jit(solution)/shard_map/ppermute | solution.py:419
  191.6 1.0 copy-start.2
  192.6 40.4 %collective-permute-start.26 = (bf16[320,1536]{1,0:T(8,128)(2,1)}, bf16[320,1536]{1,0:T(8,128)(2,1)S(1)}, u32[]{:S(2)}, u32[]{:S(2)}) collective-permute-start(bf16[320,1536]{1,0:T(8,128)(2,1)} %collective-permute-done.25.refs_2_), channel_id=1, source_target_pairs={{0,1},{1,0},{2,3},{3,2},{4,5},{5,4},{6,7},{7,6},{8,9},{9,8},{10,11... | collective-permute-start | bytes 2949128 | tf_op jit(solution)/shard_map/ppermute | solution.py:419
  205.2 40.9 %collective-permute-start.22 = (bf16[320,1536]{1,0:T(8,128)(2,1)}, bf16[320,1536]{1,0:T(8,128)(2,1)}, u32[]{:S(2)}, u32[]{:S(2)}) collective-permute-start(bf16[320,1536]{1,0:T(8,128)(2,1)} %collective-permute-done.21.refs_2_), channel_id=1, source_target_pairs={{0,1},{1,0},{2,3},{3,2},{4,5},{5,4},{6,7},{7,6},{8,9},{9,8},{10,11... | collective-permute-start | bytes 2949128 | tf_op jit(solution)/shard_map/ppermute | solution.py:419
  205.2 40.9 %collective-permute-start.20 = (bf16[320,1664]{1,0:T(8,128)(2,1)S(1)}, bf16[320,1664]{1,0:T(8,128)(2,1)S(1)}, u32[]{:S(2)}, u32[]{:S(2)}) collective-permute-start(bf16[320,1664]{1,0:T(8,128)(2,1)S(1)} %collective-permute-done.19.refs_0_), channel_id=1, source_target_pairs={{0,1},{1,0},{2,3},{3,2},{4,5},{5,4},{6,7},{7,6},{8,9},{9,8},{10,11... | collective-permute-start | bytes 3194888 | tf_op jit(solution)/shard_map/ppermute | solution.py:419
  205.7 0.9 copy-start.13
  206.6 0.9 copy-start.15
  207.6 0.9 copy-start.17
  208.5 14.5 %copy-start.19 = (bf16[320,384]{1,0:T(8,128)(2,1)S(1)}, bf16[320,384]{1,0:T(8,128)(2,1)}, u32[]{:S(2)}) copy-start(bf16[320,384]{1,0:T(8,128)(2,1)} %copy-done.18) | copy-start | bytes 737284
  217.2 1.0 copy-start
  218.2 4.8 %copy-start.3 = (bf16[320,1536]{1,0:T(8,128)(2,1)S(1)}, bf16[320,1536]{1,0:T(8,128)(2,1)}, u32[]{:S(2)}) copy-start(bf16[320,1536]{1,0:T(8,128)(2,1)} %copy-done.2) | copy-start | bytes 2949124
  218.2 1.0 copy-start.9
  219.3 1.0 copy-start.11
  220.2 2.8 %copy-start.21 = (bf16[320,384]{1,0:T(8,128)(2,1)S(1)}, bf16[320,384]{1,0:T(8,128)(2,1)}, u32[]{:S(2)}) copy-start(bf16[320,384]{1,0:T(8,128)(2,1)} %copy-done.20) | copy-start | bytes 737284
  220.2 2.8 %copy-start.23 = (bf16[320,384]{1,0:T(8,128)(2,1)S(1)}, bf16[320,384]{1,0:T(8,128)(2,1)}, u32[]{:S(2)}) copy-start(bf16[320,384]{1,0:T(8,128)(2,1)} %copy-done.22) | copy-start | bytes 737284
  232.0 1.0 copy-start.1
  233.0 0.9 copy-start.4
  233.9 1.2 copy-start.5
  (11 other events, 7.6 us)

commit v3 on v2

--- a/solution.py
+++ b/solution.py
@@ -23,6 +23,10 @@
     return lax.dot_general(
         first_op, second_op, (((0,), (0,)), ((), ())), preferred_element_type=jnp.float32
     )
+
+
+def in_hbm(*arrays):
+    return [pltpu.with_memory_space_constraint(a, pltpu.HBM) for a in arrays]
 
 
 def high_low(values):
@@ -169,10 +173,49 @@
         copy.wait()
 
 
-def expert_kernel(rank_ref, x_hbm, q_hbm, *refs, tiles):
+def activation(gate_pre, up_pre):
+    squash = jax.nn.sigmoid(sharpness * gate_pre)
+    gated = gate_pre * squash
+    more = up_pre + 1.0
+    return gated, more * gated, more * (squash + sharpness * gated * (1.0 - squash))
+
+
+def act_kernel(x_hbm, gate_hbm, up_hbm, *refs, tiles):
+    outs_hbm, outs, (x, gate, up, sems, own_sems) = refs[:3], refs[3:6], refs[6:]
+    size, width = gate.shape[1:]
+    copies = Copies(own_sems)
+
+    def tile_copy(i, tile):
+        source, target = ((gate_hbm, gate), (up_hbm, up))[i]
+        part = pl.ds(tile * size, size)
+        return pltpu.make_async_copy(source.at[part, :], target.at[tile], sems.at[i, tile])
+
+    load = copies.start(x_hbm, x)
+    for tile in range(tiles):
+        tile_copy(0, tile).start()
+        tile_copy(1, tile).start()
+    load.wait()
+
+    def step(tile, carry):
+        units = pl.ds(pl.multiple_of(tile * size, lanes), size)
+        tile_copy(0, tile).wait()
+        gate_pre = contract_last(x[:, :width], gate[tile])
+        tile_copy(1, tile).wait()
+        up_pre = contract_last(x[:, :width], up[tile])
+        for out, term in zip(outs, activation(gate_pre, up_pre)):
+            out[:, units] = term.astype(jnp.bfloat16)
+        return carry
+
+    lax.fori_loop(0, tiles, step, 0)
+    wait_all([copies.start(out, out_hbm) for out, out_hbm in zip(outs, outs_hbm)])
+
+
+def expert_kernel(rank_ref, x_hbm, q_hbm, *refs, tiles, known):
     weights_hbm, refs = refs[:3], refs[3:]
+    terms_hbm, refs = (refs[:3], refs[3:]) if known else ((), refs)
     owns_hbm, refs = refs[:3], refs[3:]
     *refs, x, q, gate, up, down, every_gate, every_up, every_act, sum_ref, prob_ref, sems, own_sems = refs
+    refs, terms = (refs[:-3], refs[-3:]) if known else (refs, ())
     outs_hbm, outs = refs[: len(refs) // 2], refs[len(refs) // 2 :]
     weights, alls = (gate, up, down), (every_gate, every_up, every_act)
     size, width = gate.shape[1:]
@@ -184,40 +227,49 @@
             weights_hbm[i].at[part, :], weights[i].at[tile], sems.at[i, tile]
         )
 
-    loads = [copies.start(x_hbm, x)]
-    tile_copy(0, 0).start()
-    tile_copy(1, 0).start()
-    loads.append(copies.start(q_hbm, q))
-    tile_copy(2, 0).start()
+    order = (2, 0, 1) if known else (0, 1, 2)
+    loads = [copies.start(q_hbm, q)] if known else [copies.start(x_hbm, x)]
+    tile_copy(order[0], 0).start()
+    facts_copy = None
+    if known:
+        facts_copy = copies.start(x_hbm.at[:, pl.ds(width, lanes)], x)
+        loads += [copies.start(source, term) for source, term in zip(terms_hbm, terms)]
+    else:
+        loads.append(copies.start(q_hbm, q))
+    tile_copy(order[1], 0).start()
+    tile_copy(order[2], 0).start()
     for tile in range(1, tiles):
-        for i in range(3):
+        for i in order:
             tile_copy(i, tile).start()
-    loads[0].wait()
-    scale, weight = slot_facts(x[:, width:])
+    if known:
+        facts_copy.wait()
+    wait_all(loads)
+    scale, weight = slot_facts(x[...] if known else x[:, width:])
     sum_ref[...] = jnp.zeros_like(sum_ref)
     prob_ref[...] = jnp.zeros_like(prob_ref)
-    loads[1].wait()
 
     def step(tile, carry):
         units = pl.ds(pl.multiple_of(tile * size, lanes), size)
-        rows = x[:, :width]
-        tile_copy(0, tile).wait()
-        gate_pre = contract_last(rows, gate[tile])
-        tile_copy(1, tile).wait()
-        up_pre = contract_last(rows, up[tile])
+        if known:
+            gated, activated, slope = (t[:, units].astype(jnp.float32) for t in terms)
+        else:
+            tile_copy(0, tile).wait()
+            gate_pre = contract_last(x[:, :width], gate[tile])
+            tile_copy(1, tile).wait()
+            gated, activated, slope = activation(
+                gate_pre, contract_last(x[:, :width], up[tile])
+            )
         tile_copy(2, tile).wait()
         back_proj = contract_last(q[...], down[tile])
-        squash = jax.nn.sigmoid(sharpness * gate_pre)
-        gated = gate_pre * squash
-        more = up_pre + 1.0
-        activated = more * gated
         delta = weight * back_proj
         up_delta = (delta * gated).astype(jnp.bfloat16)
-        slope = more * (squash + sharpness * gated * (1.0 - squash))
         gate_delta = (delta * slope).astype(jnp.bfloat16)
         every_gate[:, units] = gate_delta
         every_up[:, units] = up_delta
         every_act[:, units] = (activated * weight).astype(jnp.bfloat16)
+        if known:
+            tile_copy(0, tile).wait()
+            tile_copy(1, tile).wait()
         share = jnp.dot(gate_delta, gate[tile], preferred_element_type=jnp.float32)
         share = share + jnp.dot(up_delta, up[tile], preferred_element_type=jnp.float32)
         sum_ref[...] += share
@@ -274,14 +326,11 @@
     wait_all(second)
     back_proj = contract_last(q[known:], down[...])
     _, weight = slot_facts(x[known:, width:])
-    gate_pre, more = pre[:, :quarter], pre[:, quarter:] + 1.0
-    squash = jax.nn.sigmoid(sharpness * gate_pre)
-    gated = gate_pre * squash
+    gated, activated, slope = activation(pre[:, :quarter], pre[:, quarter:])
     delta = weight * back_proj
-    slope = more * (squash + sharpness * gated * (1.0 - squash))
     parts[0][known:, :] = (delta * slope).astype(jnp.bfloat16)
     parts[1][known:, :] = (delta * gated).astype(jnp.bfloat16)
-    parts[2][known:, :] = (more * gated * weight).astype(jnp.bfloat16)
+    parts[2][known:, :] = (activated * weight).astype(jnp.bfloat16)
     wait_all(third)
     stores = []
     for i, right in enumerate((x[:, :width], x[:, :width], q[...])):
@@ -354,7 +403,7 @@
         ),
         in_specs=[smem] + [vmem] * 5,
         out_specs=(vmem,) * 3,
-        compiler_params=pltpu.CompilerParams(vmem_limit_bytes=24 << 20),
+        compiler_params=pltpu.CompilerParams(vmem_limit_bytes=56 << 20),
         name="prep",
     )(cap_counts, expert_ids.T, priority, probs.T, grad_out, tokens)
 
@@ -418,31 +467,55 @@
     def swap(rows, step):
         return lax.ppermute(rows, "dp", [(d, d ^ step) for d in range(dp_size)])
 
-    def expert_part(rows_x, rows_q):
+    tiles = next(n for n in (3, 4, 2, 1) if hidden % (n * lanes) == 0)
+    size = hidden // tiles
+
+    def act_part(rows_x):
+        count = rows_x.shape[0]
+        return pl.pallas_call(
+            functools.partial(act_kernel, tiles=tiles),
+            in_specs=[hbm] * 3,
+            out_specs=[hbm] * 3,
+            scratch_shapes=[pltpu.VMEM((count, hidden), bf16)] * 3
+            + [pltpu.VMEM((count, wide), bf16)]
+            + [pltpu.VMEM((tiles, size, model_width), bf16)] * 2
+            + [pltpu.SemaphoreType.DMA((2, tiles)), pltpu.SemaphoreType.DMA((4,))],
+            out_shape=[pltpu.HBM((count, hidden), bf16)] * 3,
+            compiler_params=pltpu.CompilerParams(vmem_limit_bytes=26 << 20),
+            cost_estimate=pl.CostEstimate(
+                flops=4 * count * model_width * hidden,
+                bytes_accessed=4 * hidden * model_width,
+                transcendentals=count * hidden,
+            ),
+            name="act_part",
+        )(*in_hbm(rows_x, w_gate, w_up))
+
+    def expert_part(rows_x, rows_q, terms):
         count = rows_q.shape[0]
-        tiles = next(n for n in (3, 4, 2, 1) if hidden % (n * lanes) == 0)
         pieces = count // capacity
-        size = hidden // tiles
+        loads = 5 + len(terms)
         results = pl.pallas_call(
-            functools.partial(expert_kernel, tiles=tiles),
-            in_specs=[smem] + [hbm] * 5,
+            functools.partial(expert_kernel, tiles=tiles, known=bool(terms)),
+            in_specs=[smem] + [hbm] * loads,
             out_specs=[hbm] * (3 + pieces),
             scratch_shapes=[pltpu.VMEM((capacity, wide), bf16)] * pieces
-            + [pltpu.VMEM((count, wide), bf16), pltpu.VMEM((count, model_width), bf16)]
+            + [pltpu.VMEM((count, hidden), bf16)] * len(terms)
+            + [pltpu.VMEM((count, lanes if terms else wide), bf16)]
+            + [pltpu.VMEM((count, model_width), bf16)]
             + [pltpu.VMEM((tiles, size, model_width), bf16)] * 3
             + [pltpu.VMEM((count, hidden), bf16)] * 3
             + [pltpu.VMEM((count, model_width), f32), pltpu.VMEM((count, 1), f32)]
-            + [pltpu.SemaphoreType.DMA((3, tiles)), pltpu.SemaphoreType.DMA((pieces + 5,))],
-            out_shape=[shape((count, quarter), bf16)] * 3
-            + [shape((capacity, wide), bf16)] * pieces,
-            compiler_params=pltpu.CompilerParams(vmem_limit_bytes=48 << 20),
+            + [pltpu.SemaphoreType.DMA((3, tiles)), pltpu.SemaphoreType.DMA((pieces + loads,))],
+            out_shape=[pltpu.HBM((count, quarter), bf16)] * 3
+            + [pltpu.HBM((capacity, wide), bf16)] * pieces,
+            compiler_params=pltpu.CompilerParams(vmem_limit_bytes=36 << 20),
             cost_estimate=pl.CostEstimate(
                 flops=10 * count * model_width * hidden,
                 bytes_accessed=6 * hidden * model_width,
                 transcendentals=count * hidden,
             ),
             name="expert_part",
-        )(rank, rows_x, rows_q, w_gate, w_up, w_down)
+        )(rank, *in_hbm(rows_x, rows_q, w_gate, w_up, w_down, *terms))
         return results[:3], results[3:]
 
     def weight_grads(blocks_x, blocks_q, deltas, start):
@@ -471,7 +544,7 @@
                 rows=rows // count,
                 with_start=start is not None,
             ),
-            out_shape=(shape((quarter, model_width), bf16),) * 3,
+            out_shape=(pltpu.HBM((quarter, model_width), bf16),) * 3,
             in_specs=[smem] + [hbm] * len(operands),
             out_specs=(hbm,) * 3,
             scratch_shapes=scratch,
@@ -482,7 +555,7 @@
                 transcendentals=rows * quarter,
             ),
             name="weight_grads",
-        )(rank, *operands)
+        )(rank, *in_hbm(*operands))
 
     half = dp_size // 2
 
@@ -510,8 +583,9 @@
     near_ox, far_ox = replicas(other_x)
     near_oq, far_oq = replicas(other_q)
 
-    same_deltas, same_back = expert_part(same_x, same_q)
-    other_deltas, other_back = expert_part(other_x, other_q)
+    same_terms = act_part(same_x)
+    same_deltas, same_back = expert_part(same_x, same_q, same_terms)
+    other_deltas, other_back = expert_part(other_x, other_q, [])
     backs = []
     for i, rows in enumerate([*same_back, *other_back]):
         d, s = i // outer, i % outer
@@ -520,8 +594,7 @@
             rows = move(rows, home)
         backs.append(rows)
     sums = weight_grads(near_sx, near_sq, [same_deltas], None)
-    sums = weight_grads(near_ox, near_oq, [other_deltas], sums)
-    sums = weight_grads(far_sx, far_sq, [], sums)
+    sums = weight_grads(near_ox + far_sx, near_oq + far_sq, [other_deltas], sums)
     shares = weight_grads(far_ox, far_oq, [], sums)
     input_grad, prob_grad = pl.pallas_call(
         functools.partial(combine_kernel, routes=routes, outer=outer, inner=inner),

time: 257 us -> 226 us (0.88)
  waiting for transfers between devices: 109 us -> 92.2 us
  local copies, waits for them, and re-layouts: 20.4 us -> 4.83 us
  Pallas kernels: 72.9 us -> 86 us
  starting transfers between devices: 52.3 us -> 40.2 us
    ppermute x12, waiting for transfers between devices: 36.5 us -> 15.2 us  [swap(): return lax.ppermute(rows, 'dp', [(d, d ^ step) for d in range(dp_size)])]
    pallas_call x2 -> x3, Pallas kernels: 24.3 us -> 41.1 us  [the longest x2 31.2 us: expert_part(): pl.pallas_call(functools.partial(expert_kernel, tiles=tiles, known=bool(t...]
    unnamed x56 -> x40, local copies, waits for them, and re-layouts: 20.4 us -> 4.83 us
    ppermute x19, starting transfers between devices: 46.1 us -> 34.7 us  [move(): return lax.ppermute(rows, 'ep', pairs)]
    pallas_call x4 -> x3, Pallas kernels: 38.8 us -> 33.8 us  [weight_grads(): pl.pallas_call(functools.partial(weight_kernel, blocks=count, ready=ready...]
    ppermute x19, waiting for transfers between devices: 72.6 us -> 77 us  [move(): return lax.ppermute(rows, 'ep', pairs)]
  transfers between devices with their start and end apart: 31 -> 31, of which waited for: 14 -> 11; matrix products, arithmetic and copies ran while one was open for 0% -> 0% of each run, Pallas kernels for 23% -> 31%
where the time goes in v3:
time: 226 us; the launch traced here: 225 us
  waiting for transfers between devices  92.2 us (41%)
  Pallas kernels  86 us (38%)
  starting transfers between devices  40.2 us (18%)
  local copies, waits for them, and re-layouts  4.83 us (2%)
    ppermute x19, waiting for transfers between devices, move(): return lax.ppermute(rows, 'ep', pairs)  77 us
    ppermute x19, starting transfers between devices, move(): return lax.ppermute(rows, 'ep', pairs)  34.7 us
    pallas_call x3, Pallas kernels, weight_grads(): pl.pallas_call(functools.partial(weight_kernel, blocks=count, ready=ready...  33.8 us
    pallas_call x2, Pallas kernels, expert_part(): pl.pallas_call(functools.partial(expert_kernel, tiles=tiles, known=bool(t...  31.2 us
    ppermute x12, waiting for transfers between devices, swap(): return lax.ppermute(rows, 'dp', [(d, d ^ step) for d in range(dp_size)])  15.2 us
    pallas_call x1, Pallas kernels, act_part(): pl.pallas_call(functools.partial(act_kernel, tiles=tiles), in_specs=[hbm]...  9.87 us
    ppermute x12, starting transfers between devices, swap(): return lax.ppermute(rows, 'dp', [(d, d ^ step) for d in range(dp_size)])  5.46 us
    unnamed x40, local copies, waits for them, and re-layouts  4.83 us
  transfers between devices with their start and end apart: 31, of which 11 were waited for; matrix products, arithmetic and copies ran while one was open for 0% of the time, Pallas kernels for 31%

profile of v3, /device:TPU:0, one launch (start us, length us, event | category | flops | bytes accessed | tf_op | source)
XLA Modules:
  0.0 225.2 jit_solution(5708752601816026453)
XLA Ops:
  0.6 2.6 %prep.1 = (bf16[128,1664]{1,0:T(8,128)(2,1)}, bf16[128,1536]{1,0:T(8,128)(2,1)}, bf16[128,128]{1,0:T(8,128)(2,1)}) custom-call(s32[8]{0:T(128)} %cap_ref.1, s32[4,128]{1,0:T(4,128)} %bitcast.28, s32[1,128]{1,0:T(1,128)} %order_ref.1, f32[4,128]{1,0:T(4,128)} %bitcast.29, f32[128,1536]{1,0:T(8,128)} %grad_ref.1, bf16[128,1536]{1,0:T(8,128)(2,1)} %tok_ref.1), custom_call_target="tpu_custom_call" | custom-call | tf_op jit(solution)/shard_map/prep/pallas_call | solution.py:397
  3.2 5.0 %collective-permute-start = (bf16[128,1664]{1,0:T(8,128)(2,1)}, bf16[128,1664]{1,0:T(8,128)(2,1)S(1)}, u32[]{:S(2)}, u32[]{:S(2)}) collective-permute-start(bf16[128,1664]{1,0:T(8,128)(2,1)} %get-tuple-element.42.refs_0_), channel_id=1, source_target_pairs={{0,8},{4,12},{8,16},{12,20},{16,24},{20,28},{1,9},{5,13},{9,17},{1... | collective-permute-start | bytes 1277960 | tf_op jit(solution)/shard_map/ppermute | solution.py:417
  8.2 1.3 collective-permute-start.1
  9.5 4.6 %collective-permute-start.5 = (bf16[128,1536]{1,0:T(8,128)(2,1)}, bf16[128,1536]{1,0:T(8,128)(2,1)S(1)}, u32[]{:S(2)}, u32[]{:S(2)}) collective-permute-start(bf16[128,1536]{1,0:T(8,128)(2,1)} %get-tuple-element.45.refs_0_), channel_id=1, source_target_pairs={{0,8},{4,12},{8,16},{12,20},{16,24},{20,28},{1,9},{5,13},{9,17},{1... | collective-permute-start | bytes 1179656 | tf_op jit(solution)/shard_map/ppermute | solution.py:417
  14.0 1.3 collective-permute-start.6
  15.4 3.3 %collective-permute-done.refs_1_ = bf16[128,1664]{1,0:T(8,128)(2,1)S(1)} collective-permute-done((bf16[128,1664]{1,0:T(8,128)(2,1)}, bf16[128,1664]{1,0:T(8,128)(2,1)S(1)}, u32[]{:S(2)}, u32[]{:S(2)}) %collective-permute-start) | collective-permute-done | bytes 426016 | tf_op jit(solution)/shard_map/ppermute | solution.py:417
  18.6 4.3 %collective-permute-done.1.refs_2_ = bf16[128,1664]{1,0:T(8,128)(2,1)S(1)} collective-permute-done((bf16[128,1664]{1,0:T(8,128)(2,1)}, bf16[128,1664]{1,0:T(8,128)(2,1)S(1)}, u32[]{:S(2)}, u32[]{:S(2)}) %collective-permute-start.1) | collective-permute-done | bytes 426016 | tf_op jit(solution)/shard_map/ppermute | solution.py:417
  23.0 1.3 collective-permute-start.4
  24.3 1.3 collective-permute-start.2
  25.6 0.7 collective-permute-start.3
  26.3 13.2 %collective-permute-done.6.refs_2_ = bf16[128,1536]{1,0:T(8,128)(2,1)S(1)} collective-permute-done((bf16[128,1536]{1,0:T(8,128)(2,1)}, bf16[128,1536]{1,0:T(8,128)(2,1)S(1)}, u32[]{:S(2)}, u32[]{:S(2)}) %collective-permute-start.6) | collective-permute-done | bytes 393248 | tf_op jit(solution)/shard_map/ppermute | solution.py:417
  39.5 0.8 broadcast_select_fusion.1
  40.3 1.3 collective-permute-start.9
  41.5 1.3 collective-permute-start.7
  42.9 1.4 collective-permute-start.8
  44.3 12.7 %collective-permute-done.2.refs_3_ = bf16[128,1664]{1,0:T(8,128)(2,1)S(1)} collective-permute-done((bf16[128,1664]{1,0:T(8,128)(2,1)S(1)}, bf16[128,1664]{1,0:T(8,128)(2,1)S(1)}, u32[]{:S(2)}, u32[]{:S(2)}) %collective-permute-start.2) | collective-permute-done | bytes 426016 | tf_op jit(solution)/shard_map/ppermute | solution.py:417
  57.0 2.8 %x_slots.1 = (bf16[320,1664]{1,0:T(8,128)(2,1)S(1)}, bf16[320,1664]{1,0:T(8,128)(2,1)S(1)}, bf16[512,640]{1,0:T(8,128)(2,1)S(1)}) custom-call(s32[1]{0:T(128)} %bitcast.place_ref, bf16[128,1664]{1,0:T(8,128)(2,1)S(1)} %copy-done.2, bf16[128,1664]{1,0:T(8,128)(2,1)S(1)} %collective-permute-done.refs_1_, bf16[128,1664]{1,0:T(8,128)(2,1)S(1)} %collective-permute-done.1.refs_2_, ...), custom_call_target="tpu_custom_call" | custom-call | tf_op jit(solution)/shard_map/x_slots/pallas_call | solution.py:440
  59.8 1.0 copy-done
  60.8 4.3 %collective-permute-done.7.refs_3_ = bf16[128,1536]{1,0:T(8,128)(2,1)} collective-permute-done((bf16[128,1536]{1,0:T(8,128)(2,1)S(1)}, bf16[128,1536]{1,0:T(8,128)(2,1)}, u32[]{:S(2)}, u32[]{:S(2)}) %collective-permute-start.7) | collective-permute-done | bytes 393248 | tf_op jit(solution)/shard_map/ppermute | solution.py:417
  65.2 2.9 %q_slots.1 = (bf16[320,1536]{1,0:T(8,128)(2,1)}, bf16[320,1536]{1,0:T(8,128)(2,1)S(1)}) custom-call(s32[1]{0:T(128)} %bitcast.place_ref, bf16[512,640]{1,0:T(8,128)(2,1)S(1)} %get-tuple-element.44.table_ref, bf16[128,1536]{1,0:T(8,128)(2,1)S(1)} %copy-done.3, bf16[128,1536]{1,0:T(8,128)(2,1)S(1)} %collective-permute-done.5.refs_1_, ...), custom_call_target="tpu_custom_call" | custom-call | tf_op jit(solution)/shard_map/q_slots/pallas_call | solution.py:453
  68.1 1.5 collective-permute-start.14
  69.6 0.5 collective-permute-start.13
  70.1 1.5 collective-permute-start.27
  71.7 9.9 %act_part.1 = (bf16[320,1536]{1,0:T(8,128)(2,1)}, bf16[320,1536]{1,0:T(8,128)(2,1)}, bf16[320,1536]{1,0:T(8,128)(2,1)}) custom-call(bf16[320,1664]{1,0:T(8,128)(2,1)} %copy-done, bf16[1536,1536]{1,0:T(8,128)(2,1)} %bitcast.11, bf16[1536,1536]{1,0:T(8,128)(2,1)} %bitcast.17), custom_call_target="tpu_custom_call" | custom-call | flops 3019898880 | bytes 9437184 | tf_op jit(solution)/shard_map/act_part/pallas_call | solution.py:475
  81.6 14.0 %expert_part.2 = (bf16[320,384]{1,0:T(8,128)(2,1)}, bf16[320,384]{1,0:T(8,128)(2,1)}, bf16[320,384]{1,0:T(8,128)(2,1)}, bf16[80,1664]{1,0:T(8,128)(2,1)}, bf16[8...) custom-call(s32[1]{0:T(128)} %bitcast.3.rank_ref, bf16[320,1664]{1,0:T(8,128)(2,1)} %copy-done, ...), custom_call_target="tpu_custom_call" | custom-call | flops 7549747200 | bytes 14155776 | tf_op jit(solution)/shard_map/expert_part/pallas_call | solution.py:497
  96.0 2.7 %collective-permute-start.11 = (bf16[80,1664]{1,0:T(8,128)(2,1)}, bf16[80,1664]{1,0:T(8,128)(2,1)S(1)}, u32[]{:S(2)}, u32[]{:S(2)}) collective-permute-start(bf16[80,1664]{1,0:T(8,128)(2,1)} %get-tuple-element.52), channel_id=1, source_target_pairs={{0,16},{4,20},{8,24},{12,28},{16,0},{20,4},{24,8},{28,12},{1,17},{... | collective-permute-start | bytes 798728 | tf_op jit(solution)/shard_map/ppermute | solution.py:417
  98.7 4.4 %collective-permute-done.10.refs_1_ = bf16[80,1664]{1,0:T(8,128)(2,1)S(1)} collective-permute-done((bf16[80,1664]{1,0:T(8,128)(2,1)}, bf16[80,1664]{1,0:T(8,128)(2,1)S(1)}, u32[]{:S(2)}, u32[]{:S(2)}) %collective-permute-start.10) | collective-permute-done | bytes 266272 | tf_op jit(solution)/shard_map/ppermute | solution.py:417
  103.1 11.4 %collective-permute-done.11.refs_2_ = bf16[80,1664]{1,0:T(8,128)(2,1)S(1)} collective-permute-done((bf16[80,1664]{1,0:T(8,128)(2,1)}, bf16[80,1664]{1,0:T(8,128)(2,1)S(1)}, u32[]{:S(2)}, u32[]{:S(2)}) %collective-permute-start.11) | collective-permute-done | bytes 266272 | tf_op jit(solution)/shard_map/ppermute | solution.py:417
  114.5 0.6 collective-permute-start.24
  115.4 0.7 copy-done.12
  116.1 17.2 %expert_part.3 = (bf16[320,384]{1,0:T(8,128)(2,1)}, bf16[320,384]{1,0:T(8,128)(2,1)}, bf16[320,384]{1,0:T(8,128)(2,1)}, bf16[80,1664]{1,0:T(8,128)(2,1)}, bf16[8...) custom-call(s32[1]{0:T(128)} %bitcast.3.rank_ref, bf16[320,1664]{1,0:T(8,128)(2,1)} %copy-done.12, ...), custom_call_target="tpu_custom_call" | custom-call | flops 7549747200 | bytes 14155776 | tf_op jit(solution)/shard_map/expert_part/pallas_call | solution.py:497
  133.4 1.6 collective-permute-start.15
  134.9 3.7 %collective-permute-start.16 = (bf16[80,1664]{1,0:T(8,128)(2,1)}, bf16[80,1664]{1,0:T(8,128)(2,1)S(1)}, u32[]{:S(2)}, u32[]{:S(2)}) collective-permute-start(bf16[80,1664]{1,0:T(8,128)(2,1)} %get-tuple-element.57), channel_id=1, source_target_pairs={{0,28},{4,24},{8,4},{12,0},{16,12},{20,8},{24,20},{28,16},{1,29},{... | collective-permute-start | bytes 798728 | tf_op jit(solution)/shard_map/ppermute | solution.py:417
  138.7 1.5 collective-permute-start.19
  140.4 0.5 collective-permute-start.21
  140.9 7.0 %collective-permute-done.15.refs_4_ = bf16[80,1664]{1,0:T(8,128)(2,1)S(1)} collective-permute-done((bf16[80,1664]{1,0:T(8,128)(2,1)}, bf16[80,1664]{1,0:T(8,128)(2,1)S(1)}, u32[]{:S(2)}, u32[]{:S(2)}) %collective-permute-start.15) | collective-permute-done | bytes 266272 | tf_op jit(solution)/shard_map/ppermute | solution.py:417
  148.0 2.7 %collective-permute-start.17 = (bf16[80,1664]{1,0:T(8,128)(2,1)}, bf16[80,1664]{1,0:T(8,128)(2,1)S(1)}, u32[]{:S(2)}, u32[]{:S(2)}) collective-permute-start(bf16[80,1664]{1,0:T(8,128)(2,1)} %get-tuple-element.58), channel_id=1, source_target_pairs={{0,20},{4,16},{8,28},{12,24},{16,4},{20,0},{24,12},{28,8},{1,21},{... | collective-permute-start | bytes 798728 | tf_op jit(solution)/shard_map/ppermute | solution.py:417
  150.6 2.1 collective-permute-start.18
  152.8 16.3 %collective-permute-done.17.refs_6_ = bf16[80,1664]{1,0:T(8,128)(2,1)S(1)} collective-permute-done((bf16[80,1664]{1,0:T(8,128)(2,1)}, bf16[80,1664]{1,0:T(8,128)(2,1)S(1)}, u32[]{:S(2)}, u32[]{:S(2)}) %collective-permute-start.17) | collective-permute-done | bytes 266272 | tf_op jit(solution)/shard_map/ppermute | solution.py:417
  169.1 0.5 collective-permute-start.23
  169.7 15.0 %collective-permute-done.21.refs_2_ = bf16[320,1536]{1,0:T(8,128)(2,1)S(1)} collective-permute-done((bf16[320,1536]{1,0:T(8,128)(2,1)}, bf16[320,1536]{1,0:T(8,128)(2,1)S(1)}, u32[]{:S(2)}, u32[]{:S(2)}) %collective-permute-start.21) | collective-permute-done | bytes 983072 | tf_op jit(solution)/shard_map/ppermute | solution.py:468
  184.7 0.5 collective-permute-start.20
  185.2 8.5 %weight_grads.3 = (bf16[384,1536]{1,0:T(8,128)(2,1)}, bf16[384,1536]{1,0:T(8,128)(2,1)}, bf16[384,1536]{1,0:T(8,128)(2,1)}) custom-call(s32[1]{0:T(128)} %bitcast.3.rank_ref, bf16[320,1664]{1,0:T(8,128)(2,1)} %copy-done, bf16[320,1664]{1,0:T(8,128)(2,1)} %copy-done.6, bf16[320,1536]{1,0:T(8,128)(2,1)} %get-tuple-element.46.q_hbm.refs_2_, ...), custom_call_target="tpu_custom_call" | custom-call | flops 4529848320 | bytes 4259840 | tf_op jit(solution)/shard_map/weight_grads/pallas_call | solution.py:539
  193.8 2.8 %combine.1 = (bf16[128,1536]{1,0:T(8,128)(2,1)}, f32[4,128]{1,0:T(4,128)}) custom-call(s32[1]{0:T(128)} %bitcast.place_ref, bf16[128,128]{1,0:T(8,128)(2,1)S(1)} %copy-done.5, bf16[80,1664]{1,0:T(8,128)(2,1)S(1)} %copy-done.4, bf16[80,1664]{1,0:T(8,128)(2,1)S(1)} %collective-permute-done.10.refs_1_, bf16[80,1664]{1,0:T(8,128)(2,1)S(1)} %collective-permute-done.11.refs_2_, ...), custom_call_target="tpu_custom_call" | custom-call | tf_op jit(solution)/shard_map/combine/pallas_call | solution.py:599
  196.7 0.9 copy-done.19
  198.3 14.5 %weight_grads.4 = (bf16[384,1536]{1,0:T(8,128)(2,1)}, bf16[384,1536]{1,0:T(8,128)(2,1)}, bf16[384,1536]{1,0:T(8,128)(2,1)}) custom-call(s32[1]{0:T(128)} %bitcast.3.rank_ref, bf16[320,1664]{1,0:T(8,128)(2,1)} %copy-done.12, bf16[320,1664]{1,0:T(8,128)(2,1)} %copy-done.15, bf16[320,1664]{1,0:T(8,128)(2,1)} %copy-done.13, bf16[320,1664]{1,0:T(8,128)(2,1)} %copy-done.14, ...), custom_call_target="tpu_custom_call" | custom-call | flops 9059696640 | bytes 8519680 | tf_op jit(solution)/shard_map/weight_grads/pallas_call | solution.py:539
  212.9 0.9 copy-done.11
  214.2 10.8 %weight_grads.5 = (bf16[384,1536]{1,0:T(8,128)(2,1)}, bf16[384,1536]{1,0:T(8,128)(2,1)}, bf16[384,1536]{1,0:T(8,128)(2,1)}) custom-call(s32[1]{0:T(128)} %bitcast.3.rank_ref, bf16[320,1664]{1,0:T(8,128)(2,1)} %copy-done.7, bf16[320,1664]{1,0:T(8,128)(2,1)} %copy-done.8, bf16[320,1536]{1,0:T(8,128)(2,1)} %copy-done.10, bf16[320,1536]{1,0:T(8,128)(2,1)} %copy-done.11, ...), custom_call_target="tpu_custom_call" | custom-call | flops 4529848320 | bytes 4259840 | tf_op jit(solution)/shard_map/weight_grads/pallas_call | solution.py:539
  (66 shorter events, 2.3 us)
Async XLA Ops:
  3.2 15.5 %collective-permute-start = (bf16[128,1664]{1,0:T(8,128)(2,1)}, bf16[128,1664]{1,0:T(8,128)(2,1)S(1)}, u32[]{:S(2)}, u32[]{:S(2)}) collective-permute-start(bf16[128,1664]{1,0:T(8,128)(2,1)} %get-tuple-element.42.refs_0_), channel_id=1, source_target_pairs={{0,8},{4,12},{8,16},{12,20},{16,24},{20,28},{1,9},{5,13},{9,17},{1... | collective-permute-start | bytes 1277960 | tf_op jit(solution)/shard_map/ppermute | solution.py:417
  8.2 14.8 %collective-permute-start.1 = (bf16[128,1664]{1,0:T(8,128)(2,1)}, bf16[128,1664]{1,0:T(8,128)(2,1)S(1)}, u32[]{:S(2)}, u32[]{:S(2)}) collective-permute-start(bf16[128,1664]{1,0:T(8,128)(2,1)} %get-tuple-element.42.refs_0_), channel_id=1, source_target_pairs={{8,0},{12,4},{16,8},{20,12},{24,16},{28,20},{9,1},{13,5},{17,9},{2... | collective-permute-start | bytes 1277960 | tf_op jit(solution)/shard_map/ppermute | solution.py:417
  9.5 16.8 %collective-permute-start.5 = (bf16[128,1536]{1,0:T(8,128)(2,1)}, bf16[128,1536]{1,0:T(8,128)(2,1)S(1)}, u32[]{:S(2)}, u32[]{:S(2)}) collective-permute-start(bf16[128,1536]{1,0:T(8,128)(2,1)} %get-tuple-element.45.refs_0_), channel_id=1, source_target_pairs={{0,8},{4,12},{8,16},{12,20},{16,24},{20,28},{1,9},{5,13},{9,17},{1... | collective-permute-start | bytes 1179656 | tf_op jit(solution)/shard_map/ppermute | solution.py:417
  14.0 25.4 %collective-permute-start.6 = (bf16[128,1536]{1,0:T(8,128)(2,1)}, bf16[128,1536]{1,0:T(8,128)(2,1)S(1)}, u32[]{:S(2)}, u32[]{:S(2)}) collective-permute-start(bf16[128,1536]{1,0:T(8,128)(2,1)} %get-tuple-element.45.refs_0_), channel_id=1, source_target_pairs={{8,0},{12,4},{16,8},{20,12},{24,16},{28,20},{9,1},{13,5},{17,9},{2... | collective-permute-start | bytes 1179656 | tf_op jit(solution)/shard_map/ppermute | solution.py:417
  15.4 41.6 %copy-start.2 = (bf16[128,1664]{1,0:T(8,128)(2,1)S(1)}, bf16[128,1664]{1,0:T(8,128)(2,1)}, u32[]{:S(2)}) copy-start(bf16[128,1664]{1,0:T(8,128)(2,1)} %get-tuple-element.42.refs_0_) | copy-start | bytes 1277956
  23.0 19.8 %collective-permute-start.4 = (bf16[128,1664]{1,0:T(8,128)(2,1)S(1)}, bf16[128,1664]{1,0:T(8,128)(2,1)S(1)}, u32[]{:S(2)}, u32[]{:S(2)}) collective-permute-start(bf16[128,1664]{1,0:T(8,128)(2,1)S(1)} %broadcast_select_fusion), channel_id=1, source_target_pairs={{8,24},{12,28},{16,0},{20,4},{9,25},{13,29},{17,1},{21,5},{10,26},... | collective-permute-start | bytes 1277960 | tf_op jit(solution)/shard_map/ppermute | solution.py:417
  24.3 32.7 %collective-permute-start.2 = (bf16[128,1664]{1,0:T(8,128)(2,1)S(1)}, bf16[128,1664]{1,0:T(8,128)(2,1)S(1)}, u32[]{:S(2)}, u32[]{:S(2)}) collective-permute-start(bf16[128,1664]{1,0:T(8,128)(2,1)S(1)} %collective-permute-done.1.refs_2_), channel_id=1, source_target_pairs={{8,0},{12,4},{16,8},{20,12},{9,1},{13,5},{17,9},{21,13},{10,2},{14... | collective-permute-start | bytes 1277960 | tf_op jit(solution)/shard_map/ppermute | solution.py:417
  25.6 31.4 %collective-permute-start.3 = (bf16[128,1664]{1,0:T(8,128)(2,1)S(1)}, bf16[128,1664]{1,0:T(8,128)(2,1)S(1)}, u32[]{:S(2)}, u32[]{:S(2)}) collective-permute-start(bf16[128,1664]{1,0:T(8,128)(2,1)S(1)} %collective-permute-done.refs_1_), channel_id=1, source_target_pairs={{8,16},{12,20},{16,24},{20,28},{9,17},{13,21},{17,25},{21,29},{10,... | collective-permute-start | bytes 1277960 | tf_op jit(solution)/shard_map/ppermute | solution.py:417
  40.3 20.6 %collective-permute-start.9 = (bf16[128,1536]{1,0:T(8,128)(2,1)}, bf16[128,1536]{1,0:T(8,128)(2,1)}, u32[]{:S(2)}, u32[]{:S(2)}) collective-permute-start(bf16[128,1536]{1,0:T(8,128)(2,1)} %broadcast_select_fusion.1), channel_id=1, source_target_pairs={{8,24},{12,28},{16,0},{20,4},{9,25},{13,29},{17,1},{21,5},{10,26},... | collective-permute-start | bytes 1179656 | tf_op jit(solution)/shard_map/ppermute | solution.py:417
  41.5 23.6 %collective-permute-start.7 = (bf16[128,1536]{1,0:T(8,128)(2,1)S(1)}, bf16[128,1536]{1,0:T(8,128)(2,1)}, u32[]{:S(2)}, u32[]{:S(2)}) collective-permute-start(bf16[128,1536]{1,0:T(8,128)(2,1)S(1)} %collective-permute-done.6.refs_2_), channel_id=1, source_target_pairs={{8,0},{12,4},{16,8},{20,12},{9,1},{13,5},{17,9},{21,13},{10,2},{14... | collective-permute-start | bytes 1179656 | tf_op jit(solution)/shard_map/ppermute | solution.py:417
  42.9 22.3 %collective-permute-start.8 = (bf16[128,1536]{1,0:T(8,128)(2,1)S(1)}, bf16[128,1536]{1,0:T(8,128)(2,1)}, u32[]{:S(2)}, u32[]{:S(2)}) collective-permute-start(bf16[128,1536]{1,0:T(8,128)(2,1)S(1)} %collective-permute-done.5.refs_1_), channel_id=1, source_target_pairs={{8,16},{12,20},{16,24},{20,28},{9,17},{13,21},{17,25},{21,29},{10,... | collective-permute-start | bytes 1179656 | tf_op jit(solution)/shard_map/ppermute | solution.py:417
  57.0 8.2 %copy-start.3 = (bf16[128,1536]{1,0:T(8,128)(2,1)S(1)}, bf16[128,1536]{1,0:T(8,128)(2,1)}, u32[]{:S(2)}) copy-start(bf16[128,1536]{1,0:T(8,128)(2,1)} %get-tuple-element.45.refs_0_) | copy-start | bytes 1179652
  59.8 1.0 copy-start
  68.1 46.4 %collective-permute-start.14 = (bf16[320,1536]{1,0:T(8,128)(2,1)S(1)}, bf16[320,1536]{1,0:T(8,128)(2,1)S(1)}, u32[]{:S(2)}, u32[]{:S(2)}) collective-permute-start(bf16[320,1536]{1,0:T(8,128)(2,1)S(1)} %get-tuple-element.55), channel_id=1, source_target_pairs={{0,4},{4,0},{8,12},{12,8},{16,20},{20,16},{24,28},{28,24},{1,5},{5... | collective-permute-start | bytes 2949128 | tf_op jit(solution)/shard_map/ppermute | solution.py:417
  69.6 45.5 %collective-permute-start.13 = (bf16[320,1664]{1,0:T(8,128)(2,1)S(1)}, bf16[320,1664]{1,0:T(8,128)(2,1)S(1)}, u32[]{:S(2)}, u32[]{:S(2)}) collective-permute-start(bf16[320,1664]{1,0:T(8,128)(2,1)S(1)} %get-tuple-element.54), channel_id=1, source_target_pairs={{0,4},{4,0},{8,12},{12,8},{16,20},{20,16},{24,28},{28,24},{1,5},{5... | collective-permute-start | bytes 3194888 | tf_op jit(solution)/shard_map/ppermute | solution.py:417
  70.1 44.9 %collective-permute-start.27 = (bf16[320,1536]{1,0:T(8,128)(2,1)}, bf16[320,1536]{1,0:T(8,128)(2,1)S(1)}, u32[]{:S(2)}, u32[]{:S(2)}) collective-permute-start(bf16[320,1536]{1,0:T(8,128)(2,1)} %get-tuple-element.46.q_hbm.refs_2_), channel_id=1, source_target_pairs={{0,2},{1,3},{2,0},{3,1},{4,6},{5,7},{6,4},{7,5},{8,10},{9,11},{10,... | collective-permute-start | bytes 2949128 | tf_op jit(solution)/shard_map/ppermute | solution.py:468
  81.5 32.9 %copy-start.1 = (bf16[320,1664]{1,0:T(8,128)(2,1)S(1)}, bf16[320,1664]{1,0:T(8,128)(2,1)}, u32[]{:S(2)}) copy-start(bf16[320,1664]{1,0:T(8,128)(2,1)} %copy-done) | copy-start | bytes 3194884
  95.6 7.5 %collective-permute-start.10 = (bf16[80,1664]{1,0:T(8,128)(2,1)}, bf16[80,1664]{1,0:T(8,128)(2,1)S(1)}, u32[]{:S(2)}, u32[]{:S(2)}) collective-permute-start(bf16[80,1664]{1,0:T(8,128)(2,1)} %get-tuple-element.51), channel_id=1, source_target_pairs={{0,24},{4,28},{8,0},{12,4},{16,8},{20,12},{24,16},{28,20},{1,25},{... | collective-permute-start | bytes 798728 | tf_op jit(solution)/shard_map/ppermute | solution.py:417
  96.0 18.5 %collective-permute-start.11 = (bf16[80,1664]{1,0:T(8,128)(2,1)}, bf16[80,1664]{1,0:T(8,128)(2,1)S(1)}, u32[]{:S(2)}, u32[]{:S(2)}) collective-permute-start(bf16[80,1664]{1,0:T(8,128)(2,1)} %get-tuple-element.52), channel_id=1, source_target_pairs={{0,16},{4,20},{8,24},{12,28},{16,0},{20,4},{24,8},{28,12},{1,17},{... | collective-permute-start | bytes 798728 | tf_op jit(solution)/shard_map/ppermute | solution.py:417
  103.1 31.8 %collective-permute-start.30 = (bf16[320,1536]{1,0:T(8,128)(2,1)}, bf16[320,1536]{1,0:T(8,128)(2,1)S(1)}, u32[]{:S(2)}, u32[]{:S(2)}) collective-permute-start(bf16[320,1536]{1,0:T(8,128)(2,1)} %get-tuple-element.46.q_hbm.refs_2_), channel_id=1, source_target_pairs={{0,1},{1,0},{2,3},{3,2},{4,5},{5,4},{6,7},{7,6},{8,9},{9,8},{10,11... | collective-permute-start | bytes 2949128 | tf_op jit(solution)/shard_map/ppermute | solution.py:468
  114.5 24.2 %collective-permute-start.29 = (bf16[320,1664]{1,0:T(8,128)(2,1)S(1)}, bf16[320,1664]{1,0:T(8,128)(2,1)S(1)}, u32[]{:S(2)}, u32[]{:S(2)}) collective-permute-start(bf16[320,1664]{1,0:T(8,128)(2,1)S(1)} %copy-done.1), channel_id=1, source_target_pairs={{0,1},{1,0},{2,3},{3,2},{4,5},{5,4},{6,7},{7,6},{8,9},{9,8},{10,11... | collective-permute-start | bytes 3194888 | tf_op jit(solution)/shard_map/ppermute | solution.py:468
  114.5 25.9 %collective-permute-start.24 = (bf16[320,1664]{1,0:T(8,128)(2,1)S(1)}, bf16[320,1664]{1,0:T(8,128)(2,1)S(1)}, u32[]{:S(2)}, u32[]{:S(2)}) collective-permute-start(bf16[320,1664]{1,0:T(8,128)(2,1)S(1)} %copy-done.1), channel_id=1, source_target_pairs={{0,2},{1,3},{2,0},{3,1},{4,6},{5,7},{6,4},{7,5},{8,10},{9,11},{10,... | collective-permute-start | bytes 3194888 | tf_op jit(solution)/shard_map/ppermute | solution.py:468
  115.1 18.3 %copy-start.17 = (bf16[320,1536]{1,0:T(8,128)(2,1)}, bf16[320,1536]{1,0:T(8,128)(2,1)S(1)}, u32[]{:S(2)}) copy-start(bf16[320,1536]{1,0:T(8,128)(2,1)S(1)} %collective-permute-done.27.refs_6_) | copy-start | bytes 2949124
  115.1 18.3 %collective-permute-start.12 = (bf16[80,1664]{1,0:T(8,128)(2,1)}, bf16[80,1664]{1,0:T(8,128)(2,1)S(1)}, u32[]{:S(2)}, u32[]{:S(2)}) collective-permute-start(bf16[80,1664]{1,0:T(8,128)(2,1)} %get-tuple-element.53), channel_id=1, source_target_pairs={{0,8},{4,12},{8,16},{12,20},{16,24},{20,28},{24,0},{28,4},{1,9},{5... | collective-permute-start | bytes 798728 | tf_op jit(solution)/shard_map/ppermute | solution.py:417
  115.1 1.0 copy-start.12
  115.1 54.6 %collective-permute-start.28 = (bf16[320,1536]{1,0:T(8,128)(2,1)S(1)}, bf16[320,1536]{1,0:T(8,128)(2,1)S(1)}, u32[]{:S(2)}, u32[]{:S(2)}) collective-permute-start(bf16[320,1536]{1,0:T(8,128)(2,1)S(1)} %collective-permute-done.27.refs_6_), channel_id=1, source_target_pairs={{0,1},{1,0},{2,3},{3,2},{4,5},{5,4},{6,7},{7,6},{8,9},{9,8},{10,11... | collective-permute-start | bytes 2949128 | tf_op jit(solution)/shard_map/ppermute | solution.py:468
  133.4 14.6 %collective-permute-start.15 = (bf16[80,1664]{1,0:T(8,128)(2,1)}, bf16[80,1664]{1,0:T(8,128)(2,1)S(1)}, u32[]{:S(2)}, u32[]{:S(2)}) collective-permute-start(bf16[80,1664]{1,0:T(8,128)(2,1)} %get-tuple-element.56), channel_id=1, source_target_pairs={{0,4},{4,0},{8,12},{12,8},{16,20},{20,16},{24,28},{28,24},{1,5},{5... | collective-permute-start | bytes 798728 | tf_op jit(solution)/shard_map/ppermute | solution.py:417
  134.9 50.3 %copy-start.9 = (bf16[320,1536]{1,0:T(8,128)(2,1)}, bf16[320,1536]{1,0:T(8,128)(2,1)S(1)}, u32[]{:S(2)}) copy-start(bf16[320,1536]{1,0:T(8,128)(2,1)S(1)} %collective-permute-done.30.refs_3_) | copy-start | bytes 2949124
  134.9 15.7 %collective-permute-start.16 = (bf16[80,1664]{1,0:T(8,128)(2,1)}, bf16[80,1664]{1,0:T(8,128)(2,1)S(1)}, u32[]{:S(2)}, u32[]{:S(2)}) collective-permute-start(bf16[80,1664]{1,0:T(8,128)(2,1)} %get-tuple-element.57), channel_id=1, source_target_pairs={{0,28},{4,24},{8,4},{12,0},{16,12},{20,8},{24,20},{28,16},{1,29},{... | collective-permute-start | bytes 798728 | tf_op jit(solution)/shard_map/ppermute | solution.py:417
  138.7 46.6 %copy-start.6 = (bf16[320,1664]{1,0:T(8,128)(2,1)}, bf16[320,1664]{1,0:T(8,128)(2,1)S(1)}, u32[]{:S(2)}) copy-start(bf16[320,1664]{1,0:T(8,128)(2,1)S(1)} %collective-permute-done.29.refs_1_) | copy-start | bytes 3194884
  138.7 46.0 %collective-permute-start.19 = (bf16[320,1664]{1,0:T(8,128)(2,1)}, bf16[320,1664]{1,0:T(8,128)(2,1)S(1)}, u32[]{:S(2)}, u32[]{:S(2)}) collective-permute-start(bf16[320,1664]{1,0:T(8,128)(2,1)} %copy-done.12), channel_id=1, source_target_pairs={{0,2},{1,3},{2,0},{3,1},{4,6},{5,7},{6,4},{7,5},{8,10},{9,11},{10,... | collective-permute-start | bytes 3194888 | tf_op jit(solution)/shard_map/ppermute | solution.py:468
  140.4 53.4 %copy-start.13 = (bf16[320,1664]{1,0:T(8,128)(2,1)}, bf16[320,1664]{1,0:T(8,128)(2,1)S(1)}, u32[]{:S(2)}) copy-start(bf16[320,1664]{1,0:T(8,128)(2,1)S(1)} %collective-permute-done.24.refs_2_) | copy-start | bytes 3194884
  140.4 44.3 %collective-permute-start.21 = (bf16[320,1536]{1,0:T(8,128)(2,1)}, bf16[320,1536]{1,0:T(8,128)(2,1)S(1)}, u32[]{:S(2)}, u32[]{:S(2)}) collective-permute-start(bf16[320,1536]{1,0:T(8,128)(2,1)} %copy-done.16), channel_id=1, source_target_pairs={{0,2},{1,3},{2,0},{3,1},{4,6},{5,7},{6,4},{7,5},{8,10},{9,11},{10,... | collective-permute-start | bytes 2949128 | tf_op jit(solution)/shard_map/ppermute | solution.py:468
  148.0 21.2 %collective-permute-start.17 = (bf16[80,1664]{1,0:T(8,128)(2,1)}, bf16[80,1664]{1,0:T(8,128)(2,1)S(1)}, u32[]{:S(2)}, u32[]{:S(2)}) collective-permute-start(bf16[80,1664]{1,0:T(8,128)(2,1)} %get-tuple-element.58), channel_id=1, source_target_pairs={{0,20},{4,16},{8,28},{12,24},{16,4},{20,0},{24,12},{28,8},{1,21},{... | collective-permute-start | bytes 798728 | tf_op jit(solution)/shard_map/ppermute | solution.py:417
  150.6 18.5 %collective-permute-start.18 = (bf16[80,1664]{1,0:T(8,128)(2,1)}, bf16[80,1664]{1,0:T(8,128)(2,1)S(1)}, u32[]{:S(2)}, u32[]{:S(2)}) collective-permute-start(bf16[80,1664]{1,0:T(8,128)(2,1)} %get-tuple-element.59), channel_id=1, source_target_pairs={{0,12},{4,8},{8,20},{12,16},{16,28},{20,24},{24,4},{28,0},{1,13},{... | collective-permute-start | bytes 798728 | tf_op jit(solution)/shard_map/ppermute | solution.py:417
  169.1 27.5 %collective-permute-start.25 = (bf16[320,1664]{1,0:T(8,128)(2,1)S(1)}, bf16[320,1664]{1,0:T(8,128)(2,1)S(1)}, u32[]{:S(2)}, u32[]{:S(2)}) collective-permute-start(bf16[320,1664]{1,0:T(8,128)(2,1)S(1)} %collective-permute-done.24.refs_2_), channel_id=1, source_target_pairs={{0,1},{1,0},{2,3},{3,2},{4,5},{5,4},{6,7},{7,6},{8,9},{9,8},{10,11... | collective-permute-start | bytes 3194888 | tf_op jit(solution)/shard_map/ppermute | solution.py:468
  169.1 27.5 %collective-permute-start.23 = (bf16[320,1664]{1,0:T(8,128)(2,1)}, bf16[320,1664]{1,0:T(8,128)(2,1)S(1)}, u32[]{:S(2)}, u32[]{:S(2)}) collective-permute-start(bf16[320,1664]{1,0:T(8,128)(2,1)} %copy-done.12), channel_id=1, source_target_pairs={{0,1},{1,0},{2,3},{3,2},{4,5},{5,4},{6,7},{7,6},{8,9},{9,8},{10,11... | collective-permute-start | bytes 3194888 | tf_op jit(solution)/shard_map/ppermute | solution.py:468
  169.6 24.1 %copy-start.18 = (bf16[320,1536]{1,0:T(8,128)(2,1)}, bf16[320,1536]{1,0:T(8,128)(2,1)S(1)}, u32[]{:S(2)}) copy-start(bf16[320,1536]{1,0:T(8,128)(2,1)S(1)} %collective-permute-done.28.refs_7_) | copy-start | bytes 2949124
  169.6 27.0 %collective-permute-start.26 = (bf16[320,1536]{1,0:T(8,128)(2,1)}, bf16[320,1536]{1,0:T(8,128)(2,1)S(1)}, u32[]{:S(2)}, u32[]{:S(2)}) collective-permute-start(bf16[320,1536]{1,0:T(8,128)(2,1)} %copy-done.16), channel_id=1, source_target_pairs={{0,1},{1,0},{2,3},{3,2},{4,5},{5,4},{6,7},{7,6},{8,9},{9,8},{10,11... | collective-permute-start | bytes 2949128 | tf_op jit(solution)/shard_map/ppermute | solution.py:468
  184.7 9.1 %copy-start.10 = (bf16[320,1536]{1,0:T(8,128)(2,1)}, bf16[320,1536]{1,0:T(8,128)(2,1)S(1)}, u32[]{:S(2)}) copy-start(bf16[320,1536]{1,0:T(8,128)(2,1)S(1)} %collective-permute-done.21.refs_2_) | copy-start | bytes 2949124
  184.7 28.1 %collective-permute-start.22 = (bf16[320,1536]{1,0:T(8,128)(2,1)S(1)}, bf16[320,1536]{1,0:T(8,128)(2,1)S(1)}, u32[]{:S(2)}, u32[]{:S(2)}) collective-permute-start(bf16[320,1536]{1,0:T(8,128)(2,1)S(1)} %collective-permute-done.21.refs_2_), channel_id=1, source_target_pairs={{0,1},{1,0},{2,3},{3,2},{4,5},{5,4},{6,7},{7,6},{8,9},{9,8},{10,11... | collective-permute-start | bytes 2949128 | tf_op jit(solution)/shard_map/ppermute | solution.py:468
  184.7 9.1 %copy-start.7 = (bf16[320,1664]{1,0:T(8,128)(2,1)}, bf16[320,1664]{1,0:T(8,128)(2,1)S(1)}, u32[]{:S(2)}) copy-start(bf16[320,1664]{1,0:T(8,128)(2,1)S(1)} %collective-permute-done.19.refs_0_) | copy-start | bytes 3194884
  184.7 28.1 %collective-permute-start.20 = (bf16[320,1664]{1,0:T(8,128)(2,1)S(1)}, bf16[320,1664]{1,0:T(8,128)(2,1)S(1)}, u32[]{:S(2)}, u32[]{:S(2)}) collective-permute-start(bf16[320,1664]{1,0:T(8,128)(2,1)S(1)} %collective-permute-done.19.refs_0_), channel_id=1, source_target_pairs={{0,1},{1,0},{2,3},{3,2},{4,5},{5,4},{6,7},{7,6},{8,9},{9,8},{10,11... | collective-permute-start | bytes 3194888 | tf_op jit(solution)/shard_map/ppermute | solution.py:468
  185.2 8.6 %copy-start.4 = (bf16[80,1664]{1,0:T(8,128)(2,1)S(1)}, bf16[80,1664]{1,0:T(8,128)(2,1)}, u32[]{:S(2)}) copy-start(bf16[80,1664]{1,0:T(8,128)(2,1)} %get-tuple-element.50.refs_0_) | copy-start | bytes 798724
  185.2 8.6 %copy-start.5 = (bf16[128,128]{1,0:T(8,128)(2,1)S(1)}, bf16[128,128]{1,0:T(8,128)(2,1)}, u32[]{:S(2)}) copy-start(bf16[128,128]{1,0:T(8,128)(2,1)} %get-tuple-element.41.facts_ref) | copy-start | bytes 98308
  196.6 1.4 copy-start.14
  196.7 1.7 copy-start.15
  212.9 1.3 copy-start.8
  (3 other events, 2.9 us)

commit v4 on v3

--- a/solution.py
+++ b/solution.py
@@ -199,8 +199,8 @@
     def step(tile, carry):
         units = pl.ds(pl.multiple_of(tile * size, lanes), size)
         tile_copy(0, tile).wait()
+        tile_copy(1, tile).wait()
         gate_pre = contract_last(x[:, :width], gate[tile])
-        tile_copy(1, tile).wait()
         up_pre = contract_last(x[:, :width], up[tile])
         for out, term in zip(outs, activation(gate_pre, up_pre)):
             out[:, units] = term.astype(jnp.bfloat16)
@@ -250,16 +250,14 @@
 
     def step(tile, carry):
         units = pl.ds(pl.multiple_of(tile * size, lanes), size)
+        for i in range(3):
+            tile_copy(i, tile).wait()
         if known:
             gated, activated, slope = (t[:, units].astype(jnp.float32) for t in terms)
         else:
-            tile_copy(0, tile).wait()
             gate_pre = contract_last(x[:, :width], gate[tile])
-            tile_copy(1, tile).wait()
-            gated, activated, slope = activation(
-                gate_pre, contract_last(x[:, :width], up[tile])
-            )
-        tile_copy(2, tile).wait()
+            up_pre = contract_last(x[:, :width], up[tile])
+            gated, activated, slope = activation(gate_pre, up_pre)
         back_proj = contract_last(q[...], down[tile])
         delta = weight * back_proj
         up_delta = (delta * gated).astype(jnp.bfloat16)
@@ -267,9 +265,6 @@
         every_gate[:, units] = gate_delta
         every_up[:, units] = up_delta
         every_act[:, units] = (activated * weight).astype(jnp.bfloat16)
-        if known:
-            tile_copy(0, tile).wait()
-            tile_copy(1, tile).wait()
         share = jnp.dot(gate_delta, gate[tile], preferred_element_type=jnp.float32)
         share = share + jnp.dot(up_delta, up[tile], preferred_element_type=jnp.float32)
         sum_ref[...] += share
@@ -481,14 +476,14 @@
             + [pltpu.VMEM((tiles, size, model_width), bf16)] * 2
             + [pltpu.SemaphoreType.DMA((2, tiles)), pltpu.SemaphoreType.DMA((4,))],
             out_shape=[pltpu.HBM((count, hidden), bf16)] * 3,
-            compiler_params=pltpu.CompilerParams(vmem_limit_bytes=26 << 20),
+            compiler_params=pltpu.CompilerParams(vmem_limit_bytes=48 << 20),
             cost_estimate=pl.CostEstimate(
                 flops=4 * count * model_width * hidden,
                 bytes_accessed=4 * hidden * model_width,
                 transcendentals=count * hidden,
             ),
             name="act_part",
-        )(*in_hbm(rows_x, w_gate, w_up))
+        )(rows_x, *in_hbm(w_gate, w_up))
 
     def expert_part(rows_x, rows_q, terms):
         count = rows_q.shape[0]
@@ -508,14 +503,14 @@
             + [pltpu.SemaphoreType.DMA((3, tiles)), pltpu.SemaphoreType.DMA((pieces + loads,))],
             out_shape=[pltpu.HBM((count, quarter), bf16)] * 3
             + [pltpu.HBM((capacity, wide), bf16)] * pieces,
-            compiler_params=pltpu.CompilerParams(vmem_limit_bytes=36 << 20),
+            compiler_params=pltpu.CompilerParams(vmem_limit_bytes=48 << 20),
             cost_estimate=pl.CostEstimate(
                 flops=10 * count * model_width * hidden,
                 bytes_accessed=6 * hidden * model_width,
                 transcendentals=count * hidden,
             ),
             name="expert_part",
-        )(rank, *in_hbm(rows_x, rows_q, w_gate, w_up, w_down, *terms))
+        )(rank, rows_x, rows_q, *in_hbm(w_gate, w_up, w_down, *terms))
         return results[:3], results[3:]
 
     def weight_grads(blocks_x, blocks_q, deltas, start):
@@ -528,8 +523,8 @@
                 columns = [cut(c) for c in zip(*deltas)]
                 deltas = list(zip(*columns))
         count, rows, ready = len(blocks_x), sum(counts), len(deltas)
-        operands = [*blocks_x, *blocks_q, *sum(map(list, deltas), [])]
-        operands += [w_gate, w_up, w_down, *(start or ())]
+        kept = [*sum(map(list, deltas), []), w_gate, w_up, w_down, *(start or ())]
+        operands = [*blocks_x, *blocks_q, *in_hbm(*kept)]
         scratch = [pltpu.VMEM((rows, wide), bf16), pltpu.VMEM((rows, model_width), bf16)]
         scratch += [pltpu.VMEM((2 * quarter, model_width), bf16)]
         scratch += [pltpu.VMEM((quarter, model_width), bf16)]
@@ -555,7 +550,7 @@
                 transcendentals=rows * quarter,
             ),
             name="weight_grads",
-        )(rank, *in_hbm(*operands))
+        )(rank, *operands)
 
     half = dp_size // 2
 

time: 226 us -> 217 us (0.960)
  Pallas kernels: 86 us -> 76.5 us
  waiting for transfers between devices: 92.2 us -> 101 us
  local copies, waits for them, and re-layouts: 4.83 us -> 0.02 us
  starting transfers between devices: 40.2 us -> 37.1 us
    ppermute x12, waiting for transfers between devices: 15.2 us -> 24.3 us  [swap(): return lax.ppermute(rows, 'dp', [(d, d ^ step) for d in range(dp_size)])]
    pallas_call x2, Pallas kernels: 31.2 us -> 26.1 us  [expert_part(): pl.pallas_call(functools.partial(expert_kernel, tiles=tiles, known=bool(t...]
    unnamed x40 -> x8, local copies, waits for them, and re-layouts: 4.83 us -> 0.02 us
    ppermute x19, starting transfers between devices: 34.7 us -> 31.9 us  [move(): return lax.ppermute(rows, 'ep', pairs)]
    pallas_call x1, Pallas kernels: 9.87 us -> 7.18 us  [act_part(): pl.pallas_call(functools.partial(act_kernel, tiles=tiles), in_specs=[hbm]...]
  transfers between devices with their start and end apart: 31 -> 31, of which waited for: 11 -> 12; matrix products, arithmetic and copies ran while one was open for 0% -> 0% of each run, Pallas kernels for 31% -> 28%
where the time goes in v4:
time: 217 us
  waiting for transfers between devices  101 us (47%)
  Pallas kernels  76.5 us (35%)
  starting transfers between devices  37.1 us (17%)
    ppermute x19, waiting for transfers between devices, move(): return lax.ppermute(rows, 'ep', pairs)  76.9 us
    pallas_call x3, Pallas kernels, weight_grads(): pl.pallas_call(functools.partial(weight_kernel, blocks=count, ready=ready...  32.5 us
    ppermute x19, starting transfers between devices, move(): return lax.ppermute(rows, 'ep', pairs)  31.9 us
    pallas_call x2, Pallas kernels, expert_part(): pl.pallas_call(functools.partial(expert_kernel, tiles=tiles, known=bool(t...  26.1 us
    ppermute x12, waiting for transfers between devices, swap(): return lax.ppermute(rows, 'dp', [(d, d ^ step) for d in range(dp_size)])  24.3 us
    pallas_call x1, Pallas kernels, act_part(): pl.pallas_call(functools.partial(act_kernel, tiles=tiles), in_specs=[hbm]...  7.18 us
    ppermute x12, starting transfers between devices, swap(): return lax.ppermute(rows, 'dp', [(d, d ^ step) for d in range(dp_size)])  5.15 us
  transfers between devices with their start and end apart: 31, of which 12 were waited for; matrix products, arithmetic and copies ran while one was open for 0% of the time, Pallas kernels for 28%

profile of v4, /device:TPU:0, one launch (start us, length us, event | category | flops | bytes accessed | tf_op | source)
XLA Modules:
  0.0 216.6 jit_solution(12169728056255617379)
XLA Ops:
  0.6 2.6 %prep.1 = (bf16[128,1664]{1,0:T(8,128)(2,1)}, bf16[128,1536]{1,0:T(8,128)(2,1)}, bf16[128,128]{1,0:T(8,128)(2,1)}) custom-call(s32[8]{0:T(128)} %cap_ref.1, s32[4,128]{1,0:T(4,128)} %bitcast.28, s32[1,128]{1,0:T(1,128)} %order_ref.1, f32[4,128]{1,0:T(4,128)} %bitcast.29, f32[128,1536]{1,0:T(8,128)} %grad_ref.1, bf16[128,1536]{1,0:T(8,128)(2,1)} %tok_ref.1), custom_call_target="tpu_custom_call" | custom-call | tf_op jit(solution)/shard_map/prep/pallas_call | solution.py:392
  3.2 5.0 %collective-permute-start = (bf16[128,1664]{1,0:T(8,128)(2,1)}, bf16[128,1664]{1,0:T(8,128)(2,1)S(1)}, u32[]{:S(2)}, u32[]{:S(2)}) collective-permute-start(bf16[128,1664]{1,0:T(8,128)(2,1)} %get-tuple-element.42.refs_0_), channel_id=1, source_target_pairs={{0,8},{4,12},{8,16},{12,20},{16,24},{20,28},{1,9},{5,13},{9,17},{1... | collective-permute-start | bytes 1277960 | tf_op jit(solution)/shard_map/ppermute | solution.py:412
  8.2 1.3 collective-permute-start.1
  9.5 4.6 %collective-permute-start.5 = (bf16[128,1536]{1,0:T(8,128)(2,1)}, bf16[128,1536]{1,0:T(8,128)(2,1)S(1)}, u32[]{:S(2)}, u32[]{:S(2)}) collective-permute-start(bf16[128,1536]{1,0:T(8,128)(2,1)} %get-tuple-element.45.refs_0_), channel_id=1, source_target_pairs={{0,8},{4,12},{8,16},{12,20},{16,24},{20,28},{1,9},{5,13},{9,17},{1... | collective-permute-start | bytes 1179656 | tf_op jit(solution)/shard_map/ppermute | solution.py:412
  14.0 1.3 collective-permute-start.6
  15.4 3.3 %collective-permute-done.refs_1_ = bf16[128,1664]{1,0:T(8,128)(2,1)S(1)} collective-permute-done((bf16[128,1664]{1,0:T(8,128)(2,1)}, bf16[128,1664]{1,0:T(8,128)(2,1)S(1)}, u32[]{:S(2)}, u32[]{:S(2)}) %collective-permute-start) | collective-permute-done | bytes 426016 | tf_op jit(solution)/shard_map/ppermute | solution.py:412
  18.6 4.3 %collective-permute-done.1.refs_2_ = bf16[128,1664]{1,0:T(8,128)(2,1)S(1)} collective-permute-done((bf16[128,1664]{1,0:T(8,128)(2,1)}, bf16[128,1664]{1,0:T(8,128)(2,1)S(1)}, u32[]{:S(2)}, u32[]{:S(2)}) %collective-permute-start.1) | collective-permute-done | bytes 426016 | tf_op jit(solution)/shard_map/ppermute | solution.py:412
  23.0 1.3 collective-permute-start.4
  24.3 1.3 collective-permute-start.2
  25.6 0.7 collective-permute-start.3
  26.3 13.2 %collective-permute-done.6.refs_2_ = bf16[128,1536]{1,0:T(8,128)(2,1)S(1)} collective-permute-done((bf16[128,1536]{1,0:T(8,128)(2,1)}, bf16[128,1536]{1,0:T(8,128)(2,1)S(1)}, u32[]{:S(2)}, u32[]{:S(2)}) %collective-permute-start.6) | collective-permute-done | bytes 393248 | tf_op jit(solution)/shard_map/ppermute | solution.py:412
  39.5 0.8 broadcast_select_fusion.1
  40.3 1.3 collective-permute-start.9
  41.5 1.3 collective-permute-start.7
  42.9 1.4 collective-permute-start.8
  44.3 12.7 %collective-permute-done.2.refs_3_ = bf16[128,1664]{1,0:T(8,128)(2,1)S(1)} collective-permute-done((bf16[128,1664]{1,0:T(8,128)(2,1)S(1)}, bf16[128,1664]{1,0:T(8,128)(2,1)S(1)}, u32[]{:S(2)}, u32[]{:S(2)}) %collective-permute-start.2) | collective-permute-done | bytes 426016 | tf_op jit(solution)/shard_map/ppermute | solution.py:412
  57.0 2.8 %x_slots.1 = (bf16[320,1664]{1,0:T(8,128)(2,1)S(1)}, bf16[320,1664]{1,0:T(8,128)(2,1)S(1)}, bf16[512,640]{1,0:T(8,128)(2,1)S(1)}) custom-call(s32[1]{0:T(128)} %bitcast.place_ref, bf16[128,1664]{1,0:T(8,128)(2,1)S(1)} %copy-done, bf16[128,1664]{1,0:T(8,128)(2,1)S(1)} %collective-permute-done.refs_1_, bf16[128,1664]{1,0:T(8,128)(2,1)S(1)} %collective-permute-done.1.refs_2_, ...), custom_call_target="tpu_custom_call" | custom-call | tf_op jit(solution)/shard_map/x_slots/pallas_call | solution.py:435
  59.8 5.4 %collective-permute-done.7.refs_3_ = bf16[128,1536]{1,0:T(8,128)(2,1)} collective-permute-done((bf16[128,1536]{1,0:T(8,128)(2,1)S(1)}, bf16[128,1536]{1,0:T(8,128)(2,1)}, u32[]{:S(2)}, u32[]{:S(2)}) %collective-permute-start.7) | collective-permute-done | bytes 393248 | tf_op jit(solution)/shard_map/ppermute | solution.py:412
  65.2 2.5 %q_slots.1 = (bf16[320,1536]{1,0:T(8,128)(2,1)S(1)}, bf16[320,1536]{1,0:T(8,128)(2,1)S(1)}) custom-call(s32[1]{0:T(128)} %bitcast.place_ref, bf16[512,640]{1,0:T(8,128)(2,1)S(1)} %get-tuple-element.44.table_ref, bf16[128,1536]{1,0:T(8,128)(2,1)S(1)} %copy-done.1, bf16[128,1536]{1,0:T(8,128)(2,1)S(1)} %collective-permute-done.5.refs_1_, ...), custom_call_target="tpu_custom_call" | custom-call | tf_op jit(solution)/shard_map/q_slots/pallas_call | solution.py:448
  67.7 1.6 collective-permute-start.14
  69.2 0.5 collective-permute-start.13
  69.8 1.5 collective-permute-start.27
  71.3 7.2 %act_part.1 = (bf16[320,1536]{1,0:T(8,128)(2,1)}, bf16[320,1536]{1,0:T(8,128)(2,1)}, bf16[320,1536]{1,0:T(8,128)(2,1)}) custom-call(bf16[320,1664]{1,0:T(8,128)(2,1)S(1)} %get-tuple-element.43.x_hbm.refs_0_, bf16[1536,1536]{1,0:T(8,128)(2,1)} %bitcast.11, bf16[1536,1536]{1,0:T(8,128)(2,1)} %bitcast.17), custom_call_target="tpu_custom_call" | custom-call | flops 3019898880 | bytes 9437184 | tf_op jit(solution)/shard_map/act_part/pallas_call | solution.py:470
  78.5 13.3 %expert_part.2 = (bf16[320,384]{1,0:T(8,128)(2,1)}, bf16[320,384]{1,0:T(8,128)(2,1)}, bf16[320,384]{1,0:T(8,128)(2,1)}, bf16[80,1664]{1,0:T(8,128)(2,1)}, bf16[8...) custom-call(s32[1]{0:T(128)} %bitcast.3.rank_ref, ...), custom_call_target="tpu_custom_call" | custom-call | flops 7549747200 | bytes 14155776 | tf_op jit(solution)/shard_map/expert_part/pallas_call | solution.py:492
  91.8 0.4 collective-permute-start.10
  92.2 2.8 %collective-permute-start.11 = (bf16[80,1664]{1,0:T(8,128)(2,1)}, bf16[80,1664]{1,0:T(8,128)(2,1)S(1)}, u32[]{:S(2)}, u32[]{:S(2)}) collective-permute-start(bf16[80,1664]{1,0:T(8,128)(2,1)} %get-tuple-element.52), channel_id=1, source_target_pairs={{0,16},{4,20},{8,24},{12,28},{16,0},{20,4},{24,8},{28,12},{1,17},{... | collective-permute-start | bytes 798728 | tf_op jit(solution)/shard_map/ppermute | solution.py:412
  95.0 4.3 %collective-permute-done.10.refs_1_ = bf16[80,1664]{1,0:T(8,128)(2,1)S(1)} collective-permute-done((bf16[80,1664]{1,0:T(8,128)(2,1)}, bf16[80,1664]{1,0:T(8,128)(2,1)S(1)}, u32[]{:S(2)}, u32[]{:S(2)}) %collective-permute-start.10) | collective-permute-done | bytes 266272 | tf_op jit(solution)/shard_map/ppermute | solution.py:412
  99.3 11.4 %collective-permute-done.11.refs_2_ = bf16[80,1664]{1,0:T(8,128)(2,1)S(1)} collective-permute-done((bf16[80,1664]{1,0:T(8,128)(2,1)}, bf16[80,1664]{1,0:T(8,128)(2,1)S(1)}, u32[]{:S(2)}, u32[]{:S(2)}) %collective-permute-start.11) | collective-permute-done | bytes 266272 | tf_op jit(solution)/shard_map/ppermute | solution.py:412
  110.7 0.5 collective-permute-start.24
  111.2 1.7 collective-permute-done.13.x_hbm.refs_0_
  112.9 12.8 %expert_part.3 = (bf16[320,384]{1,0:T(8,128)(2,1)}, bf16[320,384]{1,0:T(8,128)(2,1)}, bf16[320,384]{1,0:T(8,128)(2,1)}, bf16[80,1664]{1,0:T(8,128)(2,1)}, bf16[8...) custom-call(s32[1]{0:T(128)} %bitcast.3.rank_ref, ...), custom_call_target="tpu_custom_call" | custom-call | flops 7549747200 | bytes 14155776 | tf_op jit(solution)/shard_map/expert_part/pallas_call | solution.py:492
  125.8 1.6 collective-permute-start.15
  127.3 2.1 collective-permute-start.16
  129.5 1.5 collective-permute-start.19
  131.0 6.2 %collective-permute-done.24.refs_2_ = bf16[320,1664]{1,0:T(8,128)(2,1)} collective-permute-done((bf16[320,1664]{1,0:T(8,128)(2,1)S(1)}, bf16[320,1664]{1,0:T(8,128)(2,1)}, u32[]{:S(2)}, u32[]{:S(2)}) %collective-permute-start.24) | collective-permute-done | bytes 1064992 | tf_op jit(solution)/shard_map/ppermute | solution.py:463
  137.2 0.5 collective-permute-start.21
  137.7 2.9 %collective-permute-done.15.refs_4_ = bf16[80,1664]{1,0:T(8,128)(2,1)S(1)} collective-permute-done((bf16[80,1664]{1,0:T(8,128)(2,1)}, bf16[80,1664]{1,0:T(8,128)(2,1)S(1)}, u32[]{:S(2)}, u32[]{:S(2)}) %collective-permute-start.15) | collective-permute-done | bytes 266272 | tf_op jit(solution)/shard_map/ppermute | solution.py:412
  140.6 1.4 collective-permute-start.17
  142.0 2.2 collective-permute-start.18
  144.2 17.8 %collective-permute-done.17.refs_6_ = bf16[80,1664]{1,0:T(8,128)(2,1)S(1)} collective-permute-done((bf16[80,1664]{1,0:T(8,128)(2,1)}, bf16[80,1664]{1,0:T(8,128)(2,1)S(1)}, u32[]{:S(2)}, u32[]{:S(2)}) %collective-permute-start.17) | collective-permute-done | bytes 266272 | tf_op jit(solution)/shard_map/ppermute | solution.py:412
  161.9 0.5 collective-permute-start.23
  162.5 0.1 collective-permute-start.26
  162.5 18.0 %collective-permute-done.21.refs_2_ = bf16[320,1536]{1,0:T(8,128)(2,1)S(1)} collective-permute-done((bf16[320,1536]{1,0:T(8,128)(2,1)S(1)}, bf16[320,1536]{1,0:T(8,128)(2,1)S(1)}, u32[]{:S(2)}, u32[]{:S(2)}) %collective-permute-start.21) | collective-permute-done | bytes 983072 | tf_op jit(solution)/shard_map/ppermute | solution.py:463
  180.5 0.5 collective-permute-start.20
  181.0 8.1 %weight_grads.3 = (bf16[384,1536]{1,0:T(8,128)(2,1)}, bf16[384,1536]{1,0:T(8,128)(2,1)}, bf16[384,1536]{1,0:T(8,128)(2,1)}) custom-call(s32[1]{0:T(128)} %bitcast.3.rank_ref, bf16[320,1664]{1,0:T(8,128)(2,1)S(1)} %get-tuple-element.43.x_hbm.refs_0_, bf16[320,1664]{1,0:T(8,128)(2,1)S(1)} %collective-permute-done.29.refs_1_, ...), custom_call_target="tpu_custom_call" | custom-call | flops 4529848320 | bytes 4259840 | tf_op jit(solution)/shard_map/weight_grads/pallas_call | solution.py:534
  189.2 2.8 %combine.1 = (bf16[128,1536]{1,0:T(8,128)(2,1)}, f32[4,128]{1,0:T(4,128)}) custom-call(s32[1]{0:T(128)} %bitcast.place_ref, bf16[128,128]{1,0:T(8,128)(2,1)S(1)} %copy-done.3, bf16[80,1664]{1,0:T(8,128)(2,1)S(1)} %copy-done.2, bf16[80,1664]{1,0:T(8,128)(2,1)S(1)} %collective-permute-done.10.refs_1_, bf16[80,1664]{1,0:T(8,128)(2,1)S(1)} %collective-permute-done.11.refs_2_, ...), custom_call_target="tpu_custom_call" | custom-call | tf_op jit(solution)/shard_map/combine/pallas_call | solution.py:594
  192.0 14.1 %weight_grads.4 = (bf16[384,1536]{1,0:T(8,128)(2,1)}, bf16[384,1536]{1,0:T(8,128)(2,1)}, bf16[384,1536]{1,0:T(8,128)(2,1)}) custom-call(s32[1]{0:T(128)} %bitcast.3.rank_ref, bf16[320,1664]{1,0:T(8,128)(2,1)S(1)} %collective-permute-done.13.x_hbm.refs_0_, bf16[320,1664]{1,0:T(8,128)(2,1)S(1)} %collective-permute-done.23.refs_1_, ...), custom_call_target="tpu_custom_call" | custom-call | flops 9059696640 | bytes 8519680 | tf_op jit(solution)/shard_map/weight_grads/pallas_call | solution.py:534
  206.1 10.3 %weight_grads.5 = (bf16[384,1536]{1,0:T(8,128)(2,1)}, bf16[384,1536]{1,0:T(8,128)(2,1)}, bf16[384,1536]{1,0:T(8,128)(2,1)}) custom-call(s32[1]{0:T(128)} %bitcast.3.rank_ref, bf16[320,1664]{1,0:T(8,128)(2,1)S(1)} %collective-permute-done.19.refs_0_, bf16[320,1664]{1,0:T(8,128)(2,1)S(1)} %collective-permute-done.20.refs_1_, ...), custom_call_target="tpu_custom_call" | custom-call | flops 4529848320 | bytes 4259840 | tf_op jit(solution)/shard_map/weight_grads/pallas_call | solution.py:534
  (34 shorter events, 0.1 us)
Async XLA Ops:
  3.2 15.5 %collective-permute-start = (bf16[128,1664]{1,0:T(8,128)(2,1)}, bf16[128,1664]{1,0:T(8,128)(2,1)S(1)}, u32[]{:S(2)}, u32[]{:S(2)}) collective-permute-start(bf16[128,1664]{1,0:T(8,128)(2,1)} %get-tuple-element.42.refs_0_), channel_id=1, source_target_pairs={{0,8},{4,12},{8,16},{12,20},{16,24},{20,28},{1,9},{5,13},{9,17},{1... | collective-permute-start | bytes 1277960 | tf_op jit(solution)/shard_map/ppermute | solution.py:412
  8.2 14.8 %collective-permute-start.1 = (bf16[128,1664]{1,0:T(8,128)(2,1)}, bf16[128,1664]{1,0:T(8,128)(2,1)S(1)}, u32[]{:S(2)}, u32[]{:S(2)}) collective-permute-start(bf16[128,1664]{1,0:T(8,128)(2,1)} %get-tuple-element.42.refs_0_), channel_id=1, source_target_pairs={{8,0},{12,4},{16,8},{20,12},{24,16},{28,20},{9,1},{13,5},{17,9},{2... | collective-permute-start | bytes 1277960 | tf_op jit(solution)/shard_map/ppermute | solution.py:412
  9.5 16.8 %collective-permute-start.5 = (bf16[128,1536]{1,0:T(8,128)(2,1)}, bf16[128,1536]{1,0:T(8,128)(2,1)S(1)}, u32[]{:S(2)}, u32[]{:S(2)}) collective-permute-start(bf16[128,1536]{1,0:T(8,128)(2,1)} %get-tuple-element.45.refs_0_), channel_id=1, source_target_pairs={{0,8},{4,12},{8,16},{12,20},{16,24},{20,28},{1,9},{5,13},{9,17},{1... | collective-permute-start | bytes 1179656 | tf_op jit(solution)/shard_map/ppermute | solution.py:412
  14.0 25.4 %collective-permute-start.6 = (bf16[128,1536]{1,0:T(8,128)(2,1)}, bf16[128,1536]{1,0:T(8,128)(2,1)S(1)}, u32[]{:S(2)}, u32[]{:S(2)}) collective-permute-start(bf16[128,1536]{1,0:T(8,128)(2,1)} %get-tuple-element.45.refs_0_), channel_id=1, source_target_pairs={{8,0},{12,4},{16,8},{20,12},{24,16},{28,20},{9,1},{13,5},{17,9},{2... | collective-permute-start | bytes 1179656 | tf_op jit(solution)/shard_map/ppermute | solution.py:412
  15.4 41.6 %copy-start = (bf16[128,1664]{1,0:T(8,128)(2,1)S(1)}, bf16[128,1664]{1,0:T(8,128)(2,1)}, u32[]{:S(2)}) copy-start(bf16[128,1664]{1,0:T(8,128)(2,1)} %get-tuple-element.42.refs_0_) | copy-start | bytes 1277956
  23.0 19.8 %collective-permute-start.4 = (bf16[128,1664]{1,0:T(8,128)(2,1)S(1)}, bf16[128,1664]{1,0:T(8,128)(2,1)S(1)}, u32[]{:S(2)}, u32[]{:S(2)}) collective-permute-start(bf16[128,1664]{1,0:T(8,128)(2,1)S(1)} %broadcast_select_fusion), channel_id=1, source_target_pairs={{8,24},{12,28},{16,0},{20,4},{9,25},{13,29},{17,1},{21,5},{10,26},... | collective-permute-start | bytes 1277960 | tf_op jit(solution)/shard_map/ppermute | solution.py:412
  24.3 32.7 %collective-permute-start.2 = (bf16[128,1664]{1,0:T(8,128)(2,1)S(1)}, bf16[128,1664]{1,0:T(8,128)(2,1)S(1)}, u32[]{:S(2)}, u32[]{:S(2)}) collective-permute-start(bf16[128,1664]{1,0:T(8,128)(2,1)S(1)} %collective-permute-done.1.refs_2_), channel_id=1, source_target_pairs={{8,0},{12,4},{16,8},{20,12},{9,1},{13,5},{17,9},{21,13},{10,2},{14... | collective-permute-start | bytes 1277960 | tf_op jit(solution)/shard_map/ppermute | solution.py:412
  25.6 31.4 %collective-permute-start.3 = (bf16[128,1664]{1,0:T(8,128)(2,1)S(1)}, bf16[128,1664]{1,0:T(8,128)(2,1)S(1)}, u32[]{:S(2)}, u32[]{:S(2)}) collective-permute-start(bf16[128,1664]{1,0:T(8,128)(2,1)S(1)} %collective-permute-done.refs_1_), channel_id=1, source_target_pairs={{8,16},{12,20},{16,24},{20,28},{9,17},{13,21},{17,25},{21,29},{10,... | collective-permute-start | bytes 1277960 | tf_op jit(solution)/shard_map/ppermute | solution.py:412
  40.3 19.6 %collective-permute-start.9 = (bf16[128,1536]{1,0:T(8,128)(2,1)}, bf16[128,1536]{1,0:T(8,128)(2,1)}, u32[]{:S(2)}, u32[]{:S(2)}) collective-permute-start(bf16[128,1536]{1,0:T(8,128)(2,1)} %broadcast_select_fusion.1), channel_id=1, source_target_pairs={{8,24},{12,28},{16,0},{20,4},{9,25},{13,29},{17,1},{21,5},{10,26},... | collective-permute-start | bytes 1179656 | tf_op jit(solution)/shard_map/ppermute | solution.py:412
  41.5 23.6 %collective-permute-start.7 = (bf16[128,1536]{1,0:T(8,128)(2,1)S(1)}, bf16[128,1536]{1,0:T(8,128)(2,1)}, u32[]{:S(2)}, u32[]{:S(2)}) collective-permute-start(bf16[128,1536]{1,0:T(8,128)(2,1)S(1)} %collective-permute-done.6.refs_2_), channel_id=1, source_target_pairs={{8,0},{12,4},{16,8},{20,12},{9,1},{13,5},{17,9},{21,13},{10,2},{14... | collective-permute-start | bytes 1179656 | tf_op jit(solution)/shard_map/ppermute | solution.py:412
  42.9 22.3 %collective-permute-start.8 = (bf16[128,1536]{1,0:T(8,128)(2,1)S(1)}, bf16[128,1536]{1,0:T(8,128)(2,1)}, u32[]{:S(2)}, u32[]{:S(2)}) collective-permute-start(bf16[128,1536]{1,0:T(8,128)(2,1)S(1)} %collective-permute-done.5.refs_1_), channel_id=1, source_target_pairs={{8,16},{12,20},{16,24},{20,28},{9,17},{13,21},{17,25},{21,29},{10,... | collective-permute-start | bytes 1179656 | tf_op jit(solution)/shard_map/ppermute | solution.py:412
  57.0 8.2 %copy-start.1 = (bf16[128,1536]{1,0:T(8,128)(2,1)S(1)}, bf16[128,1536]{1,0:T(8,128)(2,1)}, u32[]{:S(2)}) copy-start(bf16[128,1536]{1,0:T(8,128)(2,1)} %get-tuple-element.45.refs_0_) | copy-start | bytes 1179652
  67.7 43.0 %collective-permute-start.14 = (bf16[320,1536]{1,0:T(8,128)(2,1)S(1)}, bf16[320,1536]{1,0:T(8,128)(2,1)S(1)}, u32[]{:S(2)}, u32[]{:S(2)}) collective-permute-start(bf16[320,1536]{1,0:T(8,128)(2,1)S(1)} %get-tuple-element.55), channel_id=1, source_target_pairs={{0,4},{4,0},{8,12},{12,8},{16,20},{20,16},{24,28},{28,24},{1,5},{5... | collective-permute-start | bytes 2949128 | tf_op jit(solution)/shard_map/ppermute | solution.py:412
  69.2 43.7 %collective-permute-start.13 = (bf16[320,1664]{1,0:T(8,128)(2,1)S(1)}, bf16[320,1664]{1,0:T(8,128)(2,1)S(1)}, u32[]{:S(2)}, u32[]{:S(2)}) collective-permute-start(bf16[320,1664]{1,0:T(8,128)(2,1)S(1)} %get-tuple-element.54), channel_id=1, source_target_pairs={{0,4},{4,0},{8,12},{12,8},{16,20},{20,16},{24,28},{28,24},{1,5},{5... | collective-permute-start | bytes 3194888 | tf_op jit(solution)/shard_map/ppermute | solution.py:412
  69.8 41.5 %collective-permute-start.27 = (bf16[320,1536]{1,0:T(8,128)(2,1)S(1)}, bf16[320,1536]{1,0:T(8,128)(2,1)S(1)}, u32[]{:S(2)}, u32[]{:S(2)}) collective-permute-start(bf16[320,1536]{1,0:T(8,128)(2,1)S(1)} %get-tuple-element.46.q_hbm.refs_2_), channel_id=1, source_target_pairs={{0,2},{1,3},{2,0},{3,1},{4,6},{5,7},{6,4},{7,5},{8,10},{9,11},{10,... | collective-permute-start | bytes 2949128 | tf_op jit(solution)/shard_map/ppermute | solution.py:463
  91.8 7.5 %collective-permute-start.10 = (bf16[80,1664]{1,0:T(8,128)(2,1)}, bf16[80,1664]{1,0:T(8,128)(2,1)S(1)}, u32[]{:S(2)}, u32[]{:S(2)}) collective-permute-start(bf16[80,1664]{1,0:T(8,128)(2,1)} %get-tuple-element.51), channel_id=1, source_target_pairs={{0,24},{4,28},{8,0},{12,4},{16,8},{20,12},{24,16},{28,20},{1,25},{... | collective-permute-start | bytes 798728 | tf_op jit(solution)/shard_map/ppermute | solution.py:412
  92.2 18.5 %collective-permute-start.11 = (bf16[80,1664]{1,0:T(8,128)(2,1)}, bf16[80,1664]{1,0:T(8,128)(2,1)S(1)}, u32[]{:S(2)}, u32[]{:S(2)}) collective-permute-start(bf16[80,1664]{1,0:T(8,128)(2,1)} %get-tuple-element.52), channel_id=1, source_target_pairs={{0,16},{4,20},{8,24},{12,28},{16,0},{20,4},{24,8},{28,12},{1,17},{... | collective-permute-start | bytes 798728 | tf_op jit(solution)/shard_map/ppermute | solution.py:412
  99.3 28.0 %collective-permute-start.30 = (bf16[320,1536]{1,0:T(8,128)(2,1)S(1)}, bf16[320,1536]{1,0:T(8,128)(2,1)S(1)}, u32[]{:S(2)}, u32[]{:S(2)}) collective-permute-start(bf16[320,1536]{1,0:T(8,128)(2,1)S(1)} %get-tuple-element.46.q_hbm.refs_2_), channel_id=1, source_target_pairs={{0,1},{1,0},{2,3},{3,2},{4,5},{5,4},{6,7},{7,6},{8,9},{9,8},{10,11... | collective-permute-start | bytes 2949128 | tf_op jit(solution)/shard_map/ppermute | solution.py:463
  110.7 18.7 %collective-permute-start.29 = (bf16[320,1664]{1,0:T(8,128)(2,1)S(1)}, bf16[320,1664]{1,0:T(8,128)(2,1)S(1)}, u32[]{:S(2)}, u32[]{:S(2)}) collective-permute-start(bf16[320,1664]{1,0:T(8,128)(2,1)S(1)} %get-tuple-element.43.x_hbm.refs_0_), channel_id=1, source_target_pairs={{0,1},{1,0},{2,3},{3,2},{4,5},{5,4},{6,7},{7,6},{8,9},{9,8},{10,11... | collective-permute-start | bytes 3194888 | tf_op jit(solution)/shard_map/ppermute | solution.py:463
  110.7 26.5 %collective-permute-start.24 = (bf16[320,1664]{1,0:T(8,128)(2,1)S(1)}, bf16[320,1664]{1,0:T(8,128)(2,1)}, u32[]{:S(2)}, u32[]{:S(2)}) collective-permute-start(bf16[320,1664]{1,0:T(8,128)(2,1)S(1)} %get-tuple-element.43.x_hbm.refs_0_), channel_id=1, source_target_pairs={{0,2},{1,3},{2,0},{3,1},{4,6},{5,7},{6,4},{7,5},{8,10},{9,11},{10,... | collective-permute-start | bytes 3194888 | tf_op jit(solution)/shard_map/ppermute | solution.py:463
  111.2 14.6 %collective-permute-start.12 = (bf16[80,1664]{1,0:T(8,128)(2,1)}, bf16[80,1664]{1,0:T(8,128)(2,1)S(1)}, u32[]{:S(2)}, u32[]{:S(2)}) collective-permute-start(bf16[80,1664]{1,0:T(8,128)(2,1)} %get-tuple-element.53), channel_id=1, source_target_pairs={{0,8},{4,12},{8,16},{12,20},{16,24},{20,28},{24,0},{28,4},{1,9},{5... | collective-permute-start | bytes 798728 | tf_op jit(solution)/shard_map/ppermute | solution.py:412
  112.9 49.5 %collective-permute-start.28 = (bf16[320,1536]{1,0:T(8,128)(2,1)S(1)}, bf16[320,1536]{1,0:T(8,128)(2,1)S(1)}, u32[]{:S(2)}, u32[]{:S(2)}) collective-permute-start(bf16[320,1536]{1,0:T(8,128)(2,1)S(1)} %collective-permute-done.27.refs_6_), channel_id=1, source_target_pairs={{0,1},{1,0},{2,3},{3,2},{4,5},{5,4},{6,7},{7,6},{8,9},{9,8},{10,11... | collective-permute-start | bytes 2949128 | tf_op jit(solution)/shard_map/ppermute | solution.py:463
  125.8 14.8 %collective-permute-start.15 = (bf16[80,1664]{1,0:T(8,128)(2,1)}, bf16[80,1664]{1,0:T(8,128)(2,1)S(1)}, u32[]{:S(2)}, u32[]{:S(2)}) collective-permute-start(bf16[80,1664]{1,0:T(8,128)(2,1)} %get-tuple-element.56), channel_id=1, source_target_pairs={{0,4},{4,0},{8,12},{12,8},{16,20},{20,16},{24,28},{28,24},{1,5},{5... | collective-permute-start | bytes 798728 | tf_op jit(solution)/shard_map/ppermute | solution.py:412
  127.3 14.7 %collective-permute-start.16 = (bf16[80,1664]{1,0:T(8,128)(2,1)}, bf16[80,1664]{1,0:T(8,128)(2,1)S(1)}, u32[]{:S(2)}, u32[]{:S(2)}) collective-permute-start(bf16[80,1664]{1,0:T(8,128)(2,1)} %get-tuple-element.57), channel_id=1, source_target_pairs={{0,28},{4,24},{8,4},{12,0},{16,12},{20,8},{24,20},{28,16},{1,29},{... | collective-permute-start | bytes 798728 | tf_op jit(solution)/shard_map/ppermute | solution.py:412
  129.5 51.1 %collective-permute-start.19 = (bf16[320,1664]{1,0:T(8,128)(2,1)S(1)}, bf16[320,1664]{1,0:T(8,128)(2,1)S(1)}, u32[]{:S(2)}, u32[]{:S(2)}) collective-permute-start(bf16[320,1664]{1,0:T(8,128)(2,1)S(1)} %collective-permute-done.13.x_hbm.refs_0_), channel_id=1, source_target_pairs={{0,2},{1,3},{2,0},{3,1},{4,6},{5,7},{6,4},{7,5},{8,10},{9,11},{10,... | collective-permute-start | bytes 3194888 | tf_op jit(solution)/shard_map/ppermute | solution.py:463
  137.2 43.3 %collective-permute-start.21 = (bf16[320,1536]{1,0:T(8,128)(2,1)S(1)}, bf16[320,1536]{1,0:T(8,128)(2,1)S(1)}, u32[]{:S(2)}, u32[]{:S(2)}) collective-permute-start(bf16[320,1536]{1,0:T(8,128)(2,1)S(1)} %collective-permute-done.14.q_hbm.refs_4_), channel_id=1, source_target_pairs={{0,2},{1,3},{2,0},{3,1},{4,6},{5,7},{6,4},{7,5},{8,10},{9,11},{10,... | collective-permute-start | bytes 2949128 | tf_op jit(solution)/shard_map/ppermute | solution.py:463
  140.6 21.4 %collective-permute-start.17 = (bf16[80,1664]{1,0:T(8,128)(2,1)}, bf16[80,1664]{1,0:T(8,128)(2,1)S(1)}, u32[]{:S(2)}, u32[]{:S(2)}) collective-permute-start(bf16[80,1664]{1,0:T(8,128)(2,1)} %get-tuple-element.58), channel_id=1, source_target_pairs={{0,20},{4,16},{8,28},{12,24},{16,4},{20,0},{24,12},{28,8},{1,21},{... | collective-permute-start | bytes 798728 | tf_op jit(solution)/shard_map/ppermute | solution.py:412
  142.0 19.9 %collective-permute-start.18 = (bf16[80,1664]{1,0:T(8,128)(2,1)}, bf16[80,1664]{1,0:T(8,128)(2,1)S(1)}, u32[]{:S(2)}, u32[]{:S(2)}) collective-permute-start(bf16[80,1664]{1,0:T(8,128)(2,1)} %get-tuple-element.59), channel_id=1, source_target_pairs={{0,12},{4,8},{8,20},{12,16},{16,28},{20,24},{24,4},{28,0},{1,13},{... | collective-permute-start | bytes 798728 | tf_op jit(solution)/shard_map/ppermute | solution.py:412
  161.9 30.0 %collective-permute-start.25 = (bf16[320,1664]{1,0:T(8,128)(2,1)}, bf16[320,1664]{1,0:T(8,128)(2,1)}, u32[]{:S(2)}, u32[]{:S(2)}) collective-permute-start(bf16[320,1664]{1,0:T(8,128)(2,1)} %collective-permute-done.24.refs_2_), channel_id=1, source_target_pairs={{0,1},{1,0},{2,3},{3,2},{4,5},{5,4},{6,7},{7,6},{8,9},{9,8},{10,11... | collective-permute-start | bytes 3194888 | tf_op jit(solution)/shard_map/ppermute | solution.py:463
  161.9 30.0 %collective-permute-start.23 = (bf16[320,1664]{1,0:T(8,128)(2,1)S(1)}, bf16[320,1664]{1,0:T(8,128)(2,1)S(1)}, u32[]{:S(2)}, u32[]{:S(2)}) collective-permute-start(bf16[320,1664]{1,0:T(8,128)(2,1)S(1)} %collective-permute-done.13.x_hbm.refs_0_), channel_id=1, source_target_pairs={{0,1},{1,0},{2,3},{3,2},{4,5},{5,4},{6,7},{7,6},{8,9},{9,8},{10,11... | collective-permute-start | bytes 3194888 | tf_op jit(solution)/shard_map/ppermute | solution.py:463
  162.5 29.5 %collective-permute-start.26 = (bf16[320,1536]{1,0:T(8,128)(2,1)S(1)}, bf16[320,1536]{1,0:T(8,128)(2,1)}, u32[]{:S(2)}, u32[]{:S(2)}) collective-permute-start(bf16[320,1536]{1,0:T(8,128)(2,1)S(1)} %collective-permute-done.14.q_hbm.refs_4_), channel_id=1, source_target_pairs={{0,1},{1,0},{2,3},{3,2},{4,5},{5,4},{6,7},{7,6},{8,9},{9,8},{10,11... | collective-permute-start | bytes 2949128 | tf_op jit(solution)/shard_map/ppermute | solution.py:463
  180.5 25.6 %collective-permute-start.22 = (bf16[320,1536]{1,0:T(8,128)(2,1)S(1)}, bf16[320,1536]{1,0:T(8,128)(2,1)S(1)}, u32[]{:S(2)}, u32[]{:S(2)}) collective-permute-start(bf16[320,1536]{1,0:T(8,128)(2,1)S(1)} %collective-permute-done.21.refs_2_), channel_id=1, source_target_pairs={{0,1},{1,0},{2,3},{3,2},{4,5},{5,4},{6,7},{7,6},{8,9},{9,8},{10,11... | collective-permute-start | bytes 2949128 | tf_op jit(solution)/shard_map/ppermute | solution.py:463
  180.5 25.6 %collective-permute-start.20 = (bf16[320,1664]{1,0:T(8,128)(2,1)S(1)}, bf16[320,1664]{1,0:T(8,128)(2,1)S(1)}, u32[]{:S(2)}, u32[]{:S(2)}) collective-permute-start(bf16[320,1664]{1,0:T(8,128)(2,1)S(1)} %collective-permute-done.19.refs_0_), channel_id=1, source_target_pairs={{0,1},{1,0},{2,3},{3,2},{4,5},{5,4},{6,7},{7,6},{8,9},{9,8},{10,11... | collective-permute-start | bytes 3194888 | tf_op jit(solution)/shard_map/ppermute | solution.py:463
  181.0 8.1 %copy-start.2 = (bf16[80,1664]{1,0:T(8,128)(2,1)S(1)}, bf16[80,1664]{1,0:T(8,128)(2,1)}, u32[]{:S(2)}) copy-start(bf16[80,1664]{1,0:T(8,128)(2,1)} %get-tuple-element.50.refs_0_) | copy-start | bytes 798724
  181.0 8.1 %copy-start.3 = (bf16[128,128]{1,0:T(8,128)(2,1)S(1)}, bf16[128,128]{1,0:T(8,128)(2,1)}, u32[]{:S(2)}) copy-start(bf16[128,128]{1,0:T(8,128)(2,1)} %get-tuple-element.41.facts_ref) | copy-start | bytes 98308

commit v5 on v4

--- a/solution.py
+++ b/solution.py
@@ -250,15 +250,21 @@
 
     def step(tile, carry):
         units = pl.ds(pl.multiple_of(tile * size, lanes), size)
-        for i in range(3):
-            tile_copy(i, tile).wait()
         if known:
+            tile_copy(2, tile).wait()
+            back_proj = contract_last(q[...], down[tile])
+            tile_copy(0, tile).wait()
+            tile_copy(1, tile).wait()
             gated, activated, slope = (t[:, units].astype(jnp.float32) for t in terms)
         else:
-            gate_pre = contract_last(x[:, :width], gate[tile])
-            up_pre = contract_last(x[:, :width], up[tile])
+            rows = x[:, :width]
+            tile_copy(0, tile).wait()
+            gate_pre = contract_last(rows, gate[tile])
+            tile_copy(1, tile).wait()
+            up_pre = contract_last(rows, up[tile])
+            tile_copy(2, tile).wait()
+            back_proj = contract_last(q[...], down[tile])
             gated, activated, slope = activation(gate_pre, up_pre)
-        back_proj = contract_last(q[...], down[tile])
         delta = weight * back_proj
         up_delta = (delta * gated).astype(jnp.bfloat16)
         gate_delta = (delta * slope).astype(jnp.bfloat16)

time: 217 us -> 217 us (level)
  no operation moved by 1% of the time
where the time goes in v5:
time: 217 us
  waiting for transfers between devices  101 us (47%)
  Pallas kernels  76.8 us (35%)
  starting transfers between devices  37.1 us (17%)
    ppermute x19, waiting for transfers between devices, move(): return lax.ppermute(rows, 'ep', pairs)  77.1 us
    pallas_call x3, Pallas kernels, weight_grads(): pl.pallas_call(functools.partial(weight_kernel, blocks=count, ready=ready...  32.6 us
    ppermute x19, starting transfers between devices, move(): return lax.ppermute(rows, 'ep', pairs)  32 us
    pallas_call x2, Pallas kernels, expert_part(): pl.pallas_call(functools.partial(expert_kernel, tiles=tiles, known=bool(t...  26.4 us
    ppermute x12, waiting for transfers between devices, swap(): return lax.ppermute(rows, 'dp', [(d, d ^ step) for d in range(dp_size)])  23.8 us
    pallas_call x1, Pallas kernels, act_part(): pl.pallas_call(functools.partial(act_kernel, tiles=tiles), in_specs=[hbm]...  7.18 us
    ppermute x12, starting transfers between devices, swap(): return lax.ppermute(rows, 'dp', [(d, d ^ step) for d in range(dp_size)])  5.15 us
  transfers between devices with their start and end apart: 31, of which 12 were waited for; matrix products, arithmetic and copies ran while one was open for 0% of the time, Pallas kernels for 28%

profile of v5, /device:TPU:0, one launch (start us, length us, event | category | flops | bytes accessed | tf_op | source)
XLA Modules:
  0.0 216.6 jit_solution(4110248585342412489)
XLA Ops:
  0.6 2.6 %prep.1 = (bf16[128,1664]{1,0:T(8,128)(2,1)}, bf16[128,1536]{1,0:T(8,128)(2,1)}, bf16[128,128]{1,0:T(8,128)(2,1)}) custom-call(s32[8]{0:T(128)} %cap_ref.1, s32[4,128]{1,0:T(4,128)} %bitcast.28, s32[1,128]{1,0:T(1,128)} %order_ref.1, f32[4,128]{1,0:T(4,128)} %bitcast.29, f32[128,1536]{1,0:T(8,128)} %grad_ref.1, bf16[128,1536]{1,0:T(8,128)(2,1)} %tok_ref.1), custom_call_target="tpu_custom_call" | custom-call | tf_op jit(solution)/shard_map/prep/pallas_call | solution.py:398
  3.2 5.0 %collective-permute-start = (bf16[128,1664]{1,0:T(8,128)(2,1)}, bf16[128,1664]{1,0:T(8,128)(2,1)S(1)}, u32[]{:S(2)}, u32[]{:S(2)}) collective-permute-start(bf16[128,1664]{1,0:T(8,128)(2,1)} %get-tuple-element.42.refs_0_), channel_id=1, source_target_pairs={{0,8},{4,12},{8,16},{12,20},{16,24},{20,28},{1,9},{5,13},{9,17},{1... | collective-permute-start | bytes 1277960 | tf_op jit(solution)/shard_map/ppermute | solution.py:418
  8.2 1.3 collective-permute-start.1
  9.5 4.6 %collective-permute-start.5 = (bf16[128,1536]{1,0:T(8,128)(2,1)}, bf16[128,1536]{1,0:T(8,128)(2,1)S(1)}, u32[]{:S(2)}, u32[]{:S(2)}) collective-permute-start(bf16[128,1536]{1,0:T(8,128)(2,1)} %get-tuple-element.45.refs_0_), channel_id=1, source_target_pairs={{0,8},{4,12},{8,16},{12,20},{16,24},{20,28},{1,9},{5,13},{9,17},{1... | collective-permute-start | bytes 1179656 | tf_op jit(solution)/shard_map/ppermute | solution.py:418
  14.0 1.3 collective-permute-start.6
  15.4 3.3 %collective-permute-done.refs_1_ = bf16[128,1664]{1,0:T(8,128)(2,1)S(1)} collective-permute-done((bf16[128,1664]{1,0:T(8,128)(2,1)}, bf16[128,1664]{1,0:T(8,128)(2,1)S(1)}, u32[]{:S(2)}, u32[]{:S(2)}) %collective-permute-start) | collective-permute-done | bytes 426016 | tf_op jit(solution)/shard_map/ppermute | solution.py:418
  18.6 4.3 %collective-permute-done.1.refs_2_ = bf16[128,1664]{1,0:T(8,128)(2,1)S(1)} collective-permute-done((bf16[128,1664]{1,0:T(8,128)(2,1)}, bf16[128,1664]{1,0:T(8,128)(2,1)S(1)}, u32[]{:S(2)}, u32[]{:S(2)}) %collective-permute-start.1) | collective-permute-done | bytes 426016 | tf_op jit(solution)/shard_map/ppermute | solution.py:418
  23.0 1.3 collective-permute-start.4
  24.3 1.3 collective-permute-start.2
  25.6 0.7 collective-permute-start.3
  26.3 13.2 %collective-permute-done.6.refs_2_ = bf16[128,1536]{1,0:T(8,128)(2,1)S(1)} collective-permute-done((bf16[128,1536]{1,0:T(8,128)(2,1)}, bf16[128,1536]{1,0:T(8,128)(2,1)S(1)}, u32[]{:S(2)}, u32[]{:S(2)}) %collective-permute-start.6) | collective-permute-done | bytes 393248 | tf_op jit(solution)/shard_map/ppermute | solution.py:418
  39.5 0.8 broadcast_select_fusion.1
  40.3 1.3 collective-permute-start.9
  41.5 1.3 collective-permute-start.7
  42.9 1.4 collective-permute-start.8
  44.3 12.7 %collective-permute-done.2.refs_3_ = bf16[128,1664]{1,0:T(8,128)(2,1)S(1)} collective-permute-done((bf16[128,1664]{1,0:T(8,128)(2,1)S(1)}, bf16[128,1664]{1,0:T(8,128)(2,1)S(1)}, u32[]{:S(2)}, u32[]{:S(2)}) %collective-permute-start.2) | collective-permute-done | bytes 426016 | tf_op jit(solution)/shard_map/ppermute | solution.py:418
  57.0 2.8 %x_slots.1 = (bf16[320,1664]{1,0:T(8,128)(2,1)S(1)}, bf16[320,1664]{1,0:T(8,128)(2,1)S(1)}, bf16[512,640]{1,0:T(8,128)(2,1)S(1)}) custom-call(s32[1]{0:T(128)} %bitcast.place_ref, bf16[128,1664]{1,0:T(8,128)(2,1)S(1)} %copy-done, bf16[128,1664]{1,0:T(8,128)(2,1)S(1)} %collective-permute-done.refs_1_, bf16[128,1664]{1,0:T(8,128)(2,1)S(1)} %collective-permute-done.1.refs_2_, ...), custom_call_target="tpu_custom_call" | custom-call | tf_op jit(solution)/shard_map/x_slots/pallas_call | solution.py:441
  59.8 5.4 %collective-permute-done.7.refs_3_ = bf16[128,1536]{1,0:T(8,128)(2,1)} collective-permute-done((bf16[128,1536]{1,0:T(8,128)(2,1)S(1)}, bf16[128,1536]{1,0:T(8,128)(2,1)}, u32[]{:S(2)}, u32[]{:S(2)}) %collective-permute-start.7) | collective-permute-done | bytes 393248 | tf_op jit(solution)/shard_map/ppermute | solution.py:418
  65.2 2.5 %q_slots.1 = (bf16[320,1536]{1,0:T(8,128)(2,1)S(1)}, bf16[320,1536]{1,0:T(8,128)(2,1)S(1)}) custom-call(s32[1]{0:T(128)} %bitcast.place_ref, bf16[512,640]{1,0:T(8,128)(2,1)S(1)} %get-tuple-element.44.table_ref, bf16[128,1536]{1,0:T(8,128)(2,1)S(1)} %copy-done.1, bf16[128,1536]{1,0:T(8,128)(2,1)S(1)} %collective-permute-done.5.refs_1_, ...), custom_call_target="tpu_custom_call" | custom-call | tf_op jit(solution)/shard_map/q_slots/pallas_call | solution.py:454
  67.7 1.6 collective-permute-start.14
  69.2 0.5 collective-permute-start.13
  69.8 1.5 collective-permute-start.27
  71.3 7.2 %act_part.1 = (bf16[320,1536]{1,0:T(8,128)(2,1)}, bf16[320,1536]{1,0:T(8,128)(2,1)}, bf16[320,1536]{1,0:T(8,128)(2,1)}) custom-call(bf16[320,1664]{1,0:T(8,128)(2,1)S(1)} %get-tuple-element.43.x_hbm.refs_0_, bf16[1536,1536]{1,0:T(8,128)(2,1)} %bitcast.11, bf16[1536,1536]{1,0:T(8,128)(2,1)} %bitcast.17), custom_call_target="tpu_custom_call" | custom-call | flops 3019898880 | bytes 9437184 | tf_op jit(solution)/shard_map/act_part/pallas_call | solution.py:476
  78.5 13.3 %expert_part.2 = (bf16[320,384]{1,0:T(8,128)(2,1)}, bf16[320,384]{1,0:T(8,128)(2,1)}, bf16[320,384]{1,0:T(8,128)(2,1)}, bf16[80,1664]{1,0:T(8,128)(2,1)}, bf16[8...) custom-call(s32[1]{0:T(128)} %bitcast.3.rank_ref, ...), custom_call_target="tpu_custom_call" | custom-call | flops 7549747200 | bytes 14155776 | tf_op jit(solution)/shard_map/expert_part/pallas_call | solution.py:498
  91.8 0.4 collective-permute-start.10
  92.2 2.7 %collective-permute-start.11 = (bf16[80,1664]{1,0:T(8,128)(2,1)}, bf16[80,1664]{1,0:T(8,128)(2,1)S(1)}, u32[]{:S(2)}, u32[]{:S(2)}) collective-permute-start(bf16[80,1664]{1,0:T(8,128)(2,1)} %get-tuple-element.52), channel_id=1, source_target_pairs={{0,16},{4,20},{8,24},{12,28},{16,0},{20,4},{24,8},{28,12},{1,17},{... | collective-permute-start | bytes 798728 | tf_op jit(solution)/shard_map/ppermute | solution.py:418
  95.0 4.4 %collective-permute-done.10.refs_1_ = bf16[80,1664]{1,0:T(8,128)(2,1)S(1)} collective-permute-done((bf16[80,1664]{1,0:T(8,128)(2,1)}, bf16[80,1664]{1,0:T(8,128)(2,1)S(1)}, u32[]{:S(2)}, u32[]{:S(2)}) %collective-permute-start.10) | collective-permute-done | bytes 266272 | tf_op jit(solution)/shard_map/ppermute | solution.py:418
  99.3 11.4 %collective-permute-done.11.refs_2_ = bf16[80,1664]{1,0:T(8,128)(2,1)S(1)} collective-permute-done((bf16[80,1664]{1,0:T(8,128)(2,1)}, bf16[80,1664]{1,0:T(8,128)(2,1)S(1)}, u32[]{:S(2)}, u32[]{:S(2)}) %collective-permute-start.11) | collective-permute-done | bytes 266272 | tf_op jit(solution)/shard_map/ppermute | solution.py:418
  110.7 0.5 collective-permute-start.24
  111.3 1.7 collective-permute-done.13.x_hbm.refs_0_
  112.9 13.1 %expert_part.3 = (bf16[320,384]{1,0:T(8,128)(2,1)}, bf16[320,384]{1,0:T(8,128)(2,1)}, bf16[320,384]{1,0:T(8,128)(2,1)}, bf16[80,1664]{1,0:T(8,128)(2,1)}, bf16[8...) custom-call(s32[1]{0:T(128)} %bitcast.3.rank_ref, ...), custom_call_target="tpu_custom_call" | custom-call | flops 7549747200 | bytes 14155776 | tf_op jit(solution)/shard_map/expert_part/pallas_call | solution.py:498
  126.0 1.6 collective-permute-start.15
  127.6 2.1 collective-permute-start.16
  129.7 1.5 collective-permute-start.19
  131.2 6.0 %collective-permute-done.24.refs_2_ = bf16[320,1664]{1,0:T(8,128)(2,1)} collective-permute-done((bf16[320,1664]{1,0:T(8,128)(2,1)S(1)}, bf16[320,1664]{1,0:T(8,128)(2,1)}, u32[]{:S(2)}, u32[]{:S(2)}) %collective-permute-start.24) | collective-permute-done | bytes 1064992 | tf_op jit(solution)/shard_map/ppermute | solution.py:469
  137.2 0.5 collective-permute-start.21
  137.7 3.1 %collective-permute-done.15.refs_4_ = bf16[80,1664]{1,0:T(8,128)(2,1)S(1)} collective-permute-done((bf16[80,1664]{1,0:T(8,128)(2,1)}, bf16[80,1664]{1,0:T(8,128)(2,1)S(1)}, u32[]{:S(2)}, u32[]{:S(2)}) %collective-permute-start.15) | collective-permute-done | bytes 266272 | tf_op jit(solution)/shard_map/ppermute | solution.py:418
  140.8 1.4 collective-permute-start.17
  142.3 2.2 collective-permute-start.18
  144.4 17.7 %collective-permute-done.17.refs_6_ = bf16[80,1664]{1,0:T(8,128)(2,1)S(1)} collective-permute-done((bf16[80,1664]{1,0:T(8,128)(2,1)}, bf16[80,1664]{1,0:T(8,128)(2,1)S(1)}, u32[]{:S(2)}, u32[]{:S(2)}) %collective-permute-start.17) | collective-permute-done | bytes 266272 | tf_op jit(solution)/shard_map/ppermute | solution.py:418
  162.2 0.5 collective-permute-start.23
  162.7 0.1 collective-permute-start.26
  162.8 17.8 %collective-permute-done.21.refs_2_ = bf16[320,1536]{1,0:T(8,128)(2,1)S(1)} collective-permute-done((bf16[320,1536]{1,0:T(8,128)(2,1)S(1)}, bf16[320,1536]{1,0:T(8,128)(2,1)S(1)}, u32[]{:S(2)}, u32[]{:S(2)}) %collective-permute-start.21) | collective-permute-done | bytes 983072 | tf_op jit(solution)/shard_map/ppermute | solution.py:469
  180.6 0.5 collective-permute-start.20
  181.1 8.1 %weight_grads.3 = (bf16[384,1536]{1,0:T(8,128)(2,1)}, bf16[384,1536]{1,0:T(8,128)(2,1)}, bf16[384,1536]{1,0:T(8,128)(2,1)}) custom-call(s32[1]{0:T(128)} %bitcast.3.rank_ref, bf16[320,1664]{1,0:T(8,128)(2,1)S(1)} %get-tuple-element.43.x_hbm.refs_0_, bf16[320,1664]{1,0:T(8,128)(2,1)S(1)} %collective-permute-done.29.refs_1_, ...), custom_call_target="tpu_custom_call" | custom-call | flops 4529848320 | bytes 4259840 | tf_op jit(solution)/shard_map/weight_grads/pallas_call | solution.py:540
  189.2 2.8 %combine.1 = (bf16[128,1536]{1,0:T(8,128)(2,1)}, f32[4,128]{1,0:T(4,128)}) custom-call(s32[1]{0:T(128)} %bitcast.place_ref, bf16[128,128]{1,0:T(8,128)(2,1)S(1)} %copy-done.3, bf16[80,1664]{1,0:T(8,128)(2,1)S(1)} %copy-done.2, bf16[80,1664]{1,0:T(8,128)(2,1)S(1)} %collective-permute-done.10.refs_1_, bf16[80,1664]{1,0:T(8,128)(2,1)S(1)} %collective-permute-done.11.refs_2_, ...), custom_call_target="tpu_custom_call" | custom-call | tf_op jit(solution)/shard_map/combine/pallas_call | solution.py:600
  192.0 14.1 %weight_grads.4 = (bf16[384,1536]{1,0:T(8,128)(2,1)}, bf16[384,1536]{1,0:T(8,128)(2,1)}, bf16[384,1536]{1,0:T(8,128)(2,1)}) custom-call(s32[1]{0:T(128)} %bitcast.3.rank_ref, bf16[320,1664]{1,0:T(8,128)(2,1)S(1)} %collective-permute-done.13.x_hbm.refs_0_, bf16[320,1664]{1,0:T(8,128)(2,1)S(1)} %collective-permute-done.23.refs_1_, ...), custom_call_target="tpu_custom_call" | custom-call | flops 9059696640 | bytes 8519680 | tf_op jit(solution)/shard_map/weight_grads/pallas_call | solution.py:540
  206.1 10.3 %weight_grads.5 = (bf16[384,1536]{1,0:T(8,128)(2,1)}, bf16[384,1536]{1,0:T(8,128)(2,1)}, bf16[384,1536]{1,0:T(8,128)(2,1)}) custom-call(s32[1]{0:T(128)} %bitcast.3.rank_ref, bf16[320,1664]{1,0:T(8,128)(2,1)S(1)} %collective-permute-done.19.refs_0_, bf16[320,1664]{1,0:T(8,128)(2,1)S(1)} %collective-permute-done.20.refs_1_, ...), custom_call_target="tpu_custom_call" | custom-call | flops 4529848320 | bytes 4259840 | tf_op jit(solution)/shard_map/weight_grads/pallas_call | solution.py:540
  (34 shorter events, 0.1 us)
Async XLA Ops:
  3.2 15.5 %collective-permute-start = (bf16[128,1664]{1,0:T(8,128)(2,1)}, bf16[128,1664]{1,0:T(8,128)(2,1)S(1)}, u32[]{:S(2)}, u32[]{:S(2)}) collective-permute-start(bf16[128,1664]{1,0:T(8,128)(2,1)} %get-tuple-element.42.refs_0_), channel_id=1, source_target_pairs={{0,8},{4,12},{8,16},{12,20},{16,24},{20,28},{1,9},{5,13},{9,17},{1... | collective-permute-start | bytes 1277960 | tf_op jit(solution)/shard_map/ppermute | solution.py:418
  8.2 14.8 %collective-permute-start.1 = (bf16[128,1664]{1,0:T(8,128)(2,1)}, bf16[128,1664]{1,0:T(8,128)(2,1)S(1)}, u32[]{:S(2)}, u32[]{:S(2)}) collective-permute-start(bf16[128,1664]{1,0:T(8,128)(2,1)} %get-tuple-element.42.refs_0_), channel_id=1, source_target_pairs={{8,0},{12,4},{16,8},{20,12},{24,16},{28,20},{9,1},{13,5},{17,9},{2... | collective-permute-start | bytes 1277960 | tf_op jit(solution)/shard_map/ppermute | solution.py:418
  9.5 16.8 %collective-permute-start.5 = (bf16[128,1536]{1,0:T(8,128)(2,1)}, bf16[128,1536]{1,0:T(8,128)(2,1)S(1)}, u32[]{:S(2)}, u32[]{:S(2)}) collective-permute-start(bf16[128,1536]{1,0:T(8,128)(2,1)} %get-tuple-element.45.refs_0_), channel_id=1, source_target_pairs={{0,8},{4,12},{8,16},{12,20},{16,24},{20,28},{1,9},{5,13},{9,17},{1... | collective-permute-start | bytes 1179656 | tf_op jit(solution)/shard_map/ppermute | solution.py:418
  14.0 25.4 %collective-permute-start.6 = (bf16[128,1536]{1,0:T(8,128)(2,1)}, bf16[128,1536]{1,0:T(8,128)(2,1)S(1)}, u32[]{:S(2)}, u32[]{:S(2)}) collective-permute-start(bf16[128,1536]{1,0:T(8,128)(2,1)} %get-tuple-element.45.refs_0_), channel_id=1, source_target_pairs={{8,0},{12,4},{16,8},{20,12},{24,16},{28,20},{9,1},{13,5},{17,9},{2... | collective-permute-start | bytes 1179656 | tf_op jit(solution)/shard_map/ppermute | solution.py:418
  15.4 41.6 %copy-start = (bf16[128,1664]{1,0:T(8,128)(2,1)S(1)}, bf16[128,1664]{1,0:T(8,128)(2,1)}, u32[]{:S(2)}) copy-start(bf16[128,1664]{1,0:T(8,128)(2,1)} %get-tuple-element.42.refs_0_) | copy-start | bytes 1277956
  23.0 19.8 %collective-permute-start.4 = (bf16[128,1664]{1,0:T(8,128)(2,1)S(1)}, bf16[128,1664]{1,0:T(8,128)(2,1)S(1)}, u32[]{:S(2)}, u32[]{:S(2)}) collective-permute-start(bf16[128,1664]{1,0:T(8,128)(2,1)S(1)} %broadcast_select_fusion), channel_id=1, source_target_pairs={{8,24},{12,28},{16,0},{20,4},{9,25},{13,29},{17,1},{21,5},{10,26},... | collective-permute-start | bytes 1277960 | tf_op jit(solution)/shard_map/ppermute | solution.py:418
  24.3 32.7 %collective-permute-start.2 = (bf16[128,1664]{1,0:T(8,128)(2,1)S(1)}, bf16[128,1664]{1,0:T(8,128)(2,1)S(1)}, u32[]{:S(2)}, u32[]{:S(2)}) collective-permute-start(bf16[128,1664]{1,0:T(8,128)(2,1)S(1)} %collective-permute-done.1.refs_2_), channel_id=1, source_target_pairs={{8,0},{12,4},{16,8},{20,12},{9,1},{13,5},{17,9},{21,13},{10,2},{14... | collective-permute-start | bytes 1277960 | tf_op jit(solution)/shard_map/ppermute | solution.py:418
  25.6 31.4 %collective-permute-start.3 = (bf16[128,1664]{1,0:T(8,128)(2,1)S(1)}, bf16[128,1664]{1,0:T(8,128)(2,1)S(1)}, u32[]{:S(2)}, u32[]{:S(2)}) collective-permute-start(bf16[128,1664]{1,0:T(8,128)(2,1)S(1)} %collective-permute-done.refs_1_), channel_id=1, source_target_pairs={{8,16},{12,20},{16,24},{20,28},{9,17},{13,21},{17,25},{21,29},{10,... | collective-permute-start | bytes 1277960 | tf_op jit(solution)/shard_map/ppermute | solution.py:418
  40.3 19.6 %collective-permute-start.9 = (bf16[128,1536]{1,0:T(8,128)(2,1)}, bf16[128,1536]{1,0:T(8,128)(2,1)}, u32[]{:S(2)}, u32[]{:S(2)}) collective-permute-start(bf16[128,1536]{1,0:T(8,128)(2,1)} %broadcast_select_fusion.1), channel_id=1, source_target_pairs={{8,24},{12,28},{16,0},{20,4},{9,25},{13,29},{17,1},{21,5},{10,26},... | collective-permute-start | bytes 1179656 | tf_op jit(solution)/shard_map/ppermute | solution.py:418
  41.5 23.6 %collective-permute-start.7 = (bf16[128,1536]{1,0:T(8,128)(2,1)S(1)}, bf16[128,1536]{1,0:T(8,128)(2,1)}, u32[]{:S(2)}, u32[]{:S(2)}) collective-permute-start(bf16[128,1536]{1,0:T(8,128)(2,1)S(1)} %collective-permute-done.6.refs_2_), channel_id=1, source_target_pairs={{8,0},{12,4},{16,8},{20,12},{9,1},{13,5},{17,9},{21,13},{10,2},{14... | collective-permute-start | bytes 1179656 | tf_op jit(solution)/shard_map/ppermute | solution.py:418
  42.9 22.3 %collective-permute-start.8 = (bf16[128,1536]{1,0:T(8,128)(2,1)S(1)}, bf16[128,1536]{1,0:T(8,128)(2,1)}, u32[]{:S(2)}, u32[]{:S(2)}) collective-permute-start(bf16[128,1536]{1,0:T(8,128)(2,1)S(1)} %collective-permute-done.5.refs_1_), channel_id=1, source_target_pairs={{8,16},{12,20},{16,24},{20,28},{9,17},{13,21},{17,25},{21,29},{10,... | collective-permute-start | bytes 1179656 | tf_op jit(solution)/shard_map/ppermute | solution.py:418
  57.0 8.2 %copy-start.1 = (bf16[128,1536]{1,0:T(8,128)(2,1)S(1)}, bf16[128,1536]{1,0:T(8,128)(2,1)}, u32[]{:S(2)}) copy-start(bf16[128,1536]{1,0:T(8,128)(2,1)} %get-tuple-element.45.refs_0_) | copy-start | bytes 1179652
  67.7 43.1 %collective-permute-start.14 = (bf16[320,1536]{1,0:T(8,128)(2,1)S(1)}, bf16[320,1536]{1,0:T(8,128)(2,1)S(1)}, u32[]{:S(2)}, u32[]{:S(2)}) collective-permute-start(bf16[320,1536]{1,0:T(8,128)(2,1)S(1)} %get-tuple-element.55), channel_id=1, source_target_pairs={{0,4},{4,0},{8,12},{12,8},{16,20},{20,16},{24,28},{28,24},{1,5},{5... | collective-permute-start | bytes 2949128 | tf_op jit(solution)/shard_map/ppermute | solution.py:418
  69.2 43.7 %collective-permute-start.13 = (bf16[320,1664]{1,0:T(8,128)(2,1)S(1)}, bf16[320,1664]{1,0:T(8,128)(2,1)S(1)}, u32[]{:S(2)}, u32[]{:S(2)}) collective-permute-start(bf16[320,1664]{1,0:T(8,128)(2,1)S(1)} %get-tuple-element.54), channel_id=1, source_target_pairs={{0,4},{4,0},{8,12},{12,8},{16,20},{20,16},{24,28},{28,24},{1,5},{5... | collective-permute-start | bytes 3194888 | tf_op jit(solution)/shard_map/ppermute | solution.py:418
  69.8 41.5 %collective-permute-start.27 = (bf16[320,1536]{1,0:T(8,128)(2,1)S(1)}, bf16[320,1536]{1,0:T(8,128)(2,1)S(1)}, u32[]{:S(2)}, u32[]{:S(2)}) collective-permute-start(bf16[320,1536]{1,0:T(8,128)(2,1)S(1)} %get-tuple-element.46.q_hbm.refs_2_), channel_id=1, source_target_pairs={{0,2},{1,3},{2,0},{3,1},{4,6},{5,7},{6,4},{7,5},{8,10},{9,11},{10,... | collective-permute-start | bytes 2949128 | tf_op jit(solution)/shard_map/ppermute | solution.py:469
  91.8 7.5 %collective-permute-start.10 = (bf16[80,1664]{1,0:T(8,128)(2,1)}, bf16[80,1664]{1,0:T(8,128)(2,1)S(1)}, u32[]{:S(2)}, u32[]{:S(2)}) collective-permute-start(bf16[80,1664]{1,0:T(8,128)(2,1)} %get-tuple-element.51), channel_id=1, source_target_pairs={{0,24},{4,28},{8,0},{12,4},{16,8},{20,12},{24,16},{28,20},{1,25},{... | collective-permute-start | bytes 798728 | tf_op jit(solution)/shard_map/ppermute | solution.py:418
  92.2 18.5 %collective-permute-start.11 = (bf16[80,1664]{1,0:T(8,128)(2,1)}, bf16[80,1664]{1,0:T(8,128)(2,1)S(1)}, u32[]{:S(2)}, u32[]{:S(2)}) collective-permute-start(bf16[80,1664]{1,0:T(8,128)(2,1)} %get-tuple-element.52), channel_id=1, source_target_pairs={{0,16},{4,20},{8,24},{12,28},{16,0},{20,4},{24,8},{28,12},{1,17},{... | collective-permute-start | bytes 798728 | tf_op jit(solution)/shard_map/ppermute | solution.py:418
  99.3 28.2 %collective-permute-start.30 = (bf16[320,1536]{1,0:T(8,128)(2,1)S(1)}, bf16[320,1536]{1,0:T(8,128)(2,1)S(1)}, u32[]{:S(2)}, u32[]{:S(2)}) collective-permute-start(bf16[320,1536]{1,0:T(8,128)(2,1)S(1)} %get-tuple-element.46.q_hbm.refs_2_), channel_id=1, source_target_pairs={{0,1},{1,0},{2,3},{3,2},{4,5},{5,4},{6,7},{7,6},{8,9},{9,8},{10,11... | collective-permute-start | bytes 2949128 | tf_op jit(solution)/shard_map/ppermute | solution.py:469
  110.7 19.0 %collective-permute-start.29 = (bf16[320,1664]{1,0:T(8,128)(2,1)S(1)}, bf16[320,1664]{1,0:T(8,128)(2,1)S(1)}, u32[]{:S(2)}, u32[]{:S(2)}) collective-permute-start(bf16[320,1664]{1,0:T(8,128)(2,1)S(1)} %get-tuple-element.43.x_hbm.refs_0_), channel_id=1, source_target_pairs={{0,1},{1,0},{2,3},{3,2},{4,5},{5,4},{6,7},{7,6},{8,9},{9,8},{10,11... | collective-permute-start | bytes 3194888 | tf_op jit(solution)/shard_map/ppermute | solution.py:469
  110.7 26.5 %collective-permute-start.24 = (bf16[320,1664]{1,0:T(8,128)(2,1)S(1)}, bf16[320,1664]{1,0:T(8,128)(2,1)}, u32[]{:S(2)}, u32[]{:S(2)}) collective-permute-start(bf16[320,1664]{1,0:T(8,128)(2,1)S(1)} %get-tuple-element.43.x_hbm.refs_0_), channel_id=1, source_target_pairs={{0,2},{1,3},{2,0},{3,1},{4,6},{5,7},{6,4},{7,5},{8,10},{9,11},{10,... | collective-permute-start | bytes 3194888 | tf_op jit(solution)/shard_map/ppermute | solution.py:469
  111.3 14.8 %collective-permute-start.12 = (bf16[80,1664]{1,0:T(8,128)(2,1)}, bf16[80,1664]{1,0:T(8,128)(2,1)S(1)}, u32[]{:S(2)}, u32[]{:S(2)}) collective-permute-start(bf16[80,1664]{1,0:T(8,128)(2,1)} %get-tuple-element.53), channel_id=1, source_target_pairs={{0,8},{4,12},{8,16},{12,20},{16,24},{20,28},{24,0},{28,4},{1,9},{5... | collective-permute-start | bytes 798728 | tf_op jit(solution)/shard_map/ppermute | solution.py:418
  112.9 49.8 %collective-permute-start.28 = (bf16[320,1536]{1,0:T(8,128)(2,1)S(1)}, bf16[320,1536]{1,0:T(8,128)(2,1)S(1)}, u32[]{:S(2)}, u32[]{:S(2)}) collective-permute-start(bf16[320,1536]{1,0:T(8,128)(2,1)S(1)} %collective-permute-done.27.refs_6_), channel_id=1, source_target_pairs={{0,1},{1,0},{2,3},{3,2},{4,5},{5,4},{6,7},{7,6},{8,9},{9,8},{10,11... | collective-permute-start | bytes 2949128 | tf_op jit(solution)/shard_map/ppermute | solution.py:469
  126.0 14.8 %collective-permute-start.15 = (bf16[80,1664]{1,0:T(8,128)(2,1)}, bf16[80,1664]{1,0:T(8,128)(2,1)S(1)}, u32[]{:S(2)}, u32[]{:S(2)}) collective-permute-start(bf16[80,1664]{1,0:T(8,128)(2,1)} %get-tuple-element.56), channel_id=1, source_target_pairs={{0,4},{4,0},{8,12},{12,8},{16,20},{20,16},{24,28},{28,24},{1,5},{5... | collective-permute-start | bytes 798728 | tf_op jit(solution)/shard_map/ppermute | solution.py:418
  127.6 14.7 %collective-permute-start.16 = (bf16[80,1664]{1,0:T(8,128)(2,1)}, bf16[80,1664]{1,0:T(8,128)(2,1)S(1)}, u32[]{:S(2)}, u32[]{:S(2)}) collective-permute-start(bf16[80,1664]{1,0:T(8,128)(2,1)} %get-tuple-element.57), channel_id=1, source_target_pairs={{0,28},{4,24},{8,4},{12,0},{16,12},{20,8},{24,20},{28,16},{1,29},{... | collective-permute-start | bytes 798728 | tf_op jit(solution)/shard_map/ppermute | solution.py:418
  129.7 50.8 %collective-permute-start.19 = (bf16[320,1664]{1,0:T(8,128)(2,1)S(1)}, bf16[320,1664]{1,0:T(8,128)(2,1)S(1)}, u32[]{:S(2)}, u32[]{:S(2)}) collective-permute-start(bf16[320,1664]{1,0:T(8,128)(2,1)S(1)} %collective-permute-done.13.x_hbm.refs_0_), channel_id=1, source_target_pairs={{0,2},{1,3},{2,0},{3,1},{4,6},{5,7},{6,4},{7,5},{8,10},{9,11},{10,... | collective-permute-start | bytes 3194888 | tf_op jit(solution)/shard_map/ppermute | solution.py:469
  137.2 43.3 %collective-permute-start.21 = (bf16[320,1536]{1,0:T(8,128)(2,1)S(1)}, bf16[320,1536]{1,0:T(8,128)(2,1)S(1)}, u32[]{:S(2)}, u32[]{:S(2)}) collective-permute-start(bf16[320,1536]{1,0:T(8,128)(2,1)S(1)} %collective-permute-done.14.q_hbm.refs_4_), channel_id=1, source_target_pairs={{0,2},{1,3},{2,0},{3,1},{4,6},{5,7},{6,4},{7,5},{8,10},{9,11},{10,... | collective-permute-start | bytes 2949128 | tf_op jit(solution)/shard_map/ppermute | solution.py:469
  140.8 21.4 %collective-permute-start.17 = (bf16[80,1664]{1,0:T(8,128)(2,1)}, bf16[80,1664]{1,0:T(8,128)(2,1)S(1)}, u32[]{:S(2)}, u32[]{:S(2)}) collective-permute-start(bf16[80,1664]{1,0:T(8,128)(2,1)} %get-tuple-element.58), channel_id=1, source_target_pairs={{0,20},{4,16},{8,28},{12,24},{16,4},{20,0},{24,12},{28,8},{1,21},{... | collective-permute-start | bytes 798728 | tf_op jit(solution)/shard_map/ppermute | solution.py:418
  142.3 19.9 %collective-permute-start.18 = (bf16[80,1664]{1,0:T(8,128)(2,1)}, bf16[80,1664]{1,0:T(8,128)(2,1)S(1)}, u32[]{:S(2)}, u32[]{:S(2)}) collective-permute-start(bf16[80,1664]{1,0:T(8,128)(2,1)} %get-tuple-element.59), channel_id=1, source_target_pairs={{0,12},{4,8},{8,20},{12,16},{16,28},{20,24},{24,4},{28,0},{1,13},{... | collective-permute-start | bytes 798728 | tf_op jit(solution)/shard_map/ppermute | solution.py:418
  162.2 29.8 %collective-permute-start.25 = (bf16[320,1664]{1,0:T(8,128)(2,1)}, bf16[320,1664]{1,0:T(8,128)(2,1)}, u32[]{:S(2)}, u32[]{:S(2)}) collective-permute-start(bf16[320,1664]{1,0:T(8,128)(2,1)} %collective-permute-done.24.refs_2_), channel_id=1, source_target_pairs={{0,1},{1,0},{2,3},{3,2},{4,5},{5,4},{6,7},{7,6},{8,9},{9,8},{10,11... | collective-permute-start | bytes 3194888 | tf_op jit(solution)/shard_map/ppermute | solution.py:469
  162.2 29.8 %collective-permute-start.23 = (bf16[320,1664]{1,0:T(8,128)(2,1)S(1)}, bf16[320,1664]{1,0:T(8,128)(2,1)S(1)}, u32[]{:S(2)}, u32[]{:S(2)}) collective-permute-start(bf16[320,1664]{1,0:T(8,128)(2,1)S(1)} %collective-permute-done.13.x_hbm.refs_0_), channel_id=1, source_target_pairs={{0,1},{1,0},{2,3},{3,2},{4,5},{5,4},{6,7},{7,6},{8,9},{9,8},{10,11... | collective-permute-start | bytes 3194888 | tf_op jit(solution)/shard_map/ppermute | solution.py:469
  162.7 29.3 %collective-permute-start.26 = (bf16[320,1536]{1,0:T(8,128)(2,1)S(1)}, bf16[320,1536]{1,0:T(8,128)(2,1)}, u32[]{:S(2)}, u32[]{:S(2)}) collective-permute-start(bf16[320,1536]{1,0:T(8,128)(2,1)S(1)} %collective-permute-done.14.q_hbm.refs_4_), channel_id=1, source_target_pairs={{0,1},{1,0},{2,3},{3,2},{4,5},{5,4},{6,7},{7,6},{8,9},{9,8},{10,11... | collective-permute-start | bytes 2949128 | tf_op jit(solution)/shard_map/ppermute | solution.py:469
  180.6 25.6 %collective-permute-start.22 = (bf16[320,1536]{1,0:T(8,128)(2,1)S(1)}, bf16[320,1536]{1,0:T(8,128)(2,1)S(1)}, u32[]{:S(2)}, u32[]{:S(2)}) collective-permute-start(bf16[320,1536]{1,0:T(8,128)(2,1)S(1)} %collective-permute-done.21.refs_2_), channel_id=1, source_target_pairs={{0,1},{1,0},{2,3},{3,2},{4,5},{5,4},{6,7},{7,6},{8,9},{9,8},{10,11... | collective-permute-start | bytes 2949128 | tf_op jit(solution)/shard_map/ppermute | solution.py:469
  180.6 25.6 %collective-permute-start.20 = (bf16[320,1664]{1,0:T(8,128)(2,1)S(1)}, bf16[320,1664]{1,0:T(8,128)(2,1)S(1)}, u32[]{:S(2)}, u32[]{:S(2)}) collective-permute-start(bf16[320,1664]{1,0:T(8,128)(2,1)S(1)} %collective-permute-done.19.refs_0_), channel_id=1, source_target_pairs={{0,1},{1,0},{2,3},{3,2},{4,5},{5,4},{6,7},{7,6},{8,9},{9,8},{10,11... | collective-permute-start | bytes 3194888 | tf_op jit(solution)/shard_map/ppermute | solution.py:469
  181.1 8.1 %copy-start.2 = (bf16[80,1664]{1,0:T(8,128)(2,1)S(1)}, bf16[80,1664]{1,0:T(8,128)(2,1)}, u32[]{:S(2)}) copy-start(bf16[80,1664]{1,0:T(8,128)(2,1)} %get-tuple-element.50.refs_0_) | copy-start | bytes 798724
  181.1 8.1 %copy-start.3 = (bf16[128,128]{1,0:T(8,128)(2,1)S(1)}, bf16[128,128]{1,0:T(8,128)(2,1)}, u32[]{:S(2)}) copy-start(bf16[128,128]{1,0:T(8,128)(2,1)} %get-tuple-element.41.facts_ref) | copy-start | bytes 98308
